TPU v7x, 128 devices: a whole 4x4x4 slice. The times are simulated.
128 devices in a mesh: grp: 8 (over y, core), mem: 16 (over x, z).
Axes of the slice: x: 4, y: 4, z: 4, core: 2. Of those that a mesh axis runs over, the one named last changes fastest.
Arguments:
- factors: bfloat16 [256, 288, 1792], P(('grp', 'mem')), may hold values from -3 to 3
- screen: int32 [128, 18], P(('grp', 'mem')), may hold values from 0 to 1, as said below
Outputs:
- exchange_matrix: float32 [1792, 1792], P(('grp', 'mem'))
Inputs may be any that keep to these rules, and one draw needn't show every extreme that they name: screen[b, j] is 1 where auxiliary block b and occupied block j survive screening; every auxiliary block keeps at least one occupied block.
All inputs are finite; a program needn't handle non-finite values.
Results may differ from a plain program's by a relative error of at most 0.0003.
Values may be sent and summed in bfloat16 or wider, within the bound.
No kernel may reach another device: no remote copies, remote signals or barrier semaphores. Data moves between devices by JAX's collectives and lax.ppermute only.
A program may use at most 128 MiB of HBM per device.

v0:
```python
import functools

import jax
import jax.numpy as jnp
import numpy as np
from jax import lax
from jax.experimental import pallas as pl
from jax.experimental.pallas import tpu as pltpu
from jax.sharding import PartitionSpec as P


AXES = ("grp", "mem")
SIDE = 4
CORES = 2
WIDE_A = 1152
SENT = jnp.float16


def limit(mib):
    return pltpu.CompilerParams(vmem_limit_bytes=mib * 1024 * 1024)


def near(v):
    return v ^ 1


def far(v):
    return SIDE - 1 - v


def steps(dim, core):
    return (near, far) if core == (dim == 2) else (far, near)


def order(v, dim, core):
    first, second = steps(dim, core)
    return [v, second(v), first(v), second(first(v))]


def linear(y, c, x, z):
    return ((y * CORES + c) * SIDE + x) * SIDE + z


def everyone():
    return [(y, c, x, z) for y in range(SIDE) for c in range(CORES) for x in range(SIDE) for z in range(SIDE)]


def partners(*moves):
    pairs = []
    for place in everyone():
        target = list(place)
        for dim, turn in moves:
            target[dim] = steps(dim, place[1])[turn](target[dim])
        pairs.append((linear(*place), linear(*target)))
    return pairs


CORE_SWAP = [(linear(y, c, x, z), linear(y, 1 - c, x, z)) for y, c, x, z in everyone()]


def table():
    rows = []
    for y, c, x, z in everyone():
        x_order, z_order = order(x, 2, c), order(z, 3, c)
        row = [c, *order(y, 0, c), *[x_order.index(v) for v in range(SIDE)], *[z_order.index(v) for v in range(SIDE)]]
        rows.append(row + [0] * (16 - len(row)))
    return np.asarray(rows, np.int32)


def transpose_kernel(where, x_ref, out_ref, same_ref, scratch):
    aux, occ, basis = x_ref.shape
    part = out_ref.shape[1]
    same_ref[...] = x_ref[...]
    for a in range(aux):
        for t in range(basis // 128):
            scratch[t * 128 : (t + 1) * 128, a * occ : (a + 1) * occ] = x_ref[a, :, t * 128 : (t + 1) * 128].T
    for s in range(SIDE):
        at = pl.multiple_of((where[1 + s] * CORES + where[0]) * part, 16)
        out_ref[s] = scratch[pl.ds(at, part), :]


def transposed(where, x):
    aux, occ, basis = x.shape
    part = basis // (SIDE * CORES)
    return pl.pallas_call(
        transpose_kernel,
        out_shape=[jax.ShapeDtypeStruct((SIDE, part, aux * occ), x.dtype), jax.ShapeDtypeStruct(x.shape, x.dtype)],
        in_specs=[pl.BlockSpec(memory_space=pltpu.SMEM)] + [pl.BlockSpec(memory_space=pltpu.VMEM)],
        out_specs=[pl.BlockSpec(memory_space=pltpu.VMEM)] * 2,
        scratch_shapes=[pltpu.VMEM((basis, aux * occ), x.dtype)],
        compiler_params=limit(12),
    )(where, x)


def product_kernel(slots, columns, where, flags, own_t, other_t, own, other, out):
    deep = own_t.shape[2]
    part = own_t.shape[1]
    chunk = part // SIDE
    start, size = columns
    right = jnp.concatenate(
        [own[:, :, start : start + size].reshape(deep, size), other[:, :, start : start + size].reshape(deep, size)], axis=0
    )
    for at, s in enumerate(slots):
        left = jnp.concatenate([own_t[s], other_t[s]], axis=1) * flags[...]
        whole = jnp.dot(left, right, preferred_element_type=jnp.float32)
        for v in range(SIDE):
            out[at, where[5 + v]] = whole[v * chunk : (v + 1) * chunk]


def product(where, flags, own_t, other_t, own, other, slots, columns):
    chunk = own_t.shape[1] // SIDE
    n = len(slots)
    rows = n * own_t.shape[1]
    depth = 2 * own_t.shape[2]
    vmem = pl.BlockSpec(memory_space=pltpu.VMEM)
    return pl.pallas_call(
        functools.partial(product_kernel, slots, columns),
        out_shape=jax.ShapeDtypeStruct((n, SIDE, chunk, columns[1]), jnp.float32),
        in_specs=[pl.BlockSpec(memory_space=pltpu.SMEM)] + [vmem] * 5,
        out_specs=vmem,
        compiler_params=limit(16),
        cost_estimate=pl.CostEstimate(flops=2 * rows * depth * columns[1], bytes_accessed=4 * rows * columns[1], transcendentals=0),
    )(where, flags, own_t, other_t, own, other)


def last_order_kernel(where, whole_ref, *refs):
    outs, scratch = refs[:-1], refs[-1]
    whole = whole_ref[...]
    rows = whole.shape[0] // SIDE
    for v in range(SIDE):
        scratch[where[9 + v]] = whole[v * rows : (v + 1) * rows]
    for slot, out in enumerate(outs):
        out[...] = scratch[slot]


def last_order(where, whole):
    rows, basis = whole.shape
    part = jax.ShapeDtypeStruct((rows // SIDE, basis), jnp.float32)
    return pl.pallas_call(
        last_order_kernel,
        out_shape=[part] * SIDE,
        in_specs=[pl.BlockSpec(memory_space=pltpu.SMEM), pl.BlockSpec(memory_space=pltpu.VMEM)],
        out_specs=[pl.BlockSpec(memory_space=pltpu.VMEM)] * SIDE,
        scratch_shapes=[pltpu.VMEM((SIDE, rows // SIDE, basis), jnp.float32)],
        compiler_params=limit(4),
    )(where, whole)


def on_device(factors, screen):
    basis = factors.shape[2]
    f32 = jnp.float32
    where = lax.dynamic_index_in_dim(jnp.asarray(table()), lax.axis_index(AXES), 0, keepdims=False)
    other = lax.ppermute(factors, AXES, CORE_SWAP)
    other_screen = lax.ppermute(screen, AXES, CORE_SWAP)
    own_t, own = transposed(where, factors)
    other_t, other = transposed(where, other)
    both = jnp.concatenate([screen, other_screen], axis=0) == 1
    width = factors.shape[1] // screen.shape[1]
    flags = jnp.broadcast_to(both.astype(jnp.bfloat16)[:, None, :, None], (2, factors.shape[0], screen.shape[1], width))
    flags = flags.reshape(1, -1)
    left, right = (0, WIDE_A), (WIDE_A, basis - WIDE_A)

    def make(slots, columns):
        return product(where, flags, own_t, other_t, own, other, slots, columns)

    def narrow(v):
        return v.astype(SENT)

    def go(v, *moves):
        return lax.ppermute(v, AXES, partners(*moves))

    a_send = make((2, 3), left)
    a_in = go(narrow(a_send), (0, 0))
    b_all = make((0, 1, 2, 3), right)
    b_in = go(narrow(b_all[:, 2:]), (2, 0))
    a_keep = make((0, 1), left)
    a_in2 = go(narrow(a_keep[:, 2:] + a_in[:, 2:].astype(f32)), (2, 0))
    a_keep = a_keep[:, :2] + a_in[:, :2].astype(f32)
    b_in2 = go(narrow(b_all[2:, :2] + b_in[2:].astype(f32)), (0, 0))
    b_keep = b_all[:2, :2] + b_in[:2].astype(f32)

    def joined(i, j):
        return jnp.concatenate(
            [a_keep[i, j] + a_in2[i, j].astype(f32), b_keep[i, j] + b_in2[i, j].astype(f32)], axis=-1
        )

    c_y = go(narrow(joined(1, 0)), (0, 1))
    c_x = go(narrow(joined(0, 1)), (2, 1))
    c_d = go(narrow(joined(1, 1)), (0, 1), (2, 1))
    whole = joined(0, 0) + c_y.astype(f32) + c_x.astype(f32) + c_d.astype(f32)
    kept, second, first, across = last_order(where, whole)
    d_first = go(first, (3, 0))
    d_second = go(second, (3, 1))
    d_across = go(across, (3, 0), (3, 1))
    return kept + d_second + d_first + d_across


def solution(mesh):
    placed = (P(AXES, None, None), P(AXES, None))
    return jax.shard_map(on_device, mesh=mesh, in_specs=placed, out_specs=P(AXES, None), check_vma=False)
```

profile of v0, /device:TPU:0, one launch (start us, length us, event | category | flops | bytes accessed | tf_op | source)
XLA Modules:
  0.0 62.8 jit_solution(12943343070966916555)
XLA Ops:
  0.0 0.0 copy-start.1
  0.0 0.0 collective-permute-start.1
  0.0 0.5 collective-permute-start
  0.5 0.7 %dynamic-slice_bitcast_fusion.where = s32[16]{0:T(128)S(1)} fusion(s32[128,16]{1,0:T(8,128)} %constant.21.clone, s32[]{:T(128)S(6)} %select_n.4), kind=kLoop, calls=%fused_computation.37 | loop fusion | bytes 132 | tf_op jit(solution)/shard_map/jit(dynamic_index_in_dim)/squeeze | solution.py:152
  1.2 0.0 copy-start
  1.2 1.6 %copy-done = bf16[2,288,1792]{2,1,0:T(8,128)(2,1)S(1)} copy-done((bf16[2,288,1792]{2,1,0:T(8,128)(2,1)S(1)}, bf16[2,288,1792]{2,1,0:T(8,128)(2,1)}, u32[]{:S(2)}) %copy-start) | copy-done | bytes 2064408
  2.8 2.0 %shard_map.37 = (bf16[4,224,576]{2,1,0:T(8,128)(2,1)S(1)}, bf16[2,288,1792]{2,1,0:T(8,128)(2,1)S(1)}) custom-call(s32[16]{0:T(128)S(1)} %dynamic-slice_bitcast_fusion.where, bf16[2,288,1792]{2,1,0:T(8,128)(2,1)S(1)} %copy-done), custom_call_target="tpu_custom_call" | custom-call | tf_op jit(solution)/shard_map/pallas_call | solution.py:85
  4.8 0.0 collective-permute-done
  4.8 0.0 copy-done.1
  4.9 0.1 broadcast_in_dim.2
  4.9 0.1 reshape.41.flags
  5.0 0.0 collective-permute-done.1.x_ref
  5.0 3.1 %shard_map.38 = (bf16[4,224,576]{2,1,0:T(8,128)(2,1)S(1)}, bf16[2,288,1792]{2,1,0:T(8,128)(2,1)S(1)}) custom-call(s32[16]{0:T(128)S(1)} %dynamic-slice_bitcast_fusion.where, bf16[2,288,1792]{2,1,0:T(8,128)(2,1)} %collective-permute-done.1.x_ref), custom_call_target="tpu_custom_call" | custom-call | tf_op jit(solution)/shard_map/pallas_call | solution.py:85
  8.1 2.5 %shard_map.41 = f32[4,4,56,640]{3,2,1,0:T(8,128)S(1)} custom-call(s32[16]{0:T(128)S(1)} %dynamic-slice_bitcast_fusion.where, bf16[1,1152]{1,0:T(2,128)(2,1)S(1)} %reshape.41.flags, bf16[4,224,576]{2,1,0:T(8,128)(2,1)S(1)} %get-tuple-element.13.own_t, bf16[4,224,576]{2,1,0:T(8,128)(2,1)S(1)} %get-tuple-element.14.other_t, ...), custom_call_target="tpu_custom_call" | custom-call | flops 1321205760 | bytes 2293760 | tf_op jit(solution)/shard_map/pallas_call | solution.py:116
  10.7 2.3 %shard_map.40 = f32[2,4,56,1152]{3,2,1,0:T(8,128)S(1)} custom-call(s32[16]{0:T(128)S(1)} %dynamic-slice_bitcast_fusion.where, bf16[1,1152]{1,0:T(2,128)(2,1)S(1)} %reshape.41.flags, bf16[4,224,576]{2,1,0:T(8,128)(2,1)S(1)} %get-tuple-element.13.own_t, bf16[4,224,576]{2,1,0:T(8,128)(2,1)S(1)} %get-tuple-element.14.other_t, ...), custom_call_target="tpu_custom_call" | custom-call | flops 1189085184 | bytes 2064384 | tf_op jit(solution)/shard_map/pallas_call | solution.py:116
  12.9 0.1 convert_element_type.74
  13.1 1.8 %collective-permute-start.2 = (f16[2,4,56,1152]{3,2,1,0:T(8,128)(2,1)S(1)}, f16[2,4,56,1152]{3,2,1,0:T(8,128)(2,1)S(1)}, u32[]{:S(2)}, u32[]{:S(2)}) collective-permute-start(f16[2,4,56,1152]{3,2,1,0:T(8,128)(2,1)S(1)} %convert_element_type.74), channel_id=1, source_target_pairs={{0,32},{1,33},{2,34},{3,35},{4,36},{5,37},{6,38},{7,39},{8,40},{9,... | collective-permute-start | bytes 3096584 | tf_op jit(solution)/shard_map/ppermute | solution.py:170
  14.8 0.1 slice_convert_fusion
  14.9 2.8 %collective-permute-start.4 = (f16[4,2,56,640]{3,2,1,0:T(8,128)(2,1)S(1)}, f16[4,2,56,640]{3,2,1,0:T(8,128)(2,1)S(1)}, u32[]{:S(2)}, u32[]{:S(2)}) collective-permute-start(f16[4,2,56,640]{3,2,1,0:T(8,128)(2,1)S(1)} %slice_convert_fusion), channel_id=1, source_target_pairs={{0,12},{1,13},{2,14},{3,15},{4,8},{5,9},{6,10},{7,11},{8,4},{9,5},... | collective-permute-start | bytes 1720328 | tf_op jit(solution)/shard_map/ppermute | solution.py:170
  17.7 2.3 %shard_map.39 = f32[2,4,56,1152]{3,2,1,0:T(8,128)S(1)} custom-call(s32[16]{0:T(128)S(1)} %dynamic-slice_bitcast_fusion.where, bf16[1,1152]{1,0:T(2,128)(2,1)S(1)} %reshape.41.flags, bf16[4,224,576]{2,1,0:T(8,128)(2,1)S(1)} %get-tuple-element.13.own_t, bf16[4,224,576]{2,1,0:T(8,128)(2,1)S(1)} %get-tuple-element.14.other_t, ...), custom_call_target="tpu_custom_call" | custom-call | flops 1189085184 | bytes 2064384 | tf_op jit(solution)/shard_map/pallas_call | solution.py:116
  20.0 5.9 %collective-permute-done.4 = f16[4,2,56,640]{3,2,1,0:T(8,128)(2,1)S(1)} collective-permute-done((f16[4,2,56,640]{3,2,1,0:T(8,128)(2,1)S(1)}, f16[4,2,56,640]{3,2,1,0:T(8,128)(2,1)S(1)}, u32[]{:S(2)}, u32[]{:S(2)}) %collective-permute-start.4) | collective-permute-done | bytes 573472 | tf_op jit(solution)/shard_map/ppermute | solution.py:170
  25.9 0.1 fusion.1
  26.0 0.4 collective-permute-start.5
  26.4 1.3 %collective-permute-done.2 = f16[2,4,56,1152]{3,2,1,0:T(8,128)(2,1)S(1)} collective-permute-done((f16[2,4,56,1152]{3,2,1,0:T(8,128)(2,1)S(1)}, f16[2,4,56,1152]{3,2,1,0:T(8,128)(2,1)S(1)}, u32[]{:S(2)}, u32[]{:S(2)}) %collective-permute-start.2) | collective-permute-done | bytes 1032224 | tf_op jit(solution)/shard_map/ppermute | solution.py:170
  27.8 0.2 fusion
  28.0 3.0 %collective-permute-start.3 = (f16[2,2,56,1152]{3,2,1,0:T(8,128)(2,1)S(1)}, f16[2,2,56,1152]{3,2,1,0:T(8,128)(2,1)S(1)}, u32[]{:S(2)}, u32[]{:S(2)}) collective-permute-start(f16[2,2,56,1152]{3,2,1,0:T(8,128)(2,1)S(1)} %get-tuple-element.21), channel_id=1, source_target_pairs={{0,12},{1,13},{2,14},{3,15},{4,8},{5,9},{6,10},{7,11},{8,4},{9,5},... | collective-permute-start | bytes 1548296 | tf_op jit(solution)/shard_map/ppermute | solution.py:170
  30.9 1.8 %collective-permute-done.5 = f16[2,2,56,640]{3,2,1,0:T(8,128)(2,1)S(1)} collective-permute-done((f16[2,2,56,640]{3,2,1,0:T(8,128)(2,1)S(1)}, f16[2,2,56,640]{3,2,1,0:T(8,128)(2,1)S(1)}, u32[]{:S(2)}, u32[]{:S(2)}) %collective-permute-start.5) | collective-permute-done | bytes 286752 | tf_op jit(solution)/shard_map/ppermute | solution.py:170
  32.7 0.1 fusion.15
  32.8 5.5 %collective-permute-done.3 = f16[2,2,56,1152]{3,2,1,0:T(8,128)(2,1)S(1)} collective-permute-done((f16[2,2,56,1152]{3,2,1,0:T(8,128)(2,1)S(1)}, f16[2,2,56,1152]{3,2,1,0:T(8,128)(2,1)S(1)}, u32[]{:S(2)}, u32[]{:S(2)}) %collective-permute-start.3) | collective-permute-done | bytes 516128 | tf_op jit(solution)/shard_map/ppermute | solution.py:170
  38.4 0.1 fusion.12
  38.5 0.1 pad_maximum_fusion.2
  38.6 2.9 %collective-permute-start.8 = (f16[56,1792]{1,0:T(8,128)(2,1)S(1)}, f16[56,1792]{1,0:T(8,128)(2,1)S(1)}, u32[]{:S(2)}, u32[]{:S(2)}) collective-permute-start(f16[56,1792]{1,0:T(8,128)(2,1)S(1)} %pad_maximum_fusion.2), channel_id=1, source_target_pairs={{0,100},{1,101},{2,102},{3,103},{4,96},{5,97},{6,98},{7,99},{8,108... | collective-permute-start | bytes 602120 | tf_op jit(solution)/shard_map/ppermute | solution.py:170
  41.5 1.8 %collective-permute-start.7 = (f16[56,1792]{1,0:T(8,128)(2,1)S(1)}, f16[56,1792]{1,0:T(8,128)(2,1)S(1)}, u32[]{:S(2)}, u32[]{:S(2)}) collective-permute-start(f16[56,1792]{1,0:T(8,128)(2,1)S(1)} %pad_maximum_fusion.1), channel_id=1, source_target_pairs={{0,4},{1,5},{2,6},{3,7},{4,0},{5,1},{6,2},{7,3},{8,12},{9,13},{10,... | collective-permute-start | bytes 602120 | tf_op jit(solution)/shard_map/ppermute | solution.py:170
  43.4 0.2 collective-permute-start.6
  43.6 2.9 %collective-permute-done.8 = f16[56,1792]{1,0:T(8,128)(2,1)S(1)} collective-permute-done((f16[56,1792]{1,0:T(8,128)(2,1)S(1)}, f16[56,1792]{1,0:T(8,128)(2,1)S(1)}, u32[]{:S(2)}, u32[]{:S(2)}) %collective-permute-start.8) | collective-permute-done | bytes 200736 | tf_op jit(solution)/shard_map/ppermute | solution.py:170
  46.5 2.6 %collective-permute-done.7 = f16[56,1792]{1,0:T(8,128)(2,1)S(1)} collective-permute-done((f16[56,1792]{1,0:T(8,128)(2,1)S(1)}, f16[56,1792]{1,0:T(8,128)(2,1)S(1)}, u32[]{:S(2)}, u32[]{:S(2)}) %collective-permute-start.7) | collective-permute-done | bytes 200736 | tf_op jit(solution)/shard_map/ppermute | solution.py:170
  49.1 1.4 %collective-permute-done.6 = f16[56,1792]{1,0:T(8,128)(2,1)S(1)} collective-permute-done((f16[56,1792]{1,0:T(8,128)(2,1)S(1)}, f16[56,1792]{1,0:T(8,128)(2,1)S(1)}, u32[]{:S(2)}, u32[]{:S(2)}) %collective-permute-start.6) | collective-permute-done | bytes 200736 | tf_op jit(solution)/shard_map/ppermute | solution.py:170
  50.4 0.1 fusion.3.whole_ref
  50.5 0.6 shard_map.42
  51.2 4.0 %collective-permute-start.11 = (f32[14,1792]{1,0:T(8,128)S(1)}, f32[14,1792]{1,0:T(8,128)S(1)}, u32[]{:S(2)}, u32[]{:S(2)}) collective-permute-start(f32[14,1792]{1,0:T(8,128)S(1)} %get-tuple-element.20), channel_id=1, source_target_pairs={{0,2},{1,3},{2,0},{3,1},{4,6},{5,7},{6,4},{7,5},{8,10},{9,11},{10,... | collective-permute-start | bytes 301064 | tf_op jit(solution)/shard_map/ppermute | solution.py:170
  55.1 1.0 %collective-permute-start.10 = (f32[14,1792]{1,0:T(8,128)S(1)}, f32[14,1792]{1,0:T(8,128)S(1)}, u32[]{:S(2)}, u32[]{:S(2)}) collective-permute-start(f32[14,1792]{1,0:T(8,128)S(1)} %get-tuple-element.19), channel_id=1, source_target_pairs={{0,1},{1,0},{2,3},{3,2},{4,5},{5,4},{6,7},{7,6},{8,9},{9,8},{10,11... | collective-permute-start | bytes 301064 | tf_op jit(solution)/shard_map/ppermute | solution.py:170
  56.1 0.0 collective-permute-start.9
  56.1 1.8 %collective-permute-done.11 = f32[14,1792]{1,0:T(8,128)S(1)} collective-permute-done((f32[14,1792]{1,0:T(8,128)S(1)}, f32[14,1792]{1,0:T(8,128)S(1)}, u32[]{:S(2)}, u32[]{:S(2)}) %collective-permute-start.11) | collective-permute-done | bytes 100384 | tf_op jit(solution)/shard_map/ppermute | solution.py:170
  57.9 2.2 %collective-permute-done.10 = f32[14,1792]{1,0:T(8,128)S(1)} collective-permute-done((f32[14,1792]{1,0:T(8,128)S(1)}, f32[14,1792]{1,0:T(8,128)S(1)}, u32[]{:S(2)}, u32[]{:S(2)}) %collective-permute-start.10) | collective-permute-done | bytes 100384 | tf_op jit(solution)/shard_map/ppermute | solution.py:170
  60.1 2.0 %collective-permute-done.9 = f32[14,1792]{1,0:T(8,128)S(1)} collective-permute-done((f32[14,1792]{1,0:T(8,128)S(1)}, f32[14,1792]{1,0:T(8,128)S(1)}, u32[]{:S(2)}, u32[]{:S(2)}) %collective-permute-start.9) | collective-permute-done | bytes 100384 | tf_op jit(solution)/shard_map/ppermute | solution.py:170
  62.1 0.7 %add_add_fusion = f32[14,1792]{1,0:T(8,128)} fusion(f32[14,1792]{1,0:T(8,128)S(1)} %collective-permute-done.11, f32[14,1792]{1,0:T(8,128)S(1)} %collective-permute-done.10, f32[14,1792]{1,0:T(8,128)S(1)} %get-tuple-element.17, f32[14,1792]{1,0:T(8,128)S(1)} %collective-permute-done.9), kind=kLoop, calls=%fused_computation.32 | loop fusion | flops 75264 | bytes 501760 | tf_op jit(solution)/shard_map/add | solution.py:195
  (3 shorter events, 0.1 us)
Async XLA Ops:
  0.0 4.8 %copy-start.1 = (s32[1,18]{1,0:T(1,128)S(1)}, s32[1,18]{1,0:T(1,128)}, u32[]{:S(2)}) copy-start(s32[1,18]{1,0:T(1,128)} %param.4) | copy-start | bytes 220
  0.0 5.0 %collective-permute-start.1 = (bf16[2,288,1792]{2,1,0:T(8,128)(2,1)}, bf16[2,288,1792]{2,1,0:T(8,128)(2,1)}, u32[]{:S(2)}, u32[]{:S(2)}) collective-permute-start(bf16[2,288,1792]{2,1,0:T(8,128)(2,1)} %x_ref.1), channel_id=1, source_target_pairs={{0,16},{1,17},{2,18},{3,19},{4,20},{5,21},{6,22},{7,23},{8,24},{9,... | collective-permute-start | bytes 6193160 | tf_op jit(solution)/shard_map/ppermute | solution.py:153
  0.0 4.8 %collective-permute-start = (s32[1,18]{1,0:T(1,128)}, s32[1,18]{1,0:T(1,128)S(1)}, u32[]{:S(2)}, u32[]{:S(2)}) collective-permute-start(s32[1,18]{1,0:T(1,128)} %param.4), channel_id=1, source_target_pairs={{0,16},{1,17},{2,18},{3,19},{4,20},{5,21},{6,22},{7,23},{8,24},{9,... | collective-permute-start | bytes 224 | tf_op jit(solution)/shard_map/ppermute | solution.py:154
  1.2 1.6 %copy-start = (bf16[2,288,1792]{2,1,0:T(8,128)(2,1)S(1)}, bf16[2,288,1792]{2,1,0:T(8,128)(2,1)}, u32[]{:S(2)}) copy-start(bf16[2,288,1792]{2,1,0:T(8,128)(2,1)} %x_ref.1) | copy-start | bytes 6193156
  13.1 14.7 %collective-permute-start.2 = (f16[2,4,56,1152]{3,2,1,0:T(8,128)(2,1)S(1)}, f16[2,4,56,1152]{3,2,1,0:T(8,128)(2,1)S(1)}, u32[]{:S(2)}, u32[]{:S(2)}) collective-permute-start(f16[2,4,56,1152]{3,2,1,0:T(8,128)(2,1)S(1)} %convert_element_type.74), channel_id=1, source_target_pairs={{0,32},{1,33},{2,34},{3,35},{4,36},{5,37},{6,38},{7,39},{8,40},{9,... | collective-permute-start | bytes 3096584 | tf_op jit(solution)/shard_map/ppermute | solution.py:170
  14.9 11.0 %collective-permute-start.4 = (f16[4,2,56,640]{3,2,1,0:T(8,128)(2,1)S(1)}, f16[4,2,56,640]{3,2,1,0:T(8,128)(2,1)S(1)}, u32[]{:S(2)}, u32[]{:S(2)}) collective-permute-start(f16[4,2,56,640]{3,2,1,0:T(8,128)(2,1)S(1)} %slice_convert_fusion), channel_id=1, source_target_pairs={{0,12},{1,13},{2,14},{3,15},{4,8},{5,9},{6,10},{7,11},{8,4},{9,5},... | collective-permute-start | bytes 1720328 | tf_op jit(solution)/shard_map/ppermute | solution.py:170
  26.0 6.7 %collective-permute-start.5 = (f16[2,2,56,640]{3,2,1,0:T(8,128)(2,1)S(1)}, f16[2,2,56,640]{3,2,1,0:T(8,128)(2,1)S(1)}, u32[]{:S(2)}, u32[]{:S(2)}) collective-permute-start(f16[2,2,56,640]{3,2,1,0:T(8,128)(2,1)S(1)} %get-tuple-element.23), channel_id=1, source_target_pairs={{0,32},{1,33},{2,34},{3,35},{4,36},{5,37},{6,38},{7,39},{8,40},{9,... | collective-permute-start | bytes 860168 | tf_op jit(solution)/shard_map/ppermute | solution.py:170
  28.0 10.4 %collective-permute-start.3 = (f16[2,2,56,1152]{3,2,1,0:T(8,128)(2,1)S(1)}, f16[2,2,56,1152]{3,2,1,0:T(8,128)(2,1)S(1)}, u32[]{:S(2)}, u32[]{:S(2)}) collective-permute-start(f16[2,2,56,1152]{3,2,1,0:T(8,128)(2,1)S(1)} %get-tuple-element.21), channel_id=1, source_target_pairs={{0,12},{1,13},{2,14},{3,15},{4,8},{5,9},{6,10},{7,11},{8,4},{9,5},... | collective-permute-start | bytes 1548296 | tf_op jit(solution)/shard_map/ppermute | solution.py:170
  38.6 7.9 %collective-permute-start.8 = (f16[56,1792]{1,0:T(8,128)(2,1)S(1)}, f16[56,1792]{1,0:T(8,128)(2,1)S(1)}, u32[]{:S(2)}, u32[]{:S(2)}) collective-permute-start(f16[56,1792]{1,0:T(8,128)(2,1)S(1)} %pad_maximum_fusion.2), channel_id=1, source_target_pairs={{0,100},{1,101},{2,102},{3,103},{4,96},{5,97},{6,98},{7,99},{8,108... | collective-permute-start | bytes 602120 | tf_op jit(solution)/shard_map/ppermute | solution.py:170
  41.5 7.5 %collective-permute-start.7 = (f16[56,1792]{1,0:T(8,128)(2,1)S(1)}, f16[56,1792]{1,0:T(8,128)(2,1)S(1)}, u32[]{:S(2)}, u32[]{:S(2)}) collective-permute-start(f16[56,1792]{1,0:T(8,128)(2,1)S(1)} %pad_maximum_fusion.1), channel_id=1, source_target_pairs={{0,4},{1,5},{2,6},{3,7},{4,0},{5,1},{6,2},{7,3},{8,12},{9,13},{10,... | collective-permute-start | bytes 602120 | tf_op jit(solution)/shard_map/ppermute | solution.py:170
  43.4 7.0 %collective-permute-start.6 = (f16[56,1792]{1,0:T(8,128)(2,1)S(1)}, f16[56,1792]{1,0:T(8,128)(2,1)S(1)}, u32[]{:S(2)}, u32[]{:S(2)}) collective-permute-start(f16[56,1792]{1,0:T(8,128)(2,1)S(1)} %pad_maximum_fusion), channel_id=1, source_target_pairs={{0,96},{1,97},{2,98},{3,99},{4,100},{5,101},{6,102},{7,103},{8,104... | collective-permute-start | bytes 602120 | tf_op jit(solution)/shard_map/ppermute | solution.py:170
  51.2 6.7 %collective-permute-start.11 = (f32[14,1792]{1,0:T(8,128)S(1)}, f32[14,1792]{1,0:T(8,128)S(1)}, u32[]{:S(2)}, u32[]{:S(2)}) collective-permute-start(f32[14,1792]{1,0:T(8,128)S(1)} %get-tuple-element.20), channel_id=1, source_target_pairs={{0,2},{1,3},{2,0},{3,1},{4,6},{5,7},{6,4},{7,5},{8,10},{9,11},{10,... | collective-permute-start | bytes 301064 | tf_op jit(solution)/shard_map/ppermute | solution.py:170
  55.1 5.0 %collective-permute-start.10 = (f32[14,1792]{1,0:T(8,128)S(1)}, f32[14,1792]{1,0:T(8,128)S(1)}, u32[]{:S(2)}, u32[]{:S(2)}) collective-permute-start(f32[14,1792]{1,0:T(8,128)S(1)} %get-tuple-element.19), channel_id=1, source_target_pairs={{0,1},{1,0},{2,3},{3,2},{4,5},{5,4},{6,7},{7,6},{8,9},{9,8},{10,11... | collective-permute-start | bytes 301064 | tf_op jit(solution)/shard_map/ppermute | solution.py:170
  56.1 6.0 %collective-permute-start.9 = (f32[14,1792]{1,0:T(8,128)S(1)}, f32[14,1792]{1,0:T(8,128)S(1)}, u32[]{:S(2)}, u32[]{:S(2)}) collective-permute-start(f32[14,1792]{1,0:T(8,128)S(1)} %get-tuple-element.18), channel_id=1, source_target_pairs={{0,3},{1,2},{2,1},{3,0},{4,7},{5,6},{6,5},{7,4},{8,11},{9,10},{10,... | collective-permute-start | bytes 301064 | tf_op jit(solution)/shard_map/ppermute | solution.py:170
where the time goes:
time: 63 us; the launch traced here: 62.8 us
  waiting for transfers between devices  27.4 us (43%)
  starting transfers between devices  18.4 us (29%)
  Pallas kernels  12.8 us (20%)
  local copies, waits for them, and re-layouts  2.45 us (4%)
  other arithmetic  1.64 us (3%)
    ppermute x10, waiting for transfers between devices, go(): return lax.ppermute(v, AXES, partners(*moves))  27.4 us
    ppermute x10, starting transfers between devices, go(): return lax.ppermute(v, AXES, partners(*moves))  17.9 us
    pallas_call x3, Pallas kernels, product(): pl.pallas_call(functools.partial(product_kernel, slots, columns), out_sha...  7.1 us
    pallas_call x2, Pallas kernels, transposed(): pl.pallas_call(transpose_kernel, out_shape=[jax.ShapeDtypeStruct((SIDE, p...  5.1 us
    unnamed x4, local copies, waits for them, and re-layouts  1.58 us
  transfers between devices with their start and end apart: 12, of which 10 were waited for; matrix products, arithmetic and copies ran while one was open for 2% of the time, Pallas kernels for 7%

commit v1 on v0

v1 whole, which is shorter than its diff:
```python
import functools

import jax
import jax.numpy as jnp
import numpy as np
from jax import lax
from jax.experimental import pallas as pl
from jax.experimental.pallas import tpu as pltpu
from jax.sharding import PartitionSpec as P


AXES = ("grp", "mem")
SIDE = 4
CORES = 2
STRIPE = 256
SENT = jnp.float16
F32 = jnp.float32


def limit(mib):
    return pltpu.CompilerParams(vmem_limit_bytes=mib * 1024 * 1024)


VMEM = pl.BlockSpec(memory_space=pltpu.VMEM)
SMEM = pl.BlockSpec(memory_space=pltpu.SMEM)
HBM = pl.BlockSpec(memory_space=pltpu.HBM)


def near(v):
    return v ^ 1


def far(v):
    return SIDE - 1 - v


def steps(dim, core):
    return (near, far) if core == (dim == 2) else (far, near)


def order(v, dim, core):
    first, second = steps(dim, core)
    return [v, second(v), first(v), second(first(v))]


def linear(y, c, x, z):
    return ((y * CORES + c) * SIDE + x) * SIDE + z


def everyone():
    return [(y, c, x, z) for y in range(SIDE) for c in range(CORES) for x in range(SIDE) for z in range(SIDE)]


def partners(*moves):
    pairs = []
    for place in everyone():
        target = list(place)
        for dim, turn in moves:
            target[dim] = steps(dim, place[1])[turn](target[dim])
        pairs.append((linear(*place), linear(*target)))
    return pairs


CORE_SWAP = [(linear(y, c, x, z), linear(y, 1 - c, x, z)) for y, c, x, z in everyone()]


def table():
    rows = []
    for y, c, x, z in everyone():
        z_order = order(z, 3, c)
        row = [c, *order(y, 0, c), *order(x, 2, c), *[z_order.index(v) for v in range(SIDE)]]
        rows.append(row + [0] * (16 - len(row)))
    return np.asarray(rows, np.int32)


def padded(depth):
    return -(-depth // 128) * 128


def front_kernel(base, where, flags, x_ref, *refs):
    x_all, x_t, scratch, sems = refs[-4:]
    before = refs[:-4]
    aux, occ, basis = x_ref.shape
    depth = aux * occ
    part = basis // (SIDE * CORES)
    chunk = part // SIDE
    pad = padded(depth) - depth
    copies = []
    for j in range(basis // STRIPE):
        columns = slice(j * STRIPE, (j + 1) * STRIPE)
        pair = [
            pltpu.make_async_copy(
                x_ref.at[a, :, columns], x_all.at[pl.ds(base + a * occ, occ), columns], sems.at[j, a]
            )
            for a in range(aux)
        ]
        for copy in pair:
            copy.start()
        copies.append(pair)
    if before:
        x_all[:base, :] = before[0][...]
        x_t[:, :, :, :base] = before[1][...]
    x_all[base + depth : base + depth + pad, :] = jnp.zeros((pad, basis), x_all.dtype)
    for j, pair in enumerate(copies):
        for copy in pair:
            copy.wait()
        columns = slice(j * STRIPE, (j + 1) * STRIPE)
        scratch[columns, :] = x_all[base : base + depth, columns].T
    for s in range(SIDE):
        at = pl.multiple_of((where[1 + s] * CORES + where[0]) * part, 16)
        block = scratch[pl.ds(at, part), :] * flags[...]
        block = jnp.concatenate([block, jnp.zeros((part, pad), block.dtype)], axis=1)
        for v in range(SIDE):
            x_t[s, v, :, base : base + depth + pad] = block[v * chunk : (v + 1) * chunk]


def front(where, flags, x, before):
    aux, occ, basis = x.shape
    depth = aux * occ
    chunk = basis // (SIDE * CORES * SIDE)
    base = padded(depth) if before else 0
    full = base + padded(depth)
    return pl.pallas_call(
        functools.partial(front_kernel, base),
        out_shape=[
            jax.ShapeDtypeStruct((full, basis), x.dtype),
            jax.ShapeDtypeStruct((SIDE, SIDE, chunk, full), x.dtype),
        ],
        in_specs=[SMEM, VMEM, HBM] + [VMEM] * len(before),
        out_specs=[VMEM] * 2,
        scratch_shapes=[pltpu.VMEM((basis, depth), x.dtype), pltpu.SemaphoreType.DMA((basis // STRIPE, aux))],
        compiler_params=limit(16),
    )(where, flags, x, *before)


def product_kernel(slots, where, x_all, x_t, out):
    chunk = x_t.shape[2]
    left = jnp.concatenate([x_t[i, where[5 + j]] for i, j in slots], axis=0)
    whole = jnp.dot(left, x_all[...], preferred_element_type=F32)
    for at in range(len(slots)):
        out[at] = whole[at * chunk : (at + 1) * chunk]


def product(where, x_all, x_t, slots):
    chunk, depth = x_t.shape[2:]
    basis = x_all.shape[1]
    rows = len(slots) * chunk
    return pl.pallas_call(
        functools.partial(product_kernel, slots),
        out_shape=jax.ShapeDtypeStruct((len(slots), chunk, basis), F32),
        in_specs=[SMEM, VMEM, VMEM],
        out_specs=VMEM,
        compiler_params=limit(16),
        cost_estimate=pl.CostEstimate(flops=2 * rows * depth * basis, bytes_accessed=4 * rows * basis, transcendentals=0),
    )(where, x_all, x_t)


def last_order_kernel(where, whole_ref, *refs):
    outs, scratch = refs[:-1], refs[-1]
    whole = whole_ref[...]
    rows = whole.shape[0] // SIDE
    for v in range(SIDE):
        scratch[where[9 + v]] = whole[v * rows : (v + 1) * rows]
    for slot, out in enumerate(outs):
        out[...] = scratch[slot]


def last_order(where, whole):
    rows, basis = whole.shape
    part = jax.ShapeDtypeStruct((rows // SIDE, basis), F32)
    return pl.pallas_call(
        last_order_kernel,
        out_shape=[part] * SIDE,
        in_specs=[SMEM, VMEM],
        out_specs=[VMEM] * SIDE,
        scratch_shapes=[pltpu.VMEM((SIDE, rows // SIDE, basis), F32)],
        compiler_params=limit(4),
    )(where, whole)


def go(v, *moves):
    return lax.ppermute(v, AXES, partners(*moves))


def narrow(v):
    return v.astype(SENT)


def wide(v):
    return v.astype(F32)


def on_device(factors, screen):
    where = lax.dynamic_index_in_dim(jnp.asarray(table()), lax.axis_index(AXES), 0, keepdims=False)
    other = lax.ppermute(factors, AXES, CORE_SWAP)
    other_screen = lax.ppermute(screen, AXES, CORE_SWAP)
    aux, occ, _ = factors.shape
    blocks = screen.shape[1]

    def flags_of(mask):
        kept = (mask == 1).astype(factors.dtype)
        return jnp.broadcast_to(kept[:, :, None], (aux, blocks, occ // blocks)).reshape(1, aux * occ)

    held = front(where, flags_of(screen), factors, ())
    x_all, x_t = front(where, flags_of(other_screen), other, held)

    def make(*slots):
        return product(where, x_all, x_t, slots)

    y_first, x_first, y_second, x_second = (0, 0), (2, 0), (0, 1), (2, 1)
    d_out = make((2, 2), (2, 3), (3, 2), (3, 3))
    d_in = go(narrow(d_out), y_first, x_first)
    y_out = make((2, 0), (2, 1), (3, 0), (3, 1))
    y_in = go(narrow(y_out), y_first)
    x_out = make((0, 2), (0, 3), (1, 2), (1, 3))
    x_in = go(narrow(x_out), x_first)
    kept = make((0, 0), (0, 1), (1, 0), (1, 1))

    def added(i):
        return kept[i] + wide(d_in[i]) + wide(y_in[i]) + wide(x_in[i])

    d_in2 = go(narrow(added(3)), y_second, x_second)
    y_in2 = go(narrow(added(2)), y_second)
    x_in2 = go(narrow(added(1)), x_second)
    whole = added(0) + wide(d_in2) + wide(y_in2) + wide(x_in2)
    kept, second, first, across = last_order(where, whole)
    z_across = go(across, (3, 0), (3, 1))
    z_second = go(second, (3, 1))
    z_first = go(first, (3, 0))
    return kept + z_second + z_first + z_across


def solution(mesh):
    placed = (P(AXES, None, None), P(AXES, None))
    return jax.shard_map(on_device, mesh=mesh, in_specs=placed, out_specs=P(AXES, None), check_vma=False)
```

time: 63 us -> 59.4 us (0.943)
  the two profiles are of different devices: /device:TPU:0 before, /device:TPU:1 now
where the time goes in v1:
time: 59.4 us; the launch traced here: 59 us
  waiting for transfers between devices  27.8 us (47%)
  starting transfers between devices  14 us (24%)
  Pallas kernels  12.3 us (21%)
  local copies, waits for them, and re-layouts  2.61 us (4%)
  other arithmetic  2.15 us (4%)
    ppermute x9, waiting for transfers between devices, go(): return lax.ppermute(v, AXES, partners(*moves))  27.8 us
    ppermute x9, starting transfers between devices, go(): return lax.ppermute(v, AXES, partners(*moves))  12.6 us
    pallas_call x4, Pallas kernels, product(): pl.pallas_call(functools.partial(product_kernel, slots), out_shape=jax.Sh...  7.01 us
    pallas_call x2, Pallas kernels, front(): pl.pallas_call(functools.partial(front_kernel, base), out_shape=[jax.Shap...  4.67 us
    unnamed x2, local copies, waits for them, and re-layouts  1.58 us
    ppermute x1, starting transfers between devices, on_device(): other = lax.ppermute(factors, AXES, CORE_SWAP)  1.38 us
  transfers between devices with their start and end apart: 11, of which 9 were waited for; matrix products, arithmetic and copies ran while one was open for 3% of the time, Pallas kernels for 6%

profile of v1, /device:TPU:1, one launch (start us, length us, event | category | flops | bytes accessed | tf_op | source)
XLA Modules:
  0.0 59.0 jit_solution(3609100108895897181)
XLA Ops:
  0.0 1.4 %collective-permute-start.1 = (bf16[2,288,1792]{2,1,0:T(8,128)(2,1)}, bf16[2,288,1792]{2,1,0:T(8,128)(2,1)}, u32[]{:S(2)}, u32[]{:S(2)}) collective-permute-start(bf16[2,288,1792]{2,1,0:T(8,128)(2,1)} %x_ref.1), channel_id=1, source_target_pairs={{0,16},{1,17},{2,18},{3,19},{4,20},{5,21},{6,22},{7,23},{8,24},{9,... | collective-permute-start | bytes 6193160 | tf_op jit(solution)/shard_map/ppermute | solution.py:195
  1.4 0.0 collective-permute-start
  1.4 0.7 %fusion.19 = bf16[18]{0:T(256)(128)(2,1)S(1)} fusion(s32[1,18]{1,0:T(1,128)} %param.4), kind=kLoop, calls=%fused_computation.26 | loop fusion | flops 36 | bytes 108 | tf_op jit(solution)/shard_map/broadcast_in_dim | solution.py:202
  2.0 0.1 broadcast_in_dim.27
  2.1 0.1 reshape.36.flags
  2.2 0.7 %dynamic-slice_bitcast_fusion.where = s32[16]{0:T(128)S(1)} fusion(s32[128,16]{1,0:T(8,128)} %constant.21.clone, s32[]{:T(128)S(6)} %select_n.4), kind=kLoop, calls=%fused_computation.27 | loop fusion | bytes 132 | tf_op jit(solution)/shard_map/jit(dynamic_index_in_dim)/squeeze | solution.py:194
  2.9 0.0 copy-start
  2.9 1.6 %copy-done = bf16[2,288,1792]{2,1,0:T(8,128)(2,1)S(1)} copy-done((bf16[2,288,1792]{2,1,0:T(8,128)(2,1)S(1)}, bf16[2,288,1792]{2,1,0:T(8,128)(2,1)}, u32[]{:S(2)}) %copy-start) | copy-done | bytes 2064408
  4.5 1.9 %shard_map.37 = (bf16[640,1792]{1,0:T(8,128)(2,1)S(1)}, bf16[4,4,56,640]{3,2,1,0:T(8,128)(2,1)S(1)}) custom-call(s32[16]{0:T(128)S(1)} %dynamic-slice_bitcast_fusion.where, bf16[1,576]{1,0:T(2,128)(2,1)S(1)} %reshape.36.flags, bf16[2,288,1792]{2,1,0:T(8,128)(2,1)S(1)} %copy-done), custom_call_target="tpu_custom_call" | custom-call | tf_op jit(solution)/shard_map/pallas_call | solution.py:123
  6.4 0.0 collective-permute-done
  6.4 0.1 broadcast_in_dim.24
  6.5 0.1 reshape.35.flags
  6.6 0.0 collective-permute-done.1.x_ref
  6.6 2.7 %shard_map.38 = (bf16[1280,1792]{1,0:T(8,128)(2,1)S(1)}, bf16[4,4,56,1280]{3,2,1,0:T(8,128)(2,1)S(1)}) custom-call(s32[16]{0:T(128)S(1)} %dynamic-slice_bitcast_fusion.where, bf16[1,576]{1,0:T(2,128)(2,1)S(1)} %reshape.35.flags, bf16[2,288,1792]{2,1,0:T(8,128)(2,1)} %collective-permute-done.1.x_ref, bf16[640,1792]{1,0:T(8,128)(2,1)S(1)} %get-tuple-element.13.refs_0_, ...), custom_call_target="tpu_custom_call" | custom-call | tf_op jit(solution)/shard_map/pallas_call | solution.py:123
  9.4 1.8 %shard_map.40 = f32[4,56,1792]{2,1,0:T(8,128)S(1)} custom-call(s32[16]{0:T(128)S(1)} %dynamic-slice_bitcast_fusion.where, bf16[1280,1792]{1,0:T(8,128)(2,1)S(1)} %get-tuple-element.15.x_all, bf16[4,4,56,1280]{3,2,1,0:T(8,128)(2,1)S(1)} %get-tuple-element.16.x_t), custom_call_target="tpu_custom_call" | custom-call | flops 1027604480 | bytes 1605632 | tf_op jit(solution)/shard_map/pallas_call | solution.py:148
  11.1 1.8 %shard_map.41 = f32[4,56,1792]{2,1,0:T(8,128)S(1)} custom-call(s32[16]{0:T(128)S(1)} %dynamic-slice_bitcast_fusion.where, bf16[1280,1792]{1,0:T(8,128)(2,1)S(1)} %get-tuple-element.15.x_all, bf16[4,4,56,1280]{3,2,1,0:T(8,128)(2,1)S(1)} %get-tuple-element.16.x_t), custom_call_target="tpu_custom_call" | custom-call | flops 1027604480 | bytes 1605632 | tf_op jit(solution)/shard_map/pallas_call | solution.py:148
  12.9 1.8 %shard_map.42 = f32[4,56,1792]{2,1,0:T(8,128)S(1)} custom-call(s32[16]{0:T(128)S(1)} %dynamic-slice_bitcast_fusion.where, bf16[1280,1792]{1,0:T(8,128)(2,1)S(1)} %get-tuple-element.15.x_all, bf16[4,4,56,1280]{3,2,1,0:T(8,128)(2,1)S(1)} %get-tuple-element.16.x_t), custom_call_target="tpu_custom_call" | custom-call | flops 1027604480 | bytes 1605632 | tf_op jit(solution)/shard_map/pallas_call | solution.py:148
  14.7 0.1 convert_element_type.71
  14.7 3.8 %collective-permute-start.2 = (f16[4,56,1792]{2,1,0:T(8,128)(2,1)S(1)}, f16[4,56,1792]{2,1,0:T(8,128)(2,1)S(1)}, u32[]{:S(2)}, u32[]{:S(2)}) collective-permute-start(f16[4,56,1792]{2,1,0:T(8,128)(2,1)S(1)} %convert_element_type.71), channel_id=1, source_target_pairs={{0,44},{1,45},{2,46},{3,47},{4,40},{5,41},{6,42},{7,43},{8,36},{9,... | collective-permute-start | bytes 2408456 | tf_op jit(solution)/shard_map/ppermute | solution.py:182
  18.6 0.1 convert_element_type.73
  18.7 0.1 collective-permute-start.3
  18.8 0.1 convert_element_type.75
  18.9 0.4 collective-permute-start.4
  19.2 1.7 %shard_map.39 = f32[4,56,1792]{2,1,0:T(8,128)S(1)} custom-call(s32[16]{0:T(128)S(1)} %dynamic-slice_bitcast_fusion.where, bf16[1280,1792]{1,0:T(8,128)(2,1)S(1)} %get-tuple-element.15.x_all, bf16[4,4,56,1280]{3,2,1,0:T(8,128)(2,1)S(1)} %get-tuple-element.16.x_t), custom_call_target="tpu_custom_call" | custom-call | flops 1027604480 | bytes 1605632 | tf_op jit(solution)/shard_map/pallas_call | solution.py:148
  21.0 7.5 %collective-permute-done.2 = f16[4,56,1792]{2,1,0:T(8,128)(2,1)S(1)} collective-permute-done((f16[4,56,1792]{2,1,0:T(8,128)(2,1)S(1)}, f16[4,56,1792]{2,1,0:T(8,128)(2,1)S(1)}, u32[]{:S(2)}, u32[]{:S(2)}) %collective-permute-start.2) | collective-permute-done | bytes 802848 | tf_op jit(solution)/shard_map/ppermute | solution.py:182
  28.5 8.6 %collective-permute-done.3 = f16[4,56,1792]{2,1,0:T(8,128)(2,1)S(1)} collective-permute-done((f16[4,56,1792]{2,1,0:T(8,128)(2,1)S(1)}, f16[4,56,1792]{2,1,0:T(8,128)(2,1)S(1)}, u32[]{:S(2)}, u32[]{:S(2)}) %collective-permute-start.3) | collective-permute-done | bytes 802848 | tf_op jit(solution)/shard_map/ppermute | solution.py:182
  37.0 0.3 collective-permute-done.4
  37.3 0.4 fusion.15
  37.7 2.1 %collective-permute-start.5 = (f16[56,1792]{1,0:T(8,128)(2,1)S(1)}, f16[56,1792]{1,0:T(8,128)(2,1)S(1)}, u32[]{:S(2)}, u32[]{:S(2)}) collective-permute-start(f16[56,1792]{1,0:T(8,128)(2,1)S(1)} %get-tuple-element.21), channel_id=1, source_target_pairs={{0,100},{1,101},{2,102},{3,103},{4,96},{5,97},{6,98},{7,99},{8,108... | collective-permute-start | bytes 602120 | tf_op jit(solution)/shard_map/ppermute | solution.py:182
  39.8 1.6 %collective-permute-start.6 = (f16[56,1792]{1,0:T(8,128)(2,1)S(1)}, f16[56,1792]{1,0:T(8,128)(2,1)S(1)}, u32[]{:S(2)}, u32[]{:S(2)}) collective-permute-start(f16[56,1792]{1,0:T(8,128)(2,1)S(1)} %get-tuple-element.23), channel_id=1, source_target_pairs={{0,96},{1,97},{2,98},{3,99},{4,100},{5,101},{6,102},{7,103},{8,104... | collective-permute-start | bytes 602120 | tf_op jit(solution)/shard_map/ppermute | solution.py:182
  41.5 0.2 collective-permute-start.7
  41.6 3.1 %collective-permute-done.5 = f16[56,1792]{1,0:T(8,128)(2,1)S(1)} collective-permute-done((f16[56,1792]{1,0:T(8,128)(2,1)S(1)}, f16[56,1792]{1,0:T(8,128)(2,1)S(1)}, u32[]{:S(2)}, u32[]{:S(2)}) %collective-permute-start.5) | collective-permute-done | bytes 200736 | tf_op jit(solution)/shard_map/ppermute | solution.py:182
  44.8 2.1 %collective-permute-done.6 = f16[56,1792]{1,0:T(8,128)(2,1)S(1)} collective-permute-done((f16[56,1792]{1,0:T(8,128)(2,1)S(1)}, f16[56,1792]{1,0:T(8,128)(2,1)S(1)}, u32[]{:S(2)}, u32[]{:S(2)}) %collective-permute-start.6) | collective-permute-done | bytes 200736 | tf_op jit(solution)/shard_map/ppermute | solution.py:182
  46.9 0.6 %collective-permute-done.7 = f16[56,1792]{1,0:T(8,128)(2,1)S(1)} collective-permute-done((f16[56,1792]{1,0:T(8,128)(2,1)S(1)}, f16[56,1792]{1,0:T(8,128)(2,1)S(1)}, u32[]{:S(2)}, u32[]{:S(2)}) %collective-permute-start.7) | collective-permute-done | bytes 200736 | tf_op jit(solution)/shard_map/ppermute | solution.py:182
  47.5 0.2 fusion.14.whole_ref
  47.7 0.6 %shard_map.43 = (f32[14,1792]{1,0:T(8,128)S(1)}, f32[14,1792]{1,0:T(8,128)S(1)}, f32[14,1792]{1,0:T(8,128)S(1)}, f32[14,1792]{1,0:T(8,128)S(1)}) custom-call(s32[16]{0:T(128)S(1)} %dynamic-slice_bitcast_fusion.where, f32[56,1792]{1,0:T(8,128)S(1)} %fusion.14.whole_ref), custom_call_target="tpu_custom_call" | custom-call | tf_op jit(solution)/shard_map/pallas_call | solution.py:171
  48.4 3.7 %collective-permute-start.10 = (f32[14,1792]{1,0:T(8,128)S(1)}, f32[14,1792]{1,0:T(8,128)S(1)}, u32[]{:S(2)}, u32[]{:S(2)}) collective-permute-start(f32[14,1792]{1,0:T(8,128)S(1)} %get-tuple-element.20), channel_id=1, source_target_pairs={{0,2},{1,3},{2,0},{3,1},{4,6},{5,7},{6,4},{7,5},{8,10},{9,11},{10,... | collective-permute-start | bytes 301064 | tf_op jit(solution)/shard_map/ppermute | solution.py:182
  52.0 0.7 %collective-permute-start.8 = (f32[14,1792]{1,0:T(8,128)S(1)}, f32[14,1792]{1,0:T(8,128)S(1)}, u32[]{:S(2)}, u32[]{:S(2)}) collective-permute-start(f32[14,1792]{1,0:T(8,128)S(1)} %get-tuple-element.18), channel_id=1, source_target_pairs={{0,3},{1,2},{2,1},{3,0},{4,7},{5,6},{6,5},{7,4},{8,11},{9,10},{10,... | collective-permute-start | bytes 301064 | tf_op jit(solution)/shard_map/ppermute | solution.py:182
  52.8 0.0 collective-permute-start.9
  52.8 1.4 %collective-permute-done.10 = f32[14,1792]{1,0:T(8,128)S(1)} collective-permute-done((f32[14,1792]{1,0:T(8,128)S(1)}, f32[14,1792]{1,0:T(8,128)S(1)}, u32[]{:S(2)}, u32[]{:S(2)}) %collective-permute-start.10) | collective-permute-done | bytes 100384 | tf_op jit(solution)/shard_map/ppermute | solution.py:182
  54.2 2.7 %collective-permute-done.8 = f32[14,1792]{1,0:T(8,128)S(1)} collective-permute-done((f32[14,1792]{1,0:T(8,128)S(1)}, f32[14,1792]{1,0:T(8,128)S(1)}, u32[]{:S(2)}, u32[]{:S(2)}) %collective-permute-start.8) | collective-permute-done | bytes 100384 | tf_op jit(solution)/shard_map/ppermute | solution.py:182
  56.9 1.5 %collective-permute-done.9 = f32[14,1792]{1,0:T(8,128)S(1)} collective-permute-done((f32[14,1792]{1,0:T(8,128)S(1)}, f32[14,1792]{1,0:T(8,128)S(1)}, u32[]{:S(2)}, u32[]{:S(2)}) %collective-permute-start.9) | collective-permute-done | bytes 100384 | tf_op jit(solution)/shard_map/ppermute | solution.py:182
  58.4 0.7 %add_add_fusion = f32[14,1792]{1,0:T(8,128)} fusion(f32[14,1792]{1,0:T(8,128)S(1)} %collective-permute-done.10, f32[14,1792]{1,0:T(8,128)S(1)} %collective-permute-done.9, f32[14,1792]{1,0:T(8,128)S(1)} %get-tuple-element.17, f32[14,1792]{1,0:T(8,128)S(1)} %collective-permute-done.8), kind=kLoop, calls=%fused_computation.22 | loop fusion | flops 75264 | bytes 501760 | tf_op jit(solution)/shard_map/add | solution.py:230
  (1 shorter events, 0.0 us)
Async XLA Ops:
  0.0 6.6 %collective-permute-start.1 = (bf16[2,288,1792]{2,1,0:T(8,128)(2,1)}, bf16[2,288,1792]{2,1,0:T(8,128)(2,1)}, u32[]{:S(2)}, u32[]{:S(2)}) collective-permute-start(bf16[2,288,1792]{2,1,0:T(8,128)(2,1)} %x_ref.1), channel_id=1, source_target_pairs={{0,16},{1,17},{2,18},{3,19},{4,20},{5,21},{6,22},{7,23},{8,24},{9,... | collective-permute-start | bytes 6193160 | tf_op jit(solution)/shard_map/ppermute | solution.py:195
  1.4 5.0 %collective-permute-start = (s32[1,18]{1,0:T(1,128)}, s32[1,18]{1,0:T(1,128)S(1)}, u32[]{:S(2)}, u32[]{:S(2)}) collective-permute-start(s32[1,18]{1,0:T(1,128)} %param.4), channel_id=1, source_target_pairs={{0,16},{1,17},{2,18},{3,19},{4,20},{5,21},{6,22},{7,23},{8,24},{9,... | collective-permute-start | bytes 224 | tf_op jit(solution)/shard_map/ppermute | solution.py:196
  2.9 1.6 %copy-start = (bf16[2,288,1792]{2,1,0:T(8,128)(2,1)S(1)}, bf16[2,288,1792]{2,1,0:T(8,128)(2,1)}, u32[]{:S(2)}) copy-start(bf16[2,288,1792]{2,1,0:T(8,128)(2,1)} %x_ref.1) | copy-start | bytes 6193156
  14.7 13.7 %collective-permute-start.2 = (f16[4,56,1792]{2,1,0:T(8,128)(2,1)S(1)}, f16[4,56,1792]{2,1,0:T(8,128)(2,1)S(1)}, u32[]{:S(2)}, u32[]{:S(2)}) collective-permute-start(f16[4,56,1792]{2,1,0:T(8,128)(2,1)S(1)} %convert_element_type.71), channel_id=1, source_target_pairs={{0,44},{1,45},{2,46},{3,47},{4,40},{5,41},{6,42},{7,43},{8,36},{9,... | collective-permute-start | bytes 2408456 | tf_op jit(solution)/shard_map/ppermute | solution.py:182
  18.7 18.4 %collective-permute-start.3 = (f16[4,56,1792]{2,1,0:T(8,128)(2,1)S(1)}, f16[4,56,1792]{2,1,0:T(8,128)(2,1)S(1)}, u32[]{:S(2)}, u32[]{:S(2)}) collective-permute-start(f16[4,56,1792]{2,1,0:T(8,128)(2,1)S(1)} %convert_element_type.73), channel_id=1, source_target_pairs={{0,32},{1,33},{2,34},{3,35},{4,36},{5,37},{6,38},{7,39},{8,40},{9,... | collective-permute-start | bytes 2408456 | tf_op jit(solution)/shard_map/ppermute | solution.py:182
  18.9 18.5 %collective-permute-start.4 = (f16[4,56,1792]{2,1,0:T(8,128)(2,1)S(1)}, f16[4,56,1792]{2,1,0:T(8,128)(2,1)S(1)}, u32[]{:S(2)}, u32[]{:S(2)}) collective-permute-start(f16[4,56,1792]{2,1,0:T(8,128)(2,1)S(1)} %convert_element_type.75), channel_id=1, source_target_pairs={{0,12},{1,13},{2,14},{3,15},{4,8},{5,9},{6,10},{7,11},{8,4},{9,5},... | collective-permute-start | bytes 2408456 | tf_op jit(solution)/shard_map/ppermute | solution.py:182
  37.7 7.0 %collective-permute-start.5 = (f16[56,1792]{1,0:T(8,128)(2,1)S(1)}, f16[56,1792]{1,0:T(8,128)(2,1)S(1)}, u32[]{:S(2)}, u32[]{:S(2)}) collective-permute-start(f16[56,1792]{1,0:T(8,128)(2,1)S(1)} %get-tuple-element.21), channel_id=1, source_target_pairs={{0,100},{1,101},{2,102},{3,103},{4,96},{5,97},{6,98},{7,99},{8,108... | collective-permute-start | bytes 602120 | tf_op jit(solution)/shard_map/ppermute | solution.py:182
  39.8 7.1 %collective-permute-start.6 = (f16[56,1792]{1,0:T(8,128)(2,1)S(1)}, f16[56,1792]{1,0:T(8,128)(2,1)S(1)}, u32[]{:S(2)}, u32[]{:S(2)}) collective-permute-start(f16[56,1792]{1,0:T(8,128)(2,1)S(1)} %get-tuple-element.23), channel_id=1, source_target_pairs={{0,96},{1,97},{2,98},{3,99},{4,100},{5,101},{6,102},{7,103},{8,104... | collective-permute-start | bytes 602120 | tf_op jit(solution)/shard_map/ppermute | solution.py:182
  41.5 6.1 %collective-permute-start.7 = (f16[56,1792]{1,0:T(8,128)(2,1)S(1)}, f16[56,1792]{1,0:T(8,128)(2,1)S(1)}, u32[]{:S(2)}, u32[]{:S(2)}) collective-permute-start(f16[56,1792]{1,0:T(8,128)(2,1)S(1)} %get-tuple-element.22), channel_id=1, source_target_pairs={{0,4},{1,5},{2,6},{3,7},{4,0},{5,1},{6,2},{7,3},{8,12},{9,13},{10,... | collective-permute-start | bytes 602120 | tf_op jit(solution)/shard_map/ppermute | solution.py:182
  48.4 5.9 %collective-permute-start.10 = (f32[14,1792]{1,0:T(8,128)S(1)}, f32[14,1792]{1,0:T(8,128)S(1)}, u32[]{:S(2)}, u32[]{:S(2)}) collective-permute-start(f32[14,1792]{1,0:T(8,128)S(1)} %get-tuple-element.20), channel_id=1, source_target_pairs={{0,2},{1,3},{2,0},{3,1},{4,6},{5,7},{6,4},{7,5},{8,10},{9,11},{10,... | collective-permute-start | bytes 301064 | tf_op jit(solution)/shard_map/ppermute | solution.py:182
  52.0 4.8 %collective-permute-start.8 = (f32[14,1792]{1,0:T(8,128)S(1)}, f32[14,1792]{1,0:T(8,128)S(1)}, u32[]{:S(2)}, u32[]{:S(2)}) collective-permute-start(f32[14,1792]{1,0:T(8,128)S(1)} %get-tuple-element.18), channel_id=1, source_target_pairs={{0,3},{1,2},{2,1},{3,0},{4,7},{5,6},{6,5},{7,4},{8,11},{9,10},{10,... | collective-permute-start | bytes 301064 | tf_op jit(solution)/shard_map/ppermute | solution.py:182
  52.8 5.6 %collective-permute-start.9 = (f32[14,1792]{1,0:T(8,128)S(1)}, f32[14,1792]{1,0:T(8,128)S(1)}, u32[]{:S(2)}, u32[]{:S(2)}) collective-permute-start(f32[14,1792]{1,0:T(8,128)S(1)} %get-tuple-element.19), channel_id=1, source_target_pairs={{0,1},{1,0},{2,3},{3,2},{4,5},{5,4},{6,7},{7,6},{8,9},{9,8},{10,11... | collective-permute-start | bytes 301064 | tf_op jit(solution)/shard_map/ppermute | solution.py:182

commit v2 on v1

v2 whole, which is shorter than its diff:
```python
import functools

import jax
import jax.numpy as jnp
from jax import lax
from jax.experimental import pallas as pl
from jax.experimental.pallas import tpu as pltpu
from jax.sharding import PartitionSpec as P


AXES = ("grp", "mem")
SIDE = 4
CORES = 2
STRIPE = 256
SENT = jnp.float16
ROOM = 16384.0
SMALLEST = 2.0**-60
F32 = jnp.float32


def limit(mib):
    return pltpu.CompilerParams(vmem_limit_bytes=mib * 1024 * 1024)


VMEM = pl.BlockSpec(memory_space=pltpu.VMEM)
SMEM = pl.BlockSpec(memory_space=pltpu.SMEM)
HBM = pl.BlockSpec(memory_space=pltpu.HBM)


def near(v):
    return v ^ 1


def far(v):
    return SIDE - 1 - v


def steps(dim, core):
    return (near, far) if core == (dim == 2) else (far, near)


def linear(y, c, x, z):
    return ((y * CORES + c) * SIDE + x) * SIDE + z


def everyone():
    return [(y, c, x, z) for y in range(SIDE) for c in range(CORES) for x in range(SIDE) for z in range(SIDE)]


def partners(*moves):
    pairs = []
    for place in everyone():
        target = list(place)
        for dim, turn in moves:
            target[dim] = steps(dim, place[1])[turn](target[dim])
        pairs.append((linear(*place), linear(*target)))
    return pairs


CORE_SWAP = [(linear(y, c, x, z), linear(y, 1 - c, x, z)) for y, c, x, z in everyone()]


def here():
    group, member = lax.axis_index("grp"), lax.axis_index("mem")
    return lax.div(group, CORES), lax.rem(group, CORES), lax.div(member, SIDE), lax.rem(member, SIDE)


def order_here(v, dim, core):
    near_first = core == int(dim == 2)
    close, distant = v ^ 1, SIDE - 1 - v
    first, second = jnp.where(near_first, close, distant), jnp.where(near_first, distant, close)
    return [v, second, first, v ^ 2]


def bound(most, terms):
    return terms * most * most


def front_kernel(track, screen, x_ref, *refs):
    scratch, sems = refs[-2:]
    if track:
        x_out, x_t, *tail = refs[:-2]
    else:
        x_out, x_t = refs[2:4]
        tail = (*refs[:2], *refs[4:-2])
    y, core, _, _ = here()
    aux, occ, basis = x_ref.shape
    depth = aux * occ
    blocks = screen.shape[1]
    part = basis // (SIDE * CORES)
    chunk = part // SIDE
    copies = []
    for j in range(basis // STRIPE):
        columns = slice(j * STRIPE, (j + 1) * STRIPE)
        pair = [
            pltpu.make_async_copy(x_ref.at[a, :, columns], x_out.at[pl.ds(a * occ, occ), columns], sems.at[j, a])
            for a in range(aux)
        ]
        for copy in pair:
            copy.start()
        copies.append(pair)
    lane = lax.broadcasted_iota(jnp.int32, (16, depth), 1)
    block_of = lax.div(lax.rem(lane, occ), occ // blocks)
    flags = jnp.zeros((16, depth), F32)
    for b in range(blocks):
        flags = jnp.where(block_of == b, (screen[0, b] == 1).astype(F32), flags)
    flags = flags.astype(x_out.dtype)
    most = jnp.zeros((16, depth), x_out.dtype)
    for j, pair in enumerate(copies):
        for copy in pair:
            copy.wait()
        columns = slice(j * STRIPE, (j + 1) * STRIPE)
        turned = x_out[:, columns].T
        scratch[columns, :] = turned
        if track:
            sizes = jnp.abs(turned)
            for r in range(0, STRIPE, 16):
                most = jnp.maximum(most, sizes[r : r + 16])
    if track:
        most = (most * flags).astype(F32)
        top = jnp.max(jnp.max(most, axis=1, keepdims=True), axis=0, keepdims=True)
        tail[0][...] = jnp.broadcast_to(top, tail[0].shape)
    else:
        top = jnp.maximum(jnp.maximum(tail[0][...], tail[1][...]), SMALLEST)
        tail[2][...] = top
    for s, at in enumerate(order_here(y, 0, core)):
        first = pl.multiple_of((at * CORES + core) * part, 16)
        block = scratch[pl.ds(first, part), :] * flags[0:1]
        for v in range(SIDE):
            x_t[s, v] = block[v * chunk : (v + 1) * chunk]


def front(screen, x, peaks):
    aux, occ, basis = x.shape
    depth = aux * occ
    shapes = [
        jax.ShapeDtypeStruct((depth, basis), x.dtype),
        jax.ShapeDtypeStruct((SIDE, SIDE, basis // (SIDE * CORES * SIDE), depth), x.dtype),
        jax.ShapeDtypeStruct((8, 128), F32),
    ]
    return pl.pallas_call(
        functools.partial(front_kernel, not peaks),
        out_shape=shapes,
        in_specs=[SMEM, HBM] + [VMEM] * len(peaks),
        out_specs=[VMEM] * len(shapes),
        scratch_shapes=[pltpu.VMEM((basis, depth), x.dtype), pltpu.SemaphoreType.DMA((basis // STRIPE, aux))],
        compiler_params=limit(16),
    )(screen, x, *peaks)


def product_kernel(slots, x_own, t_own, x_other, t_other, *refs):
    out = refs[-1]
    _, core, x, _ = here()
    x_order = order_here(x, 2, core)
    chunk = t_own.shape[2]

    def left(x_t):
        return jnp.concatenate([x_t[i, x_order[j]] for i, j in slots], axis=0)

    whole = jnp.dot(left(t_own), x_own[...], preferred_element_type=F32)
    whole = whole + jnp.dot(left(t_other), x_other[...], preferred_element_type=F32)
    if len(refs) > 1:
        whole = whole * (ROOM / bound(refs[0][0:1, 0:1], CORES * x_own.shape[0]))
    for at in range(len(slots)):
        out[at] = whole[at * chunk : (at + 1) * chunk]


def product(parts, slots):
    chunk, depth = parts[1].shape[2:]
    basis = parts[0].shape[1]
    rows = len(slots) * chunk
    return pl.pallas_call(
        functools.partial(product_kernel, slots),
        out_shape=jax.ShapeDtypeStruct((len(slots), chunk, basis), F32),
        in_specs=[VMEM] * len(parts),
        out_specs=VMEM,
        compiler_params=limit(16),
        cost_estimate=pl.CostEstimate(flops=4 * rows * depth * basis, bytes_accessed=4 * rows * basis, transcendentals=0),
    )(*parts)


def power(e):
    return jnp.exp2(e).astype(jnp.bfloat16).astype(F32)


def settle_kernel(terms, kept, *refs):
    arrived, tiles, outs = refs[:3], refs[3:7], refs[7:]
    most = tiles[0][0:1, 0:1]
    rates = []
    for tile in tiles[1:]:
        most = jnp.maximum(most, tile[0:1, 0:1])
        rates.append(bound(tile[0:1, 0:1], terms) / ROOM)
    quarter = jnp.ceil(jnp.log2(bound(most, SIDE * terms) / ROOM) * 0.25)
    one = jnp.floor(quarter / 3)
    two = jnp.floor((quarter - one) / 2)
    scale = power(-4 * quarter)
    rows, basis = kept.shape[1:]
    for slot, out in enumerate(outs):
        whole = kept[slot]
        for block, rate in zip(arrived, rates):
            whole = whole + block[slot] * rate
        out[:rows] = whole * scale if slot else whole
        if slot:
            at = lax.broadcasted_iota(jnp.int32, (8, basis), 0)
            third = quarter - one - two
            out[rows : rows + 8] = power(jnp.where(at == 0, one, jnp.where(at == 1, two, third)))


def settle(terms, kept, arrived, tiles):
    rows, basis = kept.shape[1:]
    shapes = [jax.ShapeDtypeStruct((rows, basis), F32)]
    shapes += [jax.ShapeDtypeStruct((rows + 8, basis), F32)] * (SIDE - 1)
    return pl.pallas_call(
        functools.partial(settle_kernel, terms),
        out_shape=shapes,
        in_specs=[VMEM] * 8,
        out_specs=[VMEM] * SIDE,
        compiler_params=limit(8),
    )(kept, *arrived, *tiles)


def last_kernel(kept, *refs):
    arrived, outs, scratch = refs[:3], refs[3:-1], refs[-1]
    _, core, _, z = here()
    whole = kept[...]
    high = whole.shape[0]
    for block in arrived:
        rate = block[high : high + 1, 0:1] * block[high + 1 : high + 2, 0:1] * block[high + 2 : high + 3, 0:1]
        rate = rate * rate
        whole = whole + block[:high] * (rate * rate)
    rows = high // SIDE
    for v in range(SIDE):
        scratch[v] = whole[v * rows : (v + 1) * rows]
    for slot, out in zip(order_here(z, 3, core), outs):
        out[...] = scratch[slot]


def last(kept, arrived):
    rows, basis = kept.shape
    part = jax.ShapeDtypeStruct((rows // SIDE, basis), F32)
    return pl.pallas_call(
        last_kernel,
        out_shape=[part] * SIDE,
        in_specs=[VMEM] * 4,
        out_specs=[VMEM] * SIDE,
        scratch_shapes=[pltpu.VMEM((SIDE, rows // SIDE, basis), F32)],
        compiler_params=limit(4),
    )(kept, *arrived)


def go(v, *moves):
    return lax.ppermute(v, AXES, partners(*moves))


def on_device(factors, screen):
    other = lax.ppermute(factors, AXES, CORE_SWAP)
    other_screen = lax.ppermute(screen, AXES, CORE_SWAP)
    depth = CORES * factors.shape[0] * factors.shape[1]

    x_own, t_own, peak = front(screen, factors, ())
    x_other, t_other, peak = front(other_screen, other, (peak, lax.ppermute(peak, AXES, CORE_SWAP)))
    parts = (x_own, t_own, x_other, t_other)

    def narrow(v):
        return v.astype(SENT)

    def wide(v):
        return v.astype(F32)

    d_moves, y_moves, x_moves = ((0, 0), (2, 0)), ((0, 0),), ((2, 0),)
    d_out = product((*parts, peak), ((2, 2), (2, 3), (3, 2), (3, 3)))
    d_in = go(narrow(d_out), *d_moves)
    y_out = product((*parts, peak), ((2, 0), (2, 1), (3, 0), (3, 1)))
    y_in = go(narrow(y_out), *y_moves)
    x_out = product((*parts, peak), ((0, 2), (0, 3), (1, 2), (1, 3)))
    x_in = go(narrow(x_out), *x_moves)
    kept = product(parts, ((0, 0), (0, 1), (1, 0), (1, 1)))
    d_most = go(peak, *d_moves)
    y_most = go(peak, *y_moves)
    x_most = go(peak, *x_moves)
    kept, x_out, y_out, d_out = settle(
        depth, kept, (wide(d_in), wide(y_in), wide(x_in)), (peak, d_most, y_most, x_most)
    )

    d_moves, y_moves, x_moves = ((0, 1), (2, 1)), ((0, 1),), ((2, 1),)
    d_in = go(narrow(d_out), *d_moves)
    y_in = go(narrow(y_out), *y_moves)
    x_in = go(narrow(x_out), *x_moves)
    kept, second, first, across = last(kept, (wide(d_in), wide(y_in), wide(x_in)))
    z_across = go(across, (3, 0), (3, 1))
    z_second = go(second, (3, 1))
    z_first = go(first, (3, 0))
    return kept + z_second + z_first + z_across


def solution(mesh):
    placed = (P(AXES, None, None), P(AXES, None))
    return jax.shard_map(on_device, mesh=mesh, in_specs=placed, out_specs=P(AXES, None), check_vma=False)
```

time: 59.4 us -> 60 us (1.010)
  the two profiles are of different devices: /device:TPU:1 before, /device:TPU:0 now
where the time goes in v2:
time: 60 us; the launch traced here: 59.8 us
  starting transfers between devices  23.4 us (39%)
  waiting for transfers between devices  21.9 us (36%)
  Pallas kernels  10.7 us (18%)
  local copies, waits for them, and re-layouts  2.23 us (4%)
  other arithmetic  1.41 us (2%)
    ppermute x12, starting transfers between devices, go(): return lax.ppermute(v, AXES, partners(*moves))  22.8 us
    ppermute x12, waiting for transfers between devices, go(): return lax.ppermute(v, AXES, partners(*moves))  20.8 us
    pallas_call x4, Pallas kernels, product(): pl.pallas_call(functools.partial(product_kernel, slots), out_shape=jax.Sh...  5.64 us
    pallas_call x2, Pallas kernels, front(): pl.pallas_call(functools.partial(front_kernel, not peaks), out_shape=shap...  3.93 us
    unnamed x4, local copies, waits for them, and re-layouts  2.23 us
  transfers between devices with their start and end apart: 15, of which 9 were waited for; matrix products, arithmetic and copies ran while one was open for 1% of the time, Pallas kernels for 10%

profile of v2, /device:TPU:0, one launch (start us, length us, event | category | flops | bytes accessed | tf_op | source)
XLA Modules:
  0.0 59.8 jit_solution(18251371365810101186)
XLA Ops:
  0.0 0.0 collective-permute-start.1
  0.0 0.0 copy-start
  0.0 1.6 %copy-done = bf16[2,288,1792]{2,1,0:T(8,128)(2,1)S(1)} copy-done((bf16[2,288,1792]{2,1,0:T(8,128)(2,1)S(1)}, bf16[2,288,1792]{2,1,0:T(8,128)(2,1)}, u32[]{:S(2)}) %copy-start) | copy-done | bytes 2064408
  1.6 0.7 %copy-done.1 = s32[1,18]{1,0:T(1,128)S(1)} copy-done((s32[1,18]{1,0:T(1,128)S(1)}, s32[1,18]{1,0:T(1,128)}, u32[]{:S(2)}) %copy-start.1) | copy-done | bytes 96
  2.2 2.0 %shard_map.28 = (bf16[576,1792]{1,0:T(8,128)(2,1)S(1)}, bf16[4,4,56,576]{3,2,1,0:T(8,128)(2,1)S(1)}, f32[8,128]{1,0:T(8,128)S(1)}) custom-call(s32[1,18]{1,0:T(1,128)S(1)} %copy-done.1, bf16[2,288,1792]{2,1,0:T(8,128)(2,1)S(1)} %copy-done), custom_call_target="tpu_custom_call" | custom-call | tf_op jit(solution)/shard_map/pallas_call | solution.py:141
  4.2 0.6 collective-permute-start.2
  4.8 0.1 collective-permute-start
  4.9 1.1 %collective-permute-done.screen = s32[1,18]{1,0:T(1,128)S(1)} collective-permute-done((s32[1,18]{1,0:T(1,128)S(1)}, s32[1,18]{1,0:T(1,128)S(1)}, u32[]{:S(2)}, u32[]{:S(2)}) %collective-permute-start) | collective-permute-done | bytes 104 | tf_op jit(solution)/shard_map/ppermute | solution.py:257
  6.0 0.0 collective-permute-done.2.refs_1_
  6.0 0.0 collective-permute-done.1.x_ref
  6.0 2.0 %shard_map.29 = (bf16[576,1792]{1,0:T(8,128)(2,1)S(1)}, bf16[4,4,56,576]{3,2,1,0:T(8,128)(2,1)S(1)}, f32[8,128]{1,0:T(8,128)S(1)}) custom-call(s32[1,18]{1,0:T(1,128)S(1)} %collective-permute-done.screen, bf16[2,288,1792]{2,1,0:T(8,128)(2,1)S(1)} %collective-permute-done.1.x_ref, f32[8,128]{1,0:T(8,128)S(1)} %get-tuple-element.21.refs_0_, ...), custom_call_target="tpu_custom_call" | custom-call | tf_op jit(solution)/shard_map/pallas_call | solution.py:141
  7.9 1.4 %shard_map.33 = f32[4,56,1792]{2,1,0:T(8,128)S(1)} custom-call(bf16[576,1792]{1,0:T(8,128)(2,1)S(1)} %get-tuple-element.19.x_own, bf16[4,4,56,576]{3,2,1,0:T(8,128)(2,1)S(1)} %get-tuple-element.20.t_own, bf16[576,1792]{1,0:T(8,128)(2,1)S(1)} %get-tuple-element.22.x_other, bf16[4,4,56,576]{3,2,1,0:T(8,128)(2,1)S(1)} %get-tuple-element.23.t_other, ...), custom_call_target="tpu_custom_call" | custom-call | flops 924844032 | bytes 1605632 | tf_op jit(solution)/shard_map/pallas_call | solution.py:172
  9.4 0.1 convert_element_type.40
  9.4 3.0 %collective-permute-start.5 = (f16[4,56,1792]{2,1,0:T(8,128)(2,1)S(1)}, f16[4,56,1792]{2,1,0:T(8,128)(2,1)S(1)}, u32[]{:S(2)}, u32[]{:S(2)}) collective-permute-start(f16[4,56,1792]{2,1,0:T(8,128)(2,1)S(1)} %convert_element_type.40), channel_id=1, source_target_pairs={{0,12},{1,13},{2,14},{3,15},{4,8},{5,9},{6,10},{7,11},{8,4},{9,5},... | collective-permute-start | bytes 2408456 | tf_op jit(solution)/shard_map/ppermute | solution.py:252
  12.4 1.4 %shard_map.32 = f32[4,56,1792]{2,1,0:T(8,128)S(1)} custom-call(bf16[576,1792]{1,0:T(8,128)(2,1)S(1)} %get-tuple-element.19.x_own, bf16[4,4,56,576]{3,2,1,0:T(8,128)(2,1)S(1)} %get-tuple-element.20.t_own, bf16[576,1792]{1,0:T(8,128)(2,1)S(1)} %get-tuple-element.22.x_other, bf16[4,4,56,576]{3,2,1,0:T(8,128)(2,1)S(1)} %get-tuple-element.23.t_other, ...), custom_call_target="tpu_custom_call" | custom-call | flops 924844032 | bytes 1605632 | tf_op jit(solution)/shard_map/pallas_call | solution.py:172
  13.8 0.1 convert_element_type.38
  13.9 1.4 %shard_map.31 = f32[4,56,1792]{2,1,0:T(8,128)S(1)} custom-call(bf16[576,1792]{1,0:T(8,128)(2,1)S(1)} %get-tuple-element.19.x_own, bf16[4,4,56,576]{3,2,1,0:T(8,128)(2,1)S(1)} %get-tuple-element.20.t_own, bf16[576,1792]{1,0:T(8,128)(2,1)S(1)} %get-tuple-element.22.x_other, bf16[4,4,56,576]{3,2,1,0:T(8,128)(2,1)S(1)} %get-tuple-element.23.t_other, ...), custom_call_target="tpu_custom_call" | custom-call | flops 924844032 | bytes 1605632 | tf_op jit(solution)/shard_map/pallas_call | solution.py:172
  15.3 1.7 %collective-permute-start.4 = (f16[4,56,1792]{2,1,0:T(8,128)(2,1)S(1)}, f16[4,56,1792]{2,1,0:T(8,128)(2,1)S(1)}, u32[]{:S(2)}, u32[]{:S(2)}) collective-permute-start(f16[4,56,1792]{2,1,0:T(8,128)(2,1)S(1)} %convert_element_type.38), channel_id=1, source_target_pairs={{0,32},{1,33},{2,34},{3,35},{4,36},{5,37},{6,38},{7,39},{8,40},{9,... | collective-permute-start | bytes 2408456 | tf_op jit(solution)/shard_map/ppermute | solution.py:252
  17.0 0.1 convert_element_type.36
  17.1 0.3 collective-permute-start.3
  17.4 3.9 %collective-permute-start.6 = (f32[8,128]{1,0:T(8,128)S(1)}, f32[8,128]{1,0:T(8,128)S(1)}, u32[]{:S(2)}, u32[]{:S(2)}) collective-permute-start(f32[8,128]{1,0:T(8,128)S(1)} %get-tuple-element.24.refs_0_.refs_3_), channel_id=1, source_target_pairs={{0,44},{1,45},{2,46},{3,47},{4,40},{5,41},{6,42},{7,43},{8,36},{9,... | collective-permute-start | bytes 12296 | tf_op jit(solution)/shard_map/ppermute | solution.py:252
  21.3 0.4 collective-permute-start.7
  21.7 1.2 %collective-permute-done.5 = f16[4,56,1792]{2,1,0:T(8,128)(2,1)S(1)} collective-permute-done((f16[4,56,1792]{2,1,0:T(8,128)(2,1)S(1)}, f16[4,56,1792]{2,1,0:T(8,128)(2,1)S(1)}, u32[]{:S(2)}, u32[]{:S(2)}) %collective-permute-start.5) | collective-permute-done | bytes 802848 | tf_op jit(solution)/shard_map/ppermute | solution.py:252
  22.9 2.9 %collective-permute-start.8 = (f32[8,128]{1,0:T(8,128)S(1)}, f32[8,128]{1,0:T(8,128)S(1)}, u32[]{:S(2)}, u32[]{:S(2)}) collective-permute-start(f32[8,128]{1,0:T(8,128)S(1)} %get-tuple-element.24.refs_0_.refs_3_), channel_id=1, source_target_pairs={{0,12},{1,13},{2,14},{3,15},{4,8},{5,9},{6,10},{7,11},{8,4},{9,5},... | collective-permute-start | bytes 12296 | tf_op jit(solution)/shard_map/ppermute | solution.py:252
  25.8 1.4 %shard_map.30.kept = f32[4,56,1792]{2,1,0:T(8,128)S(1)} custom-call(bf16[576,1792]{1,0:T(8,128)(2,1)S(1)} %get-tuple-element.19.x_own, bf16[4,4,56,576]{3,2,1,0:T(8,128)(2,1)S(1)} %get-tuple-element.20.t_own, bf16[576,1792]{1,0:T(8,128)(2,1)S(1)} %get-tuple-element.22.x_other, bf16[4,4,56,576]{3,2,1,0:T(8,128)(2,1)S(1)} %get-tuple-element.23.t_other), custom_call_target="tpu_custom_call" | custom-call | flops 924844032 | bytes 1605632 | tf_op jit(solution)/shard_map/pallas_call | solution.py:172
  27.2 0.1 convert_element_type.41.refs_2_
  27.3 8.9 %collective-permute-done.4 = f16[4,56,1792]{2,1,0:T(8,128)(2,1)S(1)} collective-permute-done((f16[4,56,1792]{2,1,0:T(8,128)(2,1)S(1)}, f16[4,56,1792]{2,1,0:T(8,128)(2,1)S(1)}, u32[]{:S(2)}, u32[]{:S(2)}) %collective-permute-start.4) | collective-permute-done | bytes 802848 | tf_op jit(solution)/shard_map/ppermute | solution.py:252
  36.2 0.1 convert_element_type.39.refs_1_
  36.3 0.0 collective-permute-done.3
  36.3 0.1 convert_element_type.37.refs_0_
  36.5 0.0 collective-permute-done.6.refs_4_
  36.5 0.0 collective-permute-done.7.refs_5_
  36.5 0.0 collective-permute-done.8.refs_6_
  36.5 0.8 %shard_map.34 = (f32[56,1792]{1,0:T(8,128)S(1)}, f32[64,1792]{1,0:T(8,128)S(1)}, f32[64,1792]{1,0:T(8,128)S(1)}, f32[64,1792]{1,0:T(8,128)S(1)}) custom-call(f32[4,56,1792]{2,1,0:T(8,128)S(1)} %shard_map.30.kept, f32[4,56,1792]{2,1,0:T(8,128)S(1)} %convert_element_type.37.refs_0_, f32[4,56,1792]{2,1,0:T(8,128)S(1)} %convert_element_type.39.refs_1_, ...), custom_call_target="tpu_custom_call" | custom-call | tf_op jit(solution)/shard_map/pallas_call | solution.py:213
  37.4 2.8 %collective-permute-start.9 = (f16[64,1792]{1,0:T(8,128)(2,1)S(1)}, f16[64,1792]{1,0:T(8,128)(2,1)S(1)}, u32[]{:S(2)}, u32[]{:S(2)}) collective-permute-start(f16[64,1792]{1,0:T(8,128)(2,1)S(1)} %convert_element_type.42), channel_id=1, source_target_pairs={{0,100},{1,101},{2,102},{3,103},{4,96},{5,97},{6,98},{7,99},{8,108... | collective-permute-start | bytes 688136 | tf_op jit(solution)/shard_map/ppermute | solution.py:252
  40.1 0.4 collective-permute-start.10
  40.6 1.7 %collective-permute-start.11 = (f16[64,1792]{1,0:T(8,128)(2,1)S(1)}, f16[64,1792]{1,0:T(8,128)(2,1)S(1)}, u32[]{:S(2)}, u32[]{:S(2)}) collective-permute-start(f16[64,1792]{1,0:T(8,128)(2,1)S(1)} %convert_element_type.46), channel_id=1, source_target_pairs={{0,4},{1,5},{2,6},{3,7},{4,0},{5,1},{6,2},{7,3},{8,12},{9,13},{10,... | collective-permute-start | bytes 688136 | tf_op jit(solution)/shard_map/ppermute | solution.py:252
  42.4 3.3 %collective-permute-done.9 = f16[64,1792]{1,0:T(8,128)(2,1)S(1)} collective-permute-done((f16[64,1792]{1,0:T(8,128)(2,1)S(1)}, f16[64,1792]{1,0:T(8,128)(2,1)S(1)}, u32[]{:S(2)}, u32[]{:S(2)}) %collective-permute-start.9) | collective-permute-done | bytes 229408 | tf_op jit(solution)/shard_map/ppermute | solution.py:252
  45.7 2.4 %collective-permute-done.10 = f16[64,1792]{1,0:T(8,128)(2,1)S(1)} collective-permute-done((f16[64,1792]{1,0:T(8,128)(2,1)S(1)}, f16[64,1792]{1,0:T(8,128)(2,1)S(1)}, u32[]{:S(2)}, u32[]{:S(2)}) %collective-permute-start.10) | collective-permute-done | bytes 229408 | tf_op jit(solution)/shard_map/ppermute | solution.py:252
  48.1 0.4 collective-permute-done.11
  48.4 0.3 shard_map.35
  48.7 4.1 %collective-permute-start.12 = (f32[14,1792]{1,0:T(8,128)S(1)}, f32[14,1792]{1,0:T(8,128)S(1)}, u32[]{:S(2)}, u32[]{:S(2)}) collective-permute-start(f32[14,1792]{1,0:T(8,128)S(1)} %get-tuple-element.30), channel_id=1, source_target_pairs={{0,3},{1,2},{2,1},{3,0},{4,7},{5,6},{6,5},{7,4},{8,11},{9,10},{10,... | collective-permute-start | bytes 301064 | tf_op jit(solution)/shard_map/ppermute | solution.py:252
  52.9 0.0 collective-permute-start.13
  52.9 1.6 %collective-permute-start.14 = (f32[14,1792]{1,0:T(8,128)S(1)}, f32[14,1792]{1,0:T(8,128)S(1)}, u32[]{:S(2)}, u32[]{:S(2)}) collective-permute-start(f32[14,1792]{1,0:T(8,128)S(1)} %get-tuple-element.32), channel_id=1, source_target_pairs={{0,2},{1,3},{2,0},{3,1},{4,6},{5,7},{6,4},{7,5},{8,10},{9,11},{10,... | collective-permute-start | bytes 301064 | tf_op jit(solution)/shard_map/ppermute | solution.py:252
  54.4 2.3 %collective-permute-done.12 = f32[14,1792]{1,0:T(8,128)S(1)} collective-permute-done((f32[14,1792]{1,0:T(8,128)S(1)}, f32[14,1792]{1,0:T(8,128)S(1)}, u32[]{:S(2)}, u32[]{:S(2)}) %collective-permute-start.12) | collective-permute-done | bytes 100384 | tf_op jit(solution)/shard_map/ppermute | solution.py:252
  56.7 1.0 %collective-permute-done.13 = f32[14,1792]{1,0:T(8,128)S(1)} collective-permute-done((f32[14,1792]{1,0:T(8,128)S(1)}, f32[14,1792]{1,0:T(8,128)S(1)}, u32[]{:S(2)}, u32[]{:S(2)}) %collective-permute-start.13) | collective-permute-done | bytes 100384 | tf_op jit(solution)/shard_map/ppermute | solution.py:252
  57.7 1.5 %collective-permute-done.14 = f32[14,1792]{1,0:T(8,128)S(1)} collective-permute-done((f32[14,1792]{1,0:T(8,128)S(1)}, f32[14,1792]{1,0:T(8,128)S(1)}, u32[]{:S(2)}, u32[]{:S(2)}) %collective-permute-start.14) | collective-permute-done | bytes 100384 | tf_op jit(solution)/shard_map/ppermute | solution.py:252
  59.2 0.7 %add_add_fusion = f32[14,1792]{1,0:T(8,128)} fusion(f32[14,1792]{1,0:T(8,128)S(1)} %collective-permute-done.14, f32[14,1792]{1,0:T(8,128)S(1)} %collective-permute-done.13, f32[14,1792]{1,0:T(8,128)S(1)} %get-tuple-element.29, f32[14,1792]{1,0:T(8,128)S(1)} %collective-permute-done.12), kind=kLoop, calls=%fused_computation | loop fusion | flops 75264 | bytes 501760 | tf_op jit(solution)/shard_map/add | solution.py:293
  (7 shorter events, 0.2 us)
Async XLA Ops:
  0.0 6.0 %collective-permute-start.1 = (bf16[2,288,1792]{2,1,0:T(8,128)(2,1)}, bf16[2,288,1792]{2,1,0:T(8,128)(2,1)S(1)}, u32[]{:S(2)}, u32[]{:S(2)}) collective-permute-start(bf16[2,288,1792]{2,1,0:T(8,128)(2,1)} %x_ref.1), channel_id=1, source_target_pairs={{0,16},{1,17},{2,18},{3,19},{4,20},{5,21},{6,22},{7,23},{8,24},{9,... | collective-permute-start | bytes 6193160 | tf_op jit(solution)/shard_map/ppermute | solution.py:256
  0.0 1.6 %copy-start = (bf16[2,288,1792]{2,1,0:T(8,128)(2,1)S(1)}, bf16[2,288,1792]{2,1,0:T(8,128)(2,1)}, u32[]{:S(2)}) copy-start(bf16[2,288,1792]{2,1,0:T(8,128)(2,1)} %x_ref.1) | copy-start | bytes 6193156
  1.6 0.7 %copy-start.1 = (s32[1,18]{1,0:T(1,128)S(1)}, s32[1,18]{1,0:T(1,128)}, u32[]{:S(2)}) copy-start(s32[1,18]{1,0:T(1,128)} %screen.1) | copy-start | bytes 220
  4.2 1.8 %collective-permute-start.2 = (f32[8,128]{1,0:T(8,128)S(1)}, f32[8,128]{1,0:T(8,128)S(1)}, u32[]{:S(2)}, u32[]{:S(2)}) collective-permute-start(f32[8,128]{1,0:T(8,128)S(1)} %get-tuple-element.21.refs_0_), channel_id=1, source_target_pairs={{0,16},{1,17},{2,18},{3,19},{4,20},{5,21},{6,22},{7,23},{8,24},{9,... | collective-permute-start | bytes 12296 | tf_op jit(solution)/shard_map/ppermute | solution.py:261
  4.8 1.2 %collective-permute-start = (s32[1,18]{1,0:T(1,128)S(1)}, s32[1,18]{1,0:T(1,128)S(1)}, u32[]{:S(2)}, u32[]{:S(2)}) collective-permute-start(s32[1,18]{1,0:T(1,128)S(1)} %copy-done.1), channel_id=1, source_target_pairs={{0,16},{1,17},{2,18},{3,19},{4,20},{5,21},{6,22},{7,23},{8,24},{9,... | collective-permute-start | bytes 224 | tf_op jit(solution)/shard_map/ppermute | solution.py:257
  9.4 13.5 %collective-permute-start.5 = (f16[4,56,1792]{2,1,0:T(8,128)(2,1)S(1)}, f16[4,56,1792]{2,1,0:T(8,128)(2,1)S(1)}, u32[]{:S(2)}, u32[]{:S(2)}) collective-permute-start(f16[4,56,1792]{2,1,0:T(8,128)(2,1)S(1)} %convert_element_type.40), channel_id=1, source_target_pairs={{0,12},{1,13},{2,14},{3,15},{4,8},{5,9},{6,10},{7,11},{8,4},{9,5},... | collective-permute-start | bytes 2408456 | tf_op jit(solution)/shard_map/ppermute | solution.py:252
  15.3 20.9 %collective-permute-start.4 = (f16[4,56,1792]{2,1,0:T(8,128)(2,1)S(1)}, f16[4,56,1792]{2,1,0:T(8,128)(2,1)S(1)}, u32[]{:S(2)}, u32[]{:S(2)}) collective-permute-start(f16[4,56,1792]{2,1,0:T(8,128)(2,1)S(1)} %convert_element_type.38), channel_id=1, source_target_pairs={{0,32},{1,33},{2,34},{3,35},{4,36},{5,37},{6,38},{7,39},{8,40},{9,... | collective-permute-start | bytes 2408456 | tf_op jit(solution)/shard_map/ppermute | solution.py:252
  17.1 19.3 %collective-permute-start.3 = (f16[4,56,1792]{2,1,0:T(8,128)(2,1)S(1)}, f16[4,56,1792]{2,1,0:T(8,128)(2,1)S(1)}, u32[]{:S(2)}, u32[]{:S(2)}) collective-permute-start(f16[4,56,1792]{2,1,0:T(8,128)(2,1)S(1)} %convert_element_type.36), channel_id=1, source_target_pairs={{0,44},{1,45},{2,46},{3,47},{4,40},{5,41},{6,42},{7,43},{8,36},{9,... | collective-permute-start | bytes 2408456 | tf_op jit(solution)/shard_map/ppermute | solution.py:252
  17.4 19.1 %collective-permute-start.6 = (f32[8,128]{1,0:T(8,128)S(1)}, f32[8,128]{1,0:T(8,128)S(1)}, u32[]{:S(2)}, u32[]{:S(2)}) collective-permute-start(f32[8,128]{1,0:T(8,128)S(1)} %get-tuple-element.24.refs_0_.refs_3_), channel_id=1, source_target_pairs={{0,44},{1,45},{2,46},{3,47},{4,40},{5,41},{6,42},{7,43},{8,36},{9,... | collective-permute-start | bytes 12296 | tf_op jit(solution)/shard_map/ppermute | solution.py:252
  21.3 15.2 %collective-permute-start.7 = (f32[8,128]{1,0:T(8,128)S(1)}, f32[8,128]{1,0:T(8,128)S(1)}, u32[]{:S(2)}, u32[]{:S(2)}) collective-permute-start(f32[8,128]{1,0:T(8,128)S(1)} %get-tuple-element.24.refs_0_.refs_3_), channel_id=1, source_target_pairs={{0,32},{1,33},{2,34},{3,35},{4,36},{5,37},{6,38},{7,39},{8,40},{9,... | collective-permute-start | bytes 12296 | tf_op jit(solution)/shard_map/ppermute | solution.py:252
  22.9 13.6 %collective-permute-start.8 = (f32[8,128]{1,0:T(8,128)S(1)}, f32[8,128]{1,0:T(8,128)S(1)}, u32[]{:S(2)}, u32[]{:S(2)}) collective-permute-start(f32[8,128]{1,0:T(8,128)S(1)} %get-tuple-element.24.refs_0_.refs_3_), channel_id=1, source_target_pairs={{0,12},{1,13},{2,14},{3,15},{4,8},{5,9},{6,10},{7,11},{8,4},{9,5},... | collective-permute-start | bytes 12296 | tf_op jit(solution)/shard_map/ppermute | solution.py:252
  37.4 8.3 %collective-permute-start.9 = (f16[64,1792]{1,0:T(8,128)(2,1)S(1)}, f16[64,1792]{1,0:T(8,128)(2,1)S(1)}, u32[]{:S(2)}, u32[]{:S(2)}) collective-permute-start(f16[64,1792]{1,0:T(8,128)(2,1)S(1)} %convert_element_type.42), channel_id=1, source_target_pairs={{0,100},{1,101},{2,102},{3,103},{4,96},{5,97},{6,98},{7,99},{8,108... | collective-permute-start | bytes 688136 | tf_op jit(solution)/shard_map/ppermute | solution.py:252
  40.1 7.9 %collective-permute-start.10 = (f16[64,1792]{1,0:T(8,128)(2,1)S(1)}, f16[64,1792]{1,0:T(8,128)(2,1)S(1)}, u32[]{:S(2)}, u32[]{:S(2)}) collective-permute-start(f16[64,1792]{1,0:T(8,128)(2,1)S(1)} %convert_element_type.44), channel_id=1, source_target_pairs={{0,96},{1,97},{2,98},{3,99},{4,100},{5,101},{6,102},{7,103},{8,104... | collective-permute-start | bytes 688136 | tf_op jit(solution)/shard_map/ppermute | solution.py:252
  40.6 7.8 %collective-permute-start.11 = (f16[64,1792]{1,0:T(8,128)(2,1)S(1)}, f16[64,1792]{1,0:T(8,128)(2,1)S(1)}, u32[]{:S(2)}, u32[]{:S(2)}) collective-permute-start(f16[64,1792]{1,0:T(8,128)(2,1)S(1)} %convert_element_type.46), channel_id=1, source_target_pairs={{0,4},{1,5},{2,6},{3,7},{4,0},{5,1},{6,2},{7,3},{8,12},{9,13},{10,... | collective-permute-start | bytes 688136 | tf_op jit(solution)/shard_map/ppermute | solution.py:252
  48.7 7.9 %collective-permute-start.12 = (f32[14,1792]{1,0:T(8,128)S(1)}, f32[14,1792]{1,0:T(8,128)S(1)}, u32[]{:S(2)}, u32[]{:S(2)}) collective-permute-start(f32[14,1792]{1,0:T(8,128)S(1)} %get-tuple-element.30), channel_id=1, source_target_pairs={{0,3},{1,2},{2,1},{3,0},{4,7},{5,6},{6,5},{7,4},{8,11},{9,10},{10,... | collective-permute-start | bytes 301064 | tf_op jit(solution)/shard_map/ppermute | solution.py:252
  52.9 4.8 %collective-permute-start.13 = (f32[14,1792]{1,0:T(8,128)S(1)}, f32[14,1792]{1,0:T(8,128)S(1)}, u32[]{:S(2)}, u32[]{:S(2)}) collective-permute-start(f32[14,1792]{1,0:T(8,128)S(1)} %get-tuple-element.31), channel_id=1, source_target_pairs={{0,1},{1,0},{2,3},{3,2},{4,5},{5,4},{6,7},{7,6},{8,9},{9,8},{10,11... | collective-permute-start | bytes 301064 | tf_op jit(solution)/shard_map/ppermute | solution.py:252
  52.9 6.3 %collective-permute-start.14 = (f32[14,1792]{1,0:T(8,128)S(1)}, f32[14,1792]{1,0:T(8,128)S(1)}, u32[]{:S(2)}, u32[]{:S(2)}) collective-permute-start(f32[14,1792]{1,0:T(8,128)S(1)} %get-tuple-element.32), channel_id=1, source_target_pairs={{0,2},{1,3},{2,0},{3,1},{4,6},{5,7},{6,4},{7,5},{8,10},{9,11},{10,... | collective-permute-start | bytes 301064 | tf_op jit(solution)/shard_map/ppermute | solution.py:252

commit v3 on v2

--- a/solution.py
+++ b/solution.py
@@ -11,7 +11,6 @@
 AXES = ("grp", "mem")
 SIDE = 4
 CORES = 2
-STRIPE = 256
 SENT = jnp.float16
 ROOM = 16384.0
 SMALLEST = 2.0**-60
@@ -24,7 +23,6 @@
 
 VMEM = pl.BlockSpec(memory_space=pltpu.VMEM)
 SMEM = pl.BlockSpec(memory_space=pltpu.SMEM)
-HBM = pl.BlockSpec(memory_space=pltpu.HBM)
 
 
 def near(v):
@@ -76,76 +74,64 @@
     return terms * most * most
 
 
-def front_kernel(track, screen, x_ref, *refs):
-    scratch, sems = refs[-2:]
-    if track:
-        x_out, x_t, *tail = refs[:-2]
-    else:
-        x_out, x_t = refs[2:4]
-        tail = (*refs[:2], *refs[4:-2])
+def padded(size, tile):
+    return -(-size // tile) * tile
+
+
+def front_kernel(slots, aux, screen, x_ref, *refs):
+    outs, scratch = refs[:-1], refs[-1]
     y, core, _, _ = here()
-    aux, occ, basis = x_ref.shape
-    depth = aux * occ
+    depth, basis = x_ref.shape
     blocks = screen.shape[1]
     part = basis // (SIDE * CORES)
     chunk = part // SIDE
-    copies = []
-    for j in range(basis // STRIPE):
-        columns = slice(j * STRIPE, (j + 1) * STRIPE)
-        pair = [
-            pltpu.make_async_copy(x_ref.at[a, :, columns], x_out.at[pl.ds(a * occ, occ), columns], sems.at[j, a])
-            for a in range(aux)
-        ]
-        for copy in pair:
-            copy.start()
-        copies.append(pair)
+    span = scratch.shape[1]
+    occ = depth // aux
     lane = lax.broadcasted_iota(jnp.int32, (16, depth), 1)
     block_of = lax.div(lax.rem(lane, occ), occ // blocks)
     flags = jnp.zeros((16, depth), F32)
     for b in range(blocks):
         flags = jnp.where(block_of == b, (screen[0, b] == 1).astype(F32), flags)
-    flags = flags.astype(x_out.dtype)
-    most = jnp.zeros((16, depth), x_out.dtype)
-    for j, pair in enumerate(copies):
-        for copy in pair:
-            copy.wait()
-        columns = slice(j * STRIPE, (j + 1) * STRIPE)
-        turned = x_out[:, columns].T
-        scratch[columns, :] = turned
-        if track:
-            sizes = jnp.abs(turned)
-            for r in range(0, STRIPE, 16):
-                most = jnp.maximum(most, sizes[r : r + 16])
-    if track:
-        most = (most * flags).astype(F32)
+    flags = flags.astype(x_ref.dtype)
+    if len(outs) > len(slots):
+        width = occ // blocks
+        most = jnp.zeros((width, basis), F32)
+        for r in range(0, depth, width):
+            kept = (screen[0, (r % occ) // width] == 1).astype(F32)
+            most = jnp.maximum(most, jnp.abs(x_ref[r : r + width, :]).astype(F32) * kept)
         top = jnp.max(jnp.max(most, axis=1, keepdims=True), axis=0, keepdims=True)
-        tail[0][...] = jnp.broadcast_to(top, tail[0].shape)
-    else:
-        top = jnp.maximum(jnp.maximum(tail[0][...], tail[1][...]), SMALLEST)
-        tail[2][...] = top
-    for s, at in enumerate(order_here(y, 0, core)):
-        first = pl.multiple_of((at * CORES + core) * part, 16)
-        block = scratch[pl.ds(first, part), :] * flags[0:1]
-        for v in range(SIDE):
-            x_t[s, v] = block[v * chunk : (v + 1) * chunk]
-
-
-def front(screen, x, peaks):
-    aux, occ, basis = x.shape
-    depth = aux * occ
-    shapes = [
-        jax.ShapeDtypeStruct((depth, basis), x.dtype),
-        jax.ShapeDtypeStruct((SIDE, SIDE, basis // (SIDE * CORES * SIDE), depth), x.dtype),
-        jax.ShapeDtypeStruct((8, 128), F32),
-    ]
-    return pl.pallas_call(
-        functools.partial(front_kernel, not peaks),
+        outs[-1][...] = jnp.broadcast_to(top, outs[-1].shape)
+    places = order_here(y, 0, core)
+    for n, pair in enumerate(slots):
+        for s, slot in enumerate(pair):
+            start = (places[slot] * CORES + core) * part
+            tile = jnp.minimum(lax.div(start, 128), (basis - span) // 128)
+            held = scratch.at[(2 * n + s) % 2]
+            held[...] = x_ref[:, pl.ds(pl.multiple_of(tile * 128, 128), span)].T
+            block = held[pl.ds(pl.multiple_of(start - tile * 128, 16), part), :] * flags[0:1]
+            for v in range(SIDE):
+                outs[n][s, v] = block[v * chunk : (v + 1) * chunk]
+
+
+def front(screen, x, aux, slots, peak):
+    depth, basis = x.shape
+    part = basis // (SIDE * CORES)
+    span = padded(part + 127, 128)
+    shapes = [jax.ShapeDtypeStruct((2, SIDE, part // SIDE, depth), x.dtype)] * len(slots)
+    if peak:
+        shapes.append(jax.ShapeDtypeStruct((8, 128), F32))
+    return pl.pallas_call(
+        functools.partial(front_kernel, slots, aux),
         out_shape=shapes,
-        in_specs=[SMEM, HBM] + [VMEM] * len(peaks),
+        in_specs=[SMEM, VMEM],
         out_specs=[VMEM] * len(shapes),
-        scratch_shapes=[pltpu.VMEM((basis, depth), x.dtype), pltpu.SemaphoreType.DMA((basis // STRIPE, aux))],
-        compiler_params=limit(16),
-    )(screen, x, *peaks)
+        scratch_shapes=[pltpu.VMEM((2, span, depth), x.dtype)],
+        compiler_params=limit(12),
+    )(screen, x)
+
+
+def bound(most, terms):
+    return terms * most * most
 
 
 def product_kernel(slots, x_own, t_own, x_other, t_other, *refs):
@@ -160,7 +146,8 @@
     whole = jnp.dot(left(t_own), x_own[...], preferred_element_type=F32)
     whole = whole + jnp.dot(left(t_other), x_other[...], preferred_element_type=F32)
     if len(refs) > 1:
-        whole = whole * (ROOM / bound(refs[0][0:1, 0:1], CORES * x_own.shape[0]))
+        most = jnp.maximum(jnp.maximum(refs[0][0:1, 0:1], refs[1][0:1, 0:1]), SMALLEST)
+        whole = whole * (ROOM / bound(most, CORES * x_own.shape[0]))
     for at in range(len(slots)):
         out[at] = whole[at * chunk : (at + 1) * chunk]
 
@@ -253,13 +240,19 @@
 
 
 def on_device(factors, screen):
-    other = lax.ppermute(factors, AXES, CORE_SWAP)
+    aux, occ, basis = factors.shape
+    own = factors.reshape(aux * occ, basis)
+    other = lax.ppermute(own, AXES, CORE_SWAP)
     other_screen = lax.ppermute(screen, AXES, CORE_SWAP)
-    depth = CORES * factors.shape[0] * factors.shape[1]
-
-    x_own, t_own, peak = front(screen, factors, ())
-    x_other, t_other, peak = front(other_screen, other, (peak, lax.ppermute(peak, AXES, CORE_SWAP)))
-    parts = (x_own, t_own, x_other, t_other)
+    depth = CORES * aux * occ
+
+    own_high, own_low, peak = front(screen, own, aux, ((2, 3), (0, 1)), True)
+    peak_other = lax.ppermute(peak, AXES, CORE_SWAP)
+    (other_high,) = front(other_screen, other, aux, ((2, 3),), False)
+    (other_low,) = front(other_screen, other, aux, ((0, 1),), False)
+    high = (own, own_high, other, other_high)
+    low = (own, own_low, other, other_low)
+    peaks = (peak, peak_other)
 
     def narrow(v):
         return v.astype(SENT)
@@ -268,13 +261,14 @@
         return v.astype(F32)
 
     d_moves, y_moves, x_moves = ((0, 0), (2, 0)), ((0, 0),), ((2, 0),)
-    d_out = product((*parts, peak), ((2, 2), (2, 3), (3, 2), (3, 3)))
+    d_out = product((*high, *peaks), ((0, 2), (0, 3), (1, 2), (1, 3)))
     d_in = go(narrow(d_out), *d_moves)
-    y_out = product((*parts, peak), ((2, 0), (2, 1), (3, 0), (3, 1)))
+    y_out = product((*high, *peaks), ((0, 0), (0, 1), (1, 0), (1, 1)))
     y_in = go(narrow(y_out), *y_moves)
-    x_out = product((*parts, peak), ((0, 2), (0, 3), (1, 2), (1, 3)))
+    x_out = product((*low, *peaks), ((0, 2), (0, 3), (1, 2), (1, 3)))
     x_in = go(narrow(x_out), *x_moves)
-    kept = product(parts, ((0, 0), (0, 1), (1, 0), (1, 1)))
+    kept = product(low, ((0, 0), (0, 1), (1, 0), (1, 1)))
+    peak = jnp.maximum(jnp.maximum(peak, peak_other), SMALLEST)
     d_most = go(peak, *d_moves)
     y_most = go(peak, *y_moves)
     x_most = go(peak, *x_moves)

time: 60 us -> 57.9 us (0.965)
  the two profiles are of different devices: /device:TPU:0 before, /device:TPU:36 now
where the time goes in v3:
time: 57.9 us; the launch traced here: 57.7 us
  waiting for transfers between devices  26.9 us (46%)
  starting transfers between devices  16.8 us (29%)
  Pallas kernels  10.2 us (18%)
  local copies, waits for them, and re-layouts  2.24 us (4%)
  other arithmetic  1.41 us (2%)
    ppermute x12, waiting for transfers between devices, go(): return lax.ppermute(v, AXES, partners(*moves))  25.8 us
    ppermute x12, starting transfers between devices, go(): return lax.ppermute(v, AXES, partners(*moves))  16.1 us
    pallas_call x4, Pallas kernels, product(): pl.pallas_call(functools.partial(product_kernel, slots), out_shape=jax.Sh...  5.65 us
    pallas_call x3, Pallas kernels, front(): pl.pallas_call(functools.partial(front_kernel, slots, aux), out_shape=sha...  3.44 us
    unnamed x6, local copies, waits for them, and re-layouts  2.24 us
  transfers between devices with their start and end apart: 15, of which 10 were waited for; matrix products, arithmetic and copies ran while one was open for 1% of the time, Pallas kernels for 13%

profile of v3, /device:TPU:36, one launch (start us, length us, event | category | flops | bytes accessed | tf_op | source)
XLA Modules:
  0.0 57.7 jit_solution(11411118805477129099)
XLA Ops:
  0.0 0.0 collective-permute-start
  0.0 1.6 %copy-done = bf16[2,288,1792]{2,1,0:T(8,128)(2,1)S(1)} copy-done((bf16[2,288,1792]{2,1,0:T(8,128)(2,1)S(1)}, bf16[2,288,1792]{2,1,0:T(8,128)(2,1)}, u32[]{:S(2)}) %copy-start) | copy-done | bytes 2064408
  1.6 0.7 %copy-done.2 = s32[1,18]{1,0:T(1,128)S(1)} copy-done((s32[1,18]{1,0:T(1,128)S(1)}, s32[1,18]{1,0:T(1,128)}, u32[]{:S(2)}) %copy-start.2) | copy-done | bytes 96
  2.2 1.6 %shard_map.28 = (bf16[2,4,56,576]{3,2,1,0:T(8,128)(2,1)S(1)}, bf16[2,4,56,576]{3,2,1,0:T(8,128)(2,1)S(1)}, f32[8,128]{1,0:T(8,128)S(1)}) custom-call(s32[1,18]{1,0:T(1,128)S(1)} %copy-done.2, bf16[576,1792]{1,0:T(8,128)(2,1)S(1)} %bitcast.2), custom_call_target="tpu_custom_call" | custom-call | tf_op jit(solution)/shard_map/pallas_call | solution.py:123
  3.9 0.0 copy-start.1
  3.9 0.6 %collective-permute-start.2 = (f32[8,128]{1,0:T(8,128)S(1)}, f32[8,128]{1,0:T(8,128)S(1)}, u32[]{:S(2)}, u32[]{:S(2)}) collective-permute-start(f32[8,128]{1,0:T(8,128)S(1)} %get-tuple-element.18.refs_0_), channel_id=1, source_target_pairs={{0,16},{1,17},{2,18},{3,19},{4,20},{5,21},{6,22},{7,23},{8,24},{9,... | collective-permute-start | bytes 12296 | tf_op jit(solution)/shard_map/ppermute | solution.py:250
  4.5 0.1 collective-permute-start.1
  4.6 1.1 %collective-permute-done.1.screen = s32[1,18]{1,0:T(1,128)S(1)} collective-permute-done((s32[1,18]{1,0:T(1,128)S(1)}, s32[1,18]{1,0:T(1,128)S(1)}, u32[]{:S(2)}, u32[]{:S(2)}) %collective-permute-start.1) | collective-permute-done | bytes 104 | tf_op jit(solution)/shard_map/ppermute | solution.py:246
  5.6 0.0 collective-permute-done.x_ref.x_other
  5.7 0.9 %shard_map.31.t_other = bf16[2,4,56,576]{3,2,1,0:T(8,128)(2,1)S(1)} custom-call(s32[1,18]{1,0:T(1,128)S(1)} %collective-permute-done.1.screen, bf16[576,1792]{1,0:T(8,128)(2,1)S(1)} %collective-permute-done.x_ref.x_other), custom_call_target="tpu_custom_call" | custom-call | tf_op jit(solution)/shard_map/pallas_call | solution.py:123
  6.6 0.0 collective-permute-done.2.refs_1_
  6.6 1.4 %shard_map.33 = f32[4,56,1792]{2,1,0:T(8,128)S(1)} custom-call(bf16[576,1792]{1,0:T(8,128)(2,1)S(1)} %bitcast.3, bf16[2,4,56,576]{3,2,1,0:T(8,128)(2,1)S(1)} %get-tuple-element.17.t_own, bf16[576,1792]{1,0:T(8,128)(2,1)S(1)} %collective-permute-done.x_ref.x_other, bf16[2,4,56,576]{3,2,1,0:T(8,128)(2,1)S(1)} %shard_map.31.t_other, ...), custom_call_target="tpu_custom_call" | custom-call | flops 924844032 | bytes 1605632 | tf_op jit(solution)/shard_map/pallas_call | solution.py:159
  8.0 0.1 convert_element_type.38
  8.1 1.6 %collective-permute-start.4 = (f16[4,56,1792]{2,1,0:T(8,128)(2,1)S(1)}, f16[4,56,1792]{2,1,0:T(8,128)(2,1)S(1)}, u32[]{:S(2)}, u32[]{:S(2)}) collective-permute-start(f16[4,56,1792]{2,1,0:T(8,128)(2,1)S(1)} %convert_element_type.38), channel_id=1, source_target_pairs={{0,32},{1,33},{2,34},{3,35},{4,36},{5,37},{6,38},{7,39},{8,40},{9,... | collective-permute-start | bytes 2408456 | tf_op jit(solution)/shard_map/ppermute | solution.py:239
  9.7 0.9 %shard_map.29.t_other = bf16[2,4,56,576]{3,2,1,0:T(8,128)(2,1)S(1)} custom-call(s32[1,18]{1,0:T(1,128)S(1)} %collective-permute-done.1.screen, bf16[576,1792]{1,0:T(8,128)(2,1)S(1)} %collective-permute-done.x_ref.x_other), custom_call_target="tpu_custom_call" | custom-call | tf_op jit(solution)/shard_map/pallas_call | solution.py:123
  10.6 1.4 %shard_map.34 = f32[4,56,1792]{2,1,0:T(8,128)S(1)} custom-call(bf16[576,1792]{1,0:T(8,128)(2,1)S(1)} %bitcast.4, bf16[2,4,56,576]{3,2,1,0:T(8,128)(2,1)S(1)} %get-tuple-element.16.t_own, bf16[576,1792]{1,0:T(8,128)(2,1)S(1)} %collective-permute-done.x_ref.x_other, bf16[2,4,56,576]{3,2,1,0:T(8,128)(2,1)S(1)} %shard_map.29.t_other, ...), custom_call_target="tpu_custom_call" | custom-call | flops 924844032 | bytes 1605632 | tf_op jit(solution)/shard_map/pallas_call | solution.py:159
  12.1 0.1 convert_element_type.40
  12.2 0.6 %collective-permute-start.5 = (f16[4,56,1792]{2,1,0:T(8,128)(2,1)S(1)}, f16[4,56,1792]{2,1,0:T(8,128)(2,1)S(1)}, u32[]{:S(2)}, u32[]{:S(2)}) collective-permute-start(f16[4,56,1792]{2,1,0:T(8,128)(2,1)S(1)} %convert_element_type.40), channel_id=1, source_target_pairs={{0,12},{1,13},{2,14},{3,15},{4,8},{5,9},{6,10},{7,11},{8,4},{9,5},... | collective-permute-start | bytes 2408456 | tf_op jit(solution)/shard_map/ppermute | solution.py:239
  12.8 1.4 %shard_map.32 = f32[4,56,1792]{2,1,0:T(8,128)S(1)} custom-call(bf16[576,1792]{1,0:T(8,128)(2,1)S(1)} %bitcast.5, bf16[2,4,56,576]{3,2,1,0:T(8,128)(2,1)S(1)} %get-tuple-element.17.t_own, bf16[576,1792]{1,0:T(8,128)(2,1)S(1)} %collective-permute-done.x_ref.x_other, bf16[2,4,56,576]{3,2,1,0:T(8,128)(2,1)S(1)} %shard_map.31.t_other, ...), custom_call_target="tpu_custom_call" | custom-call | flops 924844032 | bytes 1605632 | tf_op jit(solution)/shard_map/pallas_call | solution.py:159
  14.2 0.1 convert_element_type.36
  14.3 1.5 %collective-permute-start.3 = (f16[4,56,1792]{2,1,0:T(8,128)(2,1)S(1)}, f16[4,56,1792]{2,1,0:T(8,128)(2,1)S(1)}, u32[]{:S(2)}, u32[]{:S(2)}) collective-permute-start(f16[4,56,1792]{2,1,0:T(8,128)(2,1)S(1)} %convert_element_type.36), channel_id=1, source_target_pairs={{0,44},{1,45},{2,46},{3,47},{4,40},{5,41},{6,42},{7,43},{8,36},{9,... | collective-permute-start | bytes 2408456 | tf_op jit(solution)/shard_map/ppermute | solution.py:239
  15.8 1.5 %collective-permute-start.6 = (f32[8,128]{1,0:T(8,128)S(1)}, f32[8,128]{1,0:T(8,128)S(1)}, u32[]{:S(2)}, u32[]{:S(2)}) collective-permute-start(f32[8,128]{1,0:T(8,128)S(1)} %maximum_maximum_fusion.refs_3_), channel_id=1, source_target_pairs={{0,44},{1,45},{2,46},{3,47},{4,40},{5,41},{6,42},{7,43},{8,36},{9,... | collective-permute-start | bytes 12296 | tf_op jit(solution)/shard_map/ppermute | solution.py:239
  17.3 0.5 collective-permute-start.7
  17.8 2.6 %collective-permute-done.4 = f16[4,56,1792]{2,1,0:T(8,128)(2,1)S(1)} collective-permute-done((f16[4,56,1792]{2,1,0:T(8,128)(2,1)S(1)}, f16[4,56,1792]{2,1,0:T(8,128)(2,1)S(1)}, u32[]{:S(2)}, u32[]{:S(2)}) %collective-permute-start.4) | collective-permute-done | bytes 802848 | tf_op jit(solution)/shard_map/ppermute | solution.py:239
  20.3 0.5 collective-permute-start.8
  20.9 1.4 %shard_map.30.kept = f32[4,56,1792]{2,1,0:T(8,128)S(1)} custom-call(bf16[576,1792]{1,0:T(8,128)(2,1)S(1)} %bitcast.6, bf16[2,4,56,576]{3,2,1,0:T(8,128)(2,1)S(1)} %get-tuple-element.16.t_own, bf16[576,1792]{1,0:T(8,128)(2,1)S(1)} %collective-permute-done.x_ref.x_other, bf16[2,4,56,576]{3,2,1,0:T(8,128)(2,1)S(1)} %shard_map.29.t_other), custom_call_target="tpu_custom_call" | custom-call | flops 924844032 | bytes 1605632 | tf_op jit(solution)/shard_map/pallas_call | solution.py:159
  22.3 0.1 convert_element_type.39.refs_1_
  22.4 2.0 %collective-permute-done.5 = f16[4,56,1792]{2,1,0:T(8,128)(2,1)S(1)} collective-permute-done((f16[4,56,1792]{2,1,0:T(8,128)(2,1)S(1)}, f16[4,56,1792]{2,1,0:T(8,128)(2,1)S(1)}, u32[]{:S(2)}, u32[]{:S(2)}) %collective-permute-start.5) | collective-permute-done | bytes 802848 | tf_op jit(solution)/shard_map/ppermute | solution.py:239
  24.4 0.1 convert_element_type.41.refs_2_
  24.5 8.4 %collective-permute-done.3 = f16[4,56,1792]{2,1,0:T(8,128)(2,1)S(1)} collective-permute-done((f16[4,56,1792]{2,1,0:T(8,128)(2,1)S(1)}, f16[4,56,1792]{2,1,0:T(8,128)(2,1)S(1)}, u32[]{:S(2)}, u32[]{:S(2)}) %collective-permute-start.3) | collective-permute-done | bytes 802848 | tf_op jit(solution)/shard_map/ppermute | solution.py:239
  32.9 0.1 convert_element_type.37.refs_0_
  33.0 0.0 collective-permute-done.6.refs_4_
  33.0 0.0 collective-permute-done.7.refs_5_
  33.0 0.1 collective-permute-done.8.refs_6_
  33.1 0.8 %shard_map.35 = (f32[56,1792]{1,0:T(8,128)S(1)}, f32[64,1792]{1,0:T(8,128)S(1)}, f32[64,1792]{1,0:T(8,128)S(1)}, f32[64,1792]{1,0:T(8,128)S(1)}) custom-call(f32[4,56,1792]{2,1,0:T(8,128)S(1)} %shard_map.30.kept, f32[4,56,1792]{2,1,0:T(8,128)S(1)} %convert_element_type.37.refs_0_, f32[4,56,1792]{2,1,0:T(8,128)S(1)} %convert_element_type.39.refs_1_, ...), custom_call_target="tpu_custom_call" | custom-call | tf_op jit(solution)/shard_map/pallas_call | solution.py:200
  33.9 4.9 %collective-permute-start.9 = (f16[64,1792]{1,0:T(8,128)(2,1)S(1)}, f16[64,1792]{1,0:T(8,128)(2,1)S(1)}, u32[]{:S(2)}, u32[]{:S(2)}) collective-permute-start(f16[64,1792]{1,0:T(8,128)(2,1)S(1)} %convert_element_type.42), channel_id=1, source_target_pairs={{0,100},{1,101},{2,102},{3,103},{4,96},{5,97},{6,98},{7,99},{8,108... | collective-permute-start | bytes 688136 | tf_op jit(solution)/shard_map/ppermute | solution.py:239
  38.8 0.4 collective-permute-start.10
  39.2 0.4 collective-permute-start.11
  39.6 3.2 %collective-permute-done.9 = f16[64,1792]{1,0:T(8,128)(2,1)S(1)} collective-permute-done((f16[64,1792]{1,0:T(8,128)(2,1)S(1)}, f16[64,1792]{1,0:T(8,128)(2,1)S(1)}, u32[]{:S(2)}, u32[]{:S(2)}) %collective-permute-start.9) | collective-permute-done | bytes 229408 | tf_op jit(solution)/shard_map/ppermute | solution.py:239
  42.9 3.3 %collective-permute-done.10 = f16[64,1792]{1,0:T(8,128)(2,1)S(1)} collective-permute-done((f16[64,1792]{1,0:T(8,128)(2,1)S(1)}, f16[64,1792]{1,0:T(8,128)(2,1)S(1)}, u32[]{:S(2)}, u32[]{:S(2)}) %collective-permute-start.10) | collective-permute-done | bytes 229408 | tf_op jit(solution)/shard_map/ppermute | solution.py:239
  46.2 0.0 collective-permute-done.11
  46.2 0.3 shard_map.36
  46.5 2.0 %collective-permute-start.12 = (f32[14,1792]{1,0:T(8,128)S(1)}, f32[14,1792]{1,0:T(8,128)S(1)}, u32[]{:S(2)}, u32[]{:S(2)}) collective-permute-start(f32[14,1792]{1,0:T(8,128)S(1)} %get-tuple-element.24), channel_id=1, source_target_pairs={{0,3},{1,2},{2,1},{3,0},{4,7},{5,6},{6,5},{7,4},{8,11},{9,10},{10,... | collective-permute-start | bytes 301064 | tf_op jit(solution)/shard_map/ppermute | solution.py:239
  48.5 2.2 %collective-permute-start.13 = (f32[14,1792]{1,0:T(8,128)S(1)}, f32[14,1792]{1,0:T(8,128)S(1)}, u32[]{:S(2)}, u32[]{:S(2)}) collective-permute-start(f32[14,1792]{1,0:T(8,128)S(1)} %get-tuple-element.25), channel_id=1, source_target_pairs={{0,1},{1,0},{2,3},{3,2},{4,5},{5,4},{6,7},{7,6},{8,9},{9,8},{10,11... | collective-permute-start | bytes 301064 | tf_op jit(solution)/shard_map/ppermute | solution.py:239
  50.8 1.3 %collective-permute-done.12 = f32[14,1792]{1,0:T(8,128)S(1)} collective-permute-done((f32[14,1792]{1,0:T(8,128)S(1)}, f32[14,1792]{1,0:T(8,128)S(1)}, u32[]{:S(2)}, u32[]{:S(2)}) %collective-permute-start.12) | collective-permute-done | bytes 100384 | tf_op jit(solution)/shard_map/ppermute | solution.py:239
  52.1 1.5 %collective-permute-done.13 = f32[14,1792]{1,0:T(8,128)S(1)} collective-permute-done((f32[14,1792]{1,0:T(8,128)S(1)}, f32[14,1792]{1,0:T(8,128)S(1)}, u32[]{:S(2)}, u32[]{:S(2)}) %collective-permute-start.13) | collective-permute-done | bytes 100384 | tf_op jit(solution)/shard_map/ppermute | solution.py:239
  53.5 3.5 %collective-permute-done.14 = f32[14,1792]{1,0:T(8,128)S(1)} collective-permute-done((f32[14,1792]{1,0:T(8,128)S(1)}, f32[14,1792]{1,0:T(8,128)S(1)}, u32[]{:S(2)}, u32[]{:S(2)}) %collective-permute-start.14) | collective-permute-done | bytes 100384 | tf_op jit(solution)/shard_map/ppermute | solution.py:239
  57.1 0.7 %add_add_fusion = f32[14,1792]{1,0:T(8,128)} fusion(f32[14,1792]{1,0:T(8,128)S(1)} %collective-permute-done.14, f32[14,1792]{1,0:T(8,128)S(1)} %collective-permute-done.13, f32[14,1792]{1,0:T(8,128)S(1)} %get-tuple-element.23, f32[14,1792]{1,0:T(8,128)S(1)} %collective-permute-done.12), kind=kLoop, calls=%fused_computation | loop fusion | flops 75264 | bytes 501760 | tf_op jit(solution)/shard_map/add | solution.py:287
  (11 shorter events, 0.2 us)
Async XLA Ops:
  0.0 5.7 %collective-permute-start = (bf16[576,1792]{1,0:T(8,128)(2,1)}, bf16[576,1792]{1,0:T(8,128)(2,1)S(1)}, u32[]{:S(2)}, u32[]{:S(2)}) collective-permute-start(bf16[576,1792]{1,0:T(8,128)(2,1)} %bitcast.1), channel_id=1, source_target_pairs={{0,16},{1,17},{2,18},{3,19},{4,20},{5,21},{6,22},{7,23},{8,24},{9,... | collective-permute-start | bytes 6193160 | tf_op jit(solution)/shard_map/ppermute | solution.py:245
  0.0 1.6 %copy-start = (bf16[2,288,1792]{2,1,0:T(8,128)(2,1)S(1)}, bf16[2,288,1792]{2,1,0:T(8,128)(2,1)}, u32[]{:S(2)}) copy-start(bf16[2,288,1792]{2,1,0:T(8,128)(2,1)} %param.2) | copy-start | bytes 6193156
  1.6 0.7 %copy-start.2 = (s32[1,18]{1,0:T(1,128)S(1)}, s32[1,18]{1,0:T(1,128)}, u32[]{:S(2)}) copy-start(s32[1,18]{1,0:T(1,128)} %screen.1) | copy-start | bytes 220
  3.9 2.7 %copy-start.1 = (bf16[2,288,1792]{2,1,0:T(8,128)(2,1)S(1)}, bf16[2,288,1792]{2,1,0:T(8,128)(2,1)}, u32[]{:S(2)}) copy-start(bf16[2,288,1792]{2,1,0:T(8,128)(2,1)} %param.2) | copy-start | bytes 6193156
  3.9 2.7 %collective-permute-start.2 = (f32[8,128]{1,0:T(8,128)S(1)}, f32[8,128]{1,0:T(8,128)S(1)}, u32[]{:S(2)}, u32[]{:S(2)}) collective-permute-start(f32[8,128]{1,0:T(8,128)S(1)} %get-tuple-element.18.refs_0_), channel_id=1, source_target_pairs={{0,16},{1,17},{2,18},{3,19},{4,20},{5,21},{6,22},{7,23},{8,24},{9,... | collective-permute-start | bytes 12296 | tf_op jit(solution)/shard_map/ppermute | solution.py:250
  4.5 1.2 %collective-permute-start.1 = (s32[1,18]{1,0:T(1,128)S(1)}, s32[1,18]{1,0:T(1,128)S(1)}, u32[]{:S(2)}, u32[]{:S(2)}) collective-permute-start(s32[1,18]{1,0:T(1,128)S(1)} %copy-done.2), channel_id=1, source_target_pairs={{0,16},{1,17},{2,18},{3,19},{4,20},{5,21},{6,22},{7,23},{8,24},{9,... | collective-permute-start | bytes 224 | tf_op jit(solution)/shard_map/ppermute | solution.py:246
  8.1 12.2 %collective-permute-start.4 = (f16[4,56,1792]{2,1,0:T(8,128)(2,1)S(1)}, f16[4,56,1792]{2,1,0:T(8,128)(2,1)S(1)}, u32[]{:S(2)}, u32[]{:S(2)}) collective-permute-start(f16[4,56,1792]{2,1,0:T(8,128)(2,1)S(1)} %convert_element_type.38), channel_id=1, source_target_pairs={{0,32},{1,33},{2,34},{3,35},{4,36},{5,37},{6,38},{7,39},{8,40},{9,... | collective-permute-start | bytes 2408456 | tf_op jit(solution)/shard_map/ppermute | solution.py:239
  12.2 12.2 %collective-permute-start.5 = (f16[4,56,1792]{2,1,0:T(8,128)(2,1)S(1)}, f16[4,56,1792]{2,1,0:T(8,128)(2,1)S(1)}, u32[]{:S(2)}, u32[]{:S(2)}) collective-permute-start(f16[4,56,1792]{2,1,0:T(8,128)(2,1)S(1)} %convert_element_type.40), channel_id=1, source_target_pairs={{0,12},{1,13},{2,14},{3,15},{4,8},{5,9},{6,10},{7,11},{8,4},{9,5},... | collective-permute-start | bytes 2408456 | tf_op jit(solution)/shard_map/ppermute | solution.py:239
  14.3 18.6 %collective-permute-start.3 = (f16[4,56,1792]{2,1,0:T(8,128)(2,1)S(1)}, f16[4,56,1792]{2,1,0:T(8,128)(2,1)S(1)}, u32[]{:S(2)}, u32[]{:S(2)}) collective-permute-start(f16[4,56,1792]{2,1,0:T(8,128)(2,1)S(1)} %convert_element_type.36), channel_id=1, source_target_pairs={{0,44},{1,45},{2,46},{3,47},{4,40},{5,41},{6,42},{7,43},{8,36},{9,... | collective-permute-start | bytes 2408456 | tf_op jit(solution)/shard_map/ppermute | solution.py:239
  15.8 17.3 %collective-permute-start.6 = (f32[8,128]{1,0:T(8,128)S(1)}, f32[8,128]{1,0:T(8,128)S(1)}, u32[]{:S(2)}, u32[]{:S(2)}) collective-permute-start(f32[8,128]{1,0:T(8,128)S(1)} %maximum_maximum_fusion.refs_3_), channel_id=1, source_target_pairs={{0,44},{1,45},{2,46},{3,47},{4,40},{5,41},{6,42},{7,43},{8,36},{9,... | collective-permute-start | bytes 12296 | tf_op jit(solution)/shard_map/ppermute | solution.py:239
  17.3 15.7 %collective-permute-start.7 = (f32[8,128]{1,0:T(8,128)S(1)}, f32[8,128]{1,0:T(8,128)S(1)}, u32[]{:S(2)}, u32[]{:S(2)}) collective-permute-start(f32[8,128]{1,0:T(8,128)S(1)} %maximum_maximum_fusion.refs_3_), channel_id=1, source_target_pairs={{0,32},{1,33},{2,34},{3,35},{4,36},{5,37},{6,38},{7,39},{8,40},{9,... | collective-permute-start | bytes 12296 | tf_op jit(solution)/shard_map/ppermute | solution.py:239
  20.3 12.7 %collective-permute-start.8 = (f32[8,128]{1,0:T(8,128)S(1)}, f32[8,128]{1,0:T(8,128)S(1)}, u32[]{:S(2)}, u32[]{:S(2)}) collective-permute-start(f32[8,128]{1,0:T(8,128)S(1)} %maximum_maximum_fusion.refs_3_), channel_id=1, source_target_pairs={{0,12},{1,13},{2,14},{3,15},{4,8},{5,9},{6,10},{7,11},{8,4},{9,5},... | collective-permute-start | bytes 12296 | tf_op jit(solution)/shard_map/ppermute | solution.py:239
  33.9 8.9 %collective-permute-start.9 = (f16[64,1792]{1,0:T(8,128)(2,1)S(1)}, f16[64,1792]{1,0:T(8,128)(2,1)S(1)}, u32[]{:S(2)}, u32[]{:S(2)}) collective-permute-start(f16[64,1792]{1,0:T(8,128)(2,1)S(1)} %convert_element_type.42), channel_id=1, source_target_pairs={{0,100},{1,101},{2,102},{3,103},{4,96},{5,97},{6,98},{7,99},{8,108... | collective-permute-start | bytes 688136 | tf_op jit(solution)/shard_map/ppermute | solution.py:239
  38.8 7.3 %collective-permute-start.10 = (f16[64,1792]{1,0:T(8,128)(2,1)S(1)}, f16[64,1792]{1,0:T(8,128)(2,1)S(1)}, u32[]{:S(2)}, u32[]{:S(2)}) collective-permute-start(f16[64,1792]{1,0:T(8,128)(2,1)S(1)} %convert_element_type.44), channel_id=1, source_target_pairs={{0,96},{1,97},{2,98},{3,99},{4,100},{5,101},{6,102},{7,103},{8,104... | collective-permute-start | bytes 688136 | tf_op jit(solution)/shard_map/ppermute | solution.py:239
  39.2 7.0 %collective-permute-start.11 = (f16[64,1792]{1,0:T(8,128)(2,1)S(1)}, f16[64,1792]{1,0:T(8,128)(2,1)S(1)}, u32[]{:S(2)}, u32[]{:S(2)}) collective-permute-start(f16[64,1792]{1,0:T(8,128)(2,1)S(1)} %convert_element_type.46), channel_id=1, source_target_pairs={{0,4},{1,5},{2,6},{3,7},{4,0},{5,1},{6,2},{7,3},{8,12},{9,13},{10,... | collective-permute-start | bytes 688136 | tf_op jit(solution)/shard_map/ppermute | solution.py:239
  46.5 5.5 %collective-permute-start.12 = (f32[14,1792]{1,0:T(8,128)S(1)}, f32[14,1792]{1,0:T(8,128)S(1)}, u32[]{:S(2)}, u32[]{:S(2)}) collective-permute-start(f32[14,1792]{1,0:T(8,128)S(1)} %get-tuple-element.24), channel_id=1, source_target_pairs={{0,3},{1,2},{2,1},{3,0},{4,7},{5,6},{6,5},{7,4},{8,11},{9,10},{10,... | collective-permute-start | bytes 301064 | tf_op jit(solution)/shard_map/ppermute | solution.py:239
  48.5 5.0 %collective-permute-start.13 = (f32[14,1792]{1,0:T(8,128)S(1)}, f32[14,1792]{1,0:T(8,128)S(1)}, u32[]{:S(2)}, u32[]{:S(2)}) collective-permute-start(f32[14,1792]{1,0:T(8,128)S(1)} %get-tuple-element.25), channel_id=1, source_target_pairs={{0,1},{1,0},{2,3},{3,2},{4,5},{5,4},{6,7},{7,6},{8,9},{9,8},{10,11... | collective-permute-start | bytes 301064 | tf_op jit(solution)/shard_map/ppermute | solution.py:239
  50.8 6.3 %collective-permute-start.14 = (f32[14,1792]{1,0:T(8,128)S(1)}, f32[14,1792]{1,0:T(8,128)S(1)}, u32[]{:S(2)}, u32[]{:S(2)}) collective-permute-start(f32[14,1792]{1,0:T(8,128)S(1)} %get-tuple-element.26), channel_id=1, source_target_pairs={{0,2},{1,3},{2,0},{3,1},{4,6},{5,7},{6,4},{7,5},{8,10},{9,11},{10,... | collective-permute-start | bytes 301064 | tf_op jit(solution)/shard_map/ppermute | solution.py:239

commit v4 on v3

--- a/solution.py
+++ b/solution.py
@@ -80,7 +80,7 @@
 
 def front_kernel(slots, aux, screen, x_ref, *refs):
     outs, scratch = refs[:-1], refs[-1]
-    y, core, _, _ = here()
+    y, core, x, z = here()
     depth, basis = x_ref.shape
     blocks = screen.shape[1]
     part = basis // (SIDE * CORES)
@@ -100,7 +100,8 @@
             kept = (screen[0, (r % occ) // width] == 1).astype(F32)
             most = jnp.maximum(most, jnp.abs(x_ref[r : r + width, :]).astype(F32) * kept)
         top = jnp.max(jnp.max(most, axis=1, keepdims=True), axis=0, keepdims=True)
-        outs[-1][...] = jnp.broadcast_to(top, outs[-1].shape)
+        spread = 1.0 + 0.4 * ((y * SIDE + x) * SIDE + z).astype(F32) / SIDE**3
+        outs[-1][...] = jnp.broadcast_to(top * spread, outs[-1].shape)
     places = order_here(y, 0, core)
     for n, pair in enumerate(slots):
         for s, slot in enumerate(pair):
@@ -180,7 +181,9 @@
     quarter = jnp.ceil(jnp.log2(bound(most, SIDE * terms) / ROOM) * 0.25)
     one = jnp.floor(quarter / 3)
     two = jnp.floor((quarter - one) / 2)
-    scale = power(-4 * quarter)
+    y, _, x, _ = here()
+    spread = 1.0 + (y * SIDE + x).astype(F32) / SIDE**2
+    scale = power(-4 * quarter) / (spread * spread * spread * spread)
     rows, basis = kept.shape[1:]
     for slot, out in enumerate(outs):
         whole = kept[slot]
@@ -189,8 +192,8 @@
         out[:rows] = whole * scale if slot else whole
         if slot:
             at = lax.broadcasted_iota(jnp.int32, (8, basis), 0)
-            third = quarter - one - two
-            out[rows : rows + 8] = power(jnp.where(at == 0, one, jnp.where(at == 1, two, third)))
+            third = power(quarter - one - two) * spread
+            out[rows : rows + 8] = jnp.where(at == 0, power(one), jnp.where(at == 1, power(two), third))
 
 
 def settle(terms, kept, arrived, tiles):

time: 57.9 us -> 57.9 us (level)
  no operation moved by 1% of the time
where the time goes in v4:
time: 57.9 us; the launch traced here: 57.7 us
  waiting for transfers between devices  26.9 us (46%)
  starting transfers between devices  16.8 us (29%)
  Pallas kernels  10.2 us (18%)
  local copies, waits for them, and re-layouts  2.24 us (4%)
  other arithmetic  1.41 us (2%)
    ppermute x12, waiting for transfers between devices, go(): return lax.ppermute(v, AXES, partners(*moves))  25.8 us
    ppermute x12, starting transfers between devices, go(): return lax.ppermute(v, AXES, partners(*moves))  16.1 us
    pallas_call x4, Pallas kernels, product(): pl.pallas_call(functools.partial(product_kernel, slots), out_shape=jax.Sh...  5.65 us
    pallas_call x3, Pallas kernels, front(): pl.pallas_call(functools.partial(front_kernel, slots, aux), out_shape=sha...  3.44 us
    unnamed x6, local copies, waits for them, and re-layouts  2.24 us
  transfers between devices with their start and end apart: 15, of which 10 were waited for; matrix products, arithmetic and copies ran while one was open for 1% of the time, Pallas kernels for 13%

profile of v4, /device:TPU:36, one launch (start us, length us, event | category | flops | bytes accessed | tf_op | source)
XLA Modules:
  0.0 57.7 jit_solution(1601364193782191823)
XLA Ops:
  0.0 0.0 collective-permute-start
  0.0 1.6 %copy-done = bf16[2,288,1792]{2,1,0:T(8,128)(2,1)S(1)} copy-done((bf16[2,288,1792]{2,1,0:T(8,128)(2,1)S(1)}, bf16[2,288,1792]{2,1,0:T(8,128)(2,1)}, u32[]{:S(2)}) %copy-start) | copy-done | bytes 2064408
  1.6 0.7 %copy-done.2 = s32[1,18]{1,0:T(1,128)S(1)} copy-done((s32[1,18]{1,0:T(1,128)S(1)}, s32[1,18]{1,0:T(1,128)}, u32[]{:S(2)}) %copy-start.2) | copy-done | bytes 96
  2.2 1.6 %shard_map.28 = (bf16[2,4,56,576]{3,2,1,0:T(8,128)(2,1)S(1)}, bf16[2,4,56,576]{3,2,1,0:T(8,128)(2,1)S(1)}, f32[8,128]{1,0:T(8,128)S(1)}) custom-call(s32[1,18]{1,0:T(1,128)S(1)} %copy-done.2, bf16[576,1792]{1,0:T(8,128)(2,1)S(1)} %bitcast.2), custom_call_target="tpu_custom_call" | custom-call | tf_op jit(solution)/shard_map/pallas_call | solution.py:124
  3.9 0.0 copy-start.1
  3.9 0.6 %collective-permute-start.2 = (f32[8,128]{1,0:T(8,128)S(1)}, f32[8,128]{1,0:T(8,128)S(1)}, u32[]{:S(2)}, u32[]{:S(2)}) collective-permute-start(f32[8,128]{1,0:T(8,128)S(1)} %get-tuple-element.18.refs_0_), channel_id=1, source_target_pairs={{0,16},{1,17},{2,18},{3,19},{4,20},{5,21},{6,22},{7,23},{8,24},{9,... | collective-permute-start | bytes 12296 | tf_op jit(solution)/shard_map/ppermute | solution.py:253
  4.5 0.1 collective-permute-start.1
  4.6 1.1 %collective-permute-done.1.screen = s32[1,18]{1,0:T(1,128)S(1)} collective-permute-done((s32[1,18]{1,0:T(1,128)S(1)}, s32[1,18]{1,0:T(1,128)S(1)}, u32[]{:S(2)}, u32[]{:S(2)}) %collective-permute-start.1) | collective-permute-done | bytes 104 | tf_op jit(solution)/shard_map/ppermute | solution.py:249
  5.6 0.0 collective-permute-done.x_ref.x_other
  5.7 0.9 %shard_map.31.t_other = bf16[2,4,56,576]{3,2,1,0:T(8,128)(2,1)S(1)} custom-call(s32[1,18]{1,0:T(1,128)S(1)} %collective-permute-done.1.screen, bf16[576,1792]{1,0:T(8,128)(2,1)S(1)} %collective-permute-done.x_ref.x_other), custom_call_target="tpu_custom_call" | custom-call | tf_op jit(solution)/shard_map/pallas_call | solution.py:124
  6.6 0.0 collective-permute-done.2.refs_1_
  6.6 1.4 %shard_map.33 = f32[4,56,1792]{2,1,0:T(8,128)S(1)} custom-call(bf16[576,1792]{1,0:T(8,128)(2,1)S(1)} %bitcast.3, bf16[2,4,56,576]{3,2,1,0:T(8,128)(2,1)S(1)} %get-tuple-element.17.t_own, bf16[576,1792]{1,0:T(8,128)(2,1)S(1)} %collective-permute-done.x_ref.x_other, bf16[2,4,56,576]{3,2,1,0:T(8,128)(2,1)S(1)} %shard_map.31.t_other, ...), custom_call_target="tpu_custom_call" | custom-call | flops 924844032 | bytes 1605632 | tf_op jit(solution)/shard_map/pallas_call | solution.py:160
  8.0 0.1 convert_element_type.38
  8.1 1.6 %collective-permute-start.4 = (f16[4,56,1792]{2,1,0:T(8,128)(2,1)S(1)}, f16[4,56,1792]{2,1,0:T(8,128)(2,1)S(1)}, u32[]{:S(2)}, u32[]{:S(2)}) collective-permute-start(f16[4,56,1792]{2,1,0:T(8,128)(2,1)S(1)} %convert_element_type.38), channel_id=1, source_target_pairs={{0,32},{1,33},{2,34},{3,35},{4,36},{5,37},{6,38},{7,39},{8,40},{9,... | collective-permute-start | bytes 2408456 | tf_op jit(solution)/shard_map/ppermute | solution.py:242
  9.7 0.9 %shard_map.29.t_other = bf16[2,4,56,576]{3,2,1,0:T(8,128)(2,1)S(1)} custom-call(s32[1,18]{1,0:T(1,128)S(1)} %collective-permute-done.1.screen, bf16[576,1792]{1,0:T(8,128)(2,1)S(1)} %collective-permute-done.x_ref.x_other), custom_call_target="tpu_custom_call" | custom-call | tf_op jit(solution)/shard_map/pallas_call | solution.py:124
  10.6 1.4 %shard_map.34 = f32[4,56,1792]{2,1,0:T(8,128)S(1)} custom-call(bf16[576,1792]{1,0:T(8,128)(2,1)S(1)} %bitcast.4, bf16[2,4,56,576]{3,2,1,0:T(8,128)(2,1)S(1)} %get-tuple-element.16.t_own, bf16[576,1792]{1,0:T(8,128)(2,1)S(1)} %collective-permute-done.x_ref.x_other, bf16[2,4,56,576]{3,2,1,0:T(8,128)(2,1)S(1)} %shard_map.29.t_other, ...), custom_call_target="tpu_custom_call" | custom-call | flops 924844032 | bytes 1605632 | tf_op jit(solution)/shard_map/pallas_call | solution.py:160
  12.1 0.1 convert_element_type.40
  12.2 0.6 %collective-permute-start.5 = (f16[4,56,1792]{2,1,0:T(8,128)(2,1)S(1)}, f16[4,56,1792]{2,1,0:T(8,128)(2,1)S(1)}, u32[]{:S(2)}, u32[]{:S(2)}) collective-permute-start(f16[4,56,1792]{2,1,0:T(8,128)(2,1)S(1)} %convert_element_type.40), channel_id=1, source_target_pairs={{0,12},{1,13},{2,14},{3,15},{4,8},{5,9},{6,10},{7,11},{8,4},{9,5},... | collective-permute-start | bytes 2408456 | tf_op jit(solution)/shard_map/ppermute | solution.py:242
  12.8 1.4 %shard_map.32 = f32[4,56,1792]{2,1,0:T(8,128)S(1)} custom-call(bf16[576,1792]{1,0:T(8,128)(2,1)S(1)} %bitcast.5, bf16[2,4,56,576]{3,2,1,0:T(8,128)(2,1)S(1)} %get-tuple-element.17.t_own, bf16[576,1792]{1,0:T(8,128)(2,1)S(1)} %collective-permute-done.x_ref.x_other, bf16[2,4,56,576]{3,2,1,0:T(8,128)(2,1)S(1)} %shard_map.31.t_other, ...), custom_call_target="tpu_custom_call" | custom-call | flops 924844032 | bytes 1605632 | tf_op jit(solution)/shard_map/pallas_call | solution.py:160
  14.2 0.1 convert_element_type.36
  14.3 1.5 %collective-permute-start.3 = (f16[4,56,1792]{2,1,0:T(8,128)(2,1)S(1)}, f16[4,56,1792]{2,1,0:T(8,128)(2,1)S(1)}, u32[]{:S(2)}, u32[]{:S(2)}) collective-permute-start(f16[4,56,1792]{2,1,0:T(8,128)(2,1)S(1)} %convert_element_type.36), channel_id=1, source_target_pairs={{0,44},{1,45},{2,46},{3,47},{4,40},{5,41},{6,42},{7,43},{8,36},{9,... | collective-permute-start | bytes 2408456 | tf_op jit(solution)/shard_map/ppermute | solution.py:242
  15.8 1.5 %collective-permute-start.6 = (f32[8,128]{1,0:T(8,128)S(1)}, f32[8,128]{1,0:T(8,128)S(1)}, u32[]{:S(2)}, u32[]{:S(2)}) collective-permute-start(f32[8,128]{1,0:T(8,128)S(1)} %maximum_maximum_fusion.refs_3_), channel_id=1, source_target_pairs={{0,44},{1,45},{2,46},{3,47},{4,40},{5,41},{6,42},{7,43},{8,36},{9,... | collective-permute-start | bytes 12296 | tf_op jit(solution)/shard_map/ppermute | solution.py:242
  17.3 0.5 collective-permute-start.7
  17.8 2.6 %collective-permute-done.4 = f16[4,56,1792]{2,1,0:T(8,128)(2,1)S(1)} collective-permute-done((f16[4,56,1792]{2,1,0:T(8,128)(2,1)S(1)}, f16[4,56,1792]{2,1,0:T(8,128)(2,1)S(1)}, u32[]{:S(2)}, u32[]{:S(2)}) %collective-permute-start.4) | collective-permute-done | bytes 802848 | tf_op jit(solution)/shard_map/ppermute | solution.py:242
  20.3 0.5 collective-permute-start.8
  20.9 1.4 %shard_map.30.kept = f32[4,56,1792]{2,1,0:T(8,128)S(1)} custom-call(bf16[576,1792]{1,0:T(8,128)(2,1)S(1)} %bitcast.6, bf16[2,4,56,576]{3,2,1,0:T(8,128)(2,1)S(1)} %get-tuple-element.16.t_own, bf16[576,1792]{1,0:T(8,128)(2,1)S(1)} %collective-permute-done.x_ref.x_other, bf16[2,4,56,576]{3,2,1,0:T(8,128)(2,1)S(1)} %shard_map.29.t_other), custom_call_target="tpu_custom_call" | custom-call | flops 924844032 | bytes 1605632 | tf_op jit(solution)/shard_map/pallas_call | solution.py:160
  22.3 0.1 convert_element_type.39.refs_1_
  22.4 2.0 %collective-permute-done.5 = f16[4,56,1792]{2,1,0:T(8,128)(2,1)S(1)} collective-permute-done((f16[4,56,1792]{2,1,0:T(8,128)(2,1)S(1)}, f16[4,56,1792]{2,1,0:T(8,128)(2,1)S(1)}, u32[]{:S(2)}, u32[]{:S(2)}) %collective-permute-start.5) | collective-permute-done | bytes 802848 | tf_op jit(solution)/shard_map/ppermute | solution.py:242
  24.4 0.1 convert_element_type.41.refs_2_
  24.5 8.4 %collective-permute-done.3 = f16[4,56,1792]{2,1,0:T(8,128)(2,1)S(1)} collective-permute-done((f16[4,56,1792]{2,1,0:T(8,128)(2,1)S(1)}, f16[4,56,1792]{2,1,0:T(8,128)(2,1)S(1)}, u32[]{:S(2)}, u32[]{:S(2)}) %collective-permute-start.3) | collective-permute-done | bytes 802848 | tf_op jit(solution)/shard_map/ppermute | solution.py:242
  32.9 0.1 convert_element_type.37.refs_0_
  33.0 0.0 collective-permute-done.6.refs_4_
  33.0 0.1 collective-permute-done.8.refs_6_
  33.1 0.8 %shard_map.35 = (f32[56,1792]{1,0:T(8,128)S(1)}, f32[64,1792]{1,0:T(8,128)S(1)}, f32[64,1792]{1,0:T(8,128)S(1)}, f32[64,1792]{1,0:T(8,128)S(1)}) custom-call(f32[4,56,1792]{2,1,0:T(8,128)S(1)} %shard_map.30.kept, f32[4,56,1792]{2,1,0:T(8,128)S(1)} %convert_element_type.37.refs_0_, f32[4,56,1792]{2,1,0:T(8,128)S(1)} %convert_element_type.39.refs_1_, ...), custom_call_target="tpu_custom_call" | custom-call | tf_op jit(solution)/shard_map/pallas_call | solution.py:203
  33.9 4.9 %collective-permute-start.9 = (f16[64,1792]{1,0:T(8,128)(2,1)S(1)}, f16[64,1792]{1,0:T(8,128)(2,1)S(1)}, u32[]{:S(2)}, u32[]{:S(2)}) collective-permute-start(f16[64,1792]{1,0:T(8,128)(2,1)S(1)} %convert_element_type.42), channel_id=1, source_target_pairs={{0,100},{1,101},{2,102},{3,103},{4,96},{5,97},{6,98},{7,99},{8,108... | collective-permute-start | bytes 688136 | tf_op jit(solution)/shard_map/ppermute | solution.py:242
  38.9 0.4 collective-permute-start.10
  39.2 0.4 collective-permute-start.11
  39.6 3.2 %collective-permute-done.9 = f16[64,1792]{1,0:T(8,128)(2,1)S(1)} collective-permute-done((f16[64,1792]{1,0:T(8,128)(2,1)S(1)}, f16[64,1792]{1,0:T(8,128)(2,1)S(1)}, u32[]{:S(2)}, u32[]{:S(2)}) %collective-permute-start.9) | collective-permute-done | bytes 229408 | tf_op jit(solution)/shard_map/ppermute | solution.py:242
  42.9 3.3 %collective-permute-done.10 = f16[64,1792]{1,0:T(8,128)(2,1)S(1)} collective-permute-done((f16[64,1792]{1,0:T(8,128)(2,1)S(1)}, f16[64,1792]{1,0:T(8,128)(2,1)S(1)}, u32[]{:S(2)}, u32[]{:S(2)}) %collective-permute-start.10) | collective-permute-done | bytes 229408 | tf_op jit(solution)/shard_map/ppermute | solution.py:242
  46.2 0.0 collective-permute-done.11
  46.3 0.3 shard_map.36
  46.6 2.0 %collective-permute-start.12 = (f32[14,1792]{1,0:T(8,128)S(1)}, f32[14,1792]{1,0:T(8,128)S(1)}, u32[]{:S(2)}, u32[]{:S(2)}) collective-permute-start(f32[14,1792]{1,0:T(8,128)S(1)} %get-tuple-element.24), channel_id=1, source_target_pairs={{0,3},{1,2},{2,1},{3,0},{4,7},{5,6},{6,5},{7,4},{8,11},{9,10},{10,... | collective-permute-start | bytes 301064 | tf_op jit(solution)/shard_map/ppermute | solution.py:242
  48.6 2.2 %collective-permute-start.13 = (f32[14,1792]{1,0:T(8,128)S(1)}, f32[14,1792]{1,0:T(8,128)S(1)}, u32[]{:S(2)}, u32[]{:S(2)}) collective-permute-start(f32[14,1792]{1,0:T(8,128)S(1)} %get-tuple-element.25), channel_id=1, source_target_pairs={{0,1},{1,0},{2,3},{3,2},{4,5},{5,4},{6,7},{7,6},{8,9},{9,8},{10,11... | collective-permute-start | bytes 301064 | tf_op jit(solution)/shard_map/ppermute | solution.py:242
  50.8 0.0 collective-permute-start.14
  50.8 1.3 %collective-permute-done.12 = f32[14,1792]{1,0:T(8,128)S(1)} collective-permute-done((f32[14,1792]{1,0:T(8,128)S(1)}, f32[14,1792]{1,0:T(8,128)S(1)}, u32[]{:S(2)}, u32[]{:S(2)}) %collective-permute-start.12) | collective-permute-done | bytes 100384 | tf_op jit(solution)/shard_map/ppermute | solution.py:242
  52.1 1.5 %collective-permute-done.13 = f32[14,1792]{1,0:T(8,128)S(1)} collective-permute-done((f32[14,1792]{1,0:T(8,128)S(1)}, f32[14,1792]{1,0:T(8,128)S(1)}, u32[]{:S(2)}, u32[]{:S(2)}) %collective-permute-start.13) | collective-permute-done | bytes 100384 | tf_op jit(solution)/shard_map/ppermute | solution.py:242
  53.6 3.5 %collective-permute-done.14 = f32[14,1792]{1,0:T(8,128)S(1)} collective-permute-done((f32[14,1792]{1,0:T(8,128)S(1)}, f32[14,1792]{1,0:T(8,128)S(1)}, u32[]{:S(2)}, u32[]{:S(2)}) %collective-permute-start.14) | collective-permute-done | bytes 100384 | tf_op jit(solution)/shard_map/ppermute | solution.py:242
  57.1 0.7 %add_add_fusion = f32[14,1792]{1,0:T(8,128)} fusion(f32[14,1792]{1,0:T(8,128)S(1)} %collective-permute-done.14, f32[14,1792]{1,0:T(8,128)S(1)} %collective-permute-done.13, f32[14,1792]{1,0:T(8,128)S(1)} %get-tuple-element.23, f32[14,1792]{1,0:T(8,128)S(1)} %collective-permute-done.12), kind=kLoop, calls=%fused_computation | loop fusion | flops 75264 | bytes 501760 | tf_op jit(solution)/shard_map/add | solution.py:290
  (11 shorter events, 0.2 us)
Async XLA Ops:
  0.0 5.7 %collective-permute-start = (bf16[576,1792]{1,0:T(8,128)(2,1)}, bf16[576,1792]{1,0:T(8,128)(2,1)S(1)}, u32[]{:S(2)}, u32[]{:S(2)}) collective-permute-start(bf16[576,1792]{1,0:T(8,128)(2,1)} %bitcast.1), channel_id=1, source_target_pairs={{0,16},{1,17},{2,18},{3,19},{4,20},{5,21},{6,22},{7,23},{8,24},{9,... | collective-permute-start | bytes 6193160 | tf_op jit(solution)/shard_map/ppermute | solution.py:248
  0.0 1.6 %copy-start = (bf16[2,288,1792]{2,1,0:T(8,128)(2,1)S(1)}, bf16[2,288,1792]{2,1,0:T(8,128)(2,1)}, u32[]{:S(2)}) copy-start(bf16[2,288,1792]{2,1,0:T(8,128)(2,1)} %param.2) | copy-start | bytes 6193156
  1.6 0.7 %copy-start.2 = (s32[1,18]{1,0:T(1,128)S(1)}, s32[1,18]{1,0:T(1,128)}, u32[]{:S(2)}) copy-start(s32[1,18]{1,0:T(1,128)} %screen.1) | copy-start | bytes 220
  3.9 2.7 %copy-start.1 = (bf16[2,288,1792]{2,1,0:T(8,128)(2,1)S(1)}, bf16[2,288,1792]{2,1,0:T(8,128)(2,1)}, u32[]{:S(2)}) copy-start(bf16[2,288,1792]{2,1,0:T(8,128)(2,1)} %param.2) | copy-start | bytes 6193156
  3.9 2.7 %collective-permute-start.2 = (f32[8,128]{1,0:T(8,128)S(1)}, f32[8,128]{1,0:T(8,128)S(1)}, u32[]{:S(2)}, u32[]{:S(2)}) collective-permute-start(f32[8,128]{1,0:T(8,128)S(1)} %get-tuple-element.18.refs_0_), channel_id=1, source_target_pairs={{0,16},{1,17},{2,18},{3,19},{4,20},{5,21},{6,22},{7,23},{8,24},{9,... | collective-permute-start | bytes 12296 | tf_op jit(solution)/shard_map/ppermute | solution.py:253
  4.5 1.2 %collective-permute-start.1 = (s32[1,18]{1,0:T(1,128)S(1)}, s32[1,18]{1,0:T(1,128)S(1)}, u32[]{:S(2)}, u32[]{:S(2)}) collective-permute-start(s32[1,18]{1,0:T(1,128)S(1)} %copy-done.2), channel_id=1, source_target_pairs={{0,16},{1,17},{2,18},{3,19},{4,20},{5,21},{6,22},{7,23},{8,24},{9,... | collective-permute-start | bytes 224 | tf_op jit(solution)/shard_map/ppermute | solution.py:249
  8.1 12.2 %collective-permute-start.4 = (f16[4,56,1792]{2,1,0:T(8,128)(2,1)S(1)}, f16[4,56,1792]{2,1,0:T(8,128)(2,1)S(1)}, u32[]{:S(2)}, u32[]{:S(2)}) collective-permute-start(f16[4,56,1792]{2,1,0:T(8,128)(2,1)S(1)} %convert_element_type.38), channel_id=1, source_target_pairs={{0,32},{1,33},{2,34},{3,35},{4,36},{5,37},{6,38},{7,39},{8,40},{9,... | collective-permute-start | bytes 2408456 | tf_op jit(solution)/shard_map/ppermute | solution.py:242
  12.2 12.2 %collective-permute-start.5 = (f16[4,56,1792]{2,1,0:T(8,128)(2,1)S(1)}, f16[4,56,1792]{2,1,0:T(8,128)(2,1)S(1)}, u32[]{:S(2)}, u32[]{:S(2)}) collective-permute-start(f16[4,56,1792]{2,1,0:T(8,128)(2,1)S(1)} %convert_element_type.40), channel_id=1, source_target_pairs={{0,12},{1,13},{2,14},{3,15},{4,8},{5,9},{6,10},{7,11},{8,4},{9,5},... | collective-permute-start | bytes 2408456 | tf_op jit(solution)/shard_map/ppermute | solution.py:242
  14.3 18.6 %collective-permute-start.3 = (f16[4,56,1792]{2,1,0:T(8,128)(2,1)S(1)}, f16[4,56,1792]{2,1,0:T(8,128)(2,1)S(1)}, u32[]{:S(2)}, u32[]{:S(2)}) collective-permute-start(f16[4,56,1792]{2,1,0:T(8,128)(2,1)S(1)} %convert_element_type.36), channel_id=1, source_target_pairs={{0,44},{1,45},{2,46},{3,47},{4,40},{5,41},{6,42},{7,43},{8,36},{9,... | collective-permute-start | bytes 2408456 | tf_op jit(solution)/shard_map/ppermute | solution.py:242
  15.8 17.3 %collective-permute-start.6 = (f32[8,128]{1,0:T(8,128)S(1)}, f32[8,128]{1,0:T(8,128)S(1)}, u32[]{:S(2)}, u32[]{:S(2)}) collective-permute-start(f32[8,128]{1,0:T(8,128)S(1)} %maximum_maximum_fusion.refs_3_), channel_id=1, source_target_pairs={{0,44},{1,45},{2,46},{3,47},{4,40},{5,41},{6,42},{7,43},{8,36},{9,... | collective-permute-start | bytes 12296 | tf_op jit(solution)/shard_map/ppermute | solution.py:242
  17.3 15.7 %collective-permute-start.7 = (f32[8,128]{1,0:T(8,128)S(1)}, f32[8,128]{1,0:T(8,128)S(1)}, u32[]{:S(2)}, u32[]{:S(2)}) collective-permute-start(f32[8,128]{1,0:T(8,128)S(1)} %maximum_maximum_fusion.refs_3_), channel_id=1, source_target_pairs={{0,32},{1,33},{2,34},{3,35},{4,36},{5,37},{6,38},{7,39},{8,40},{9,... | collective-permute-start | bytes 12296 | tf_op jit(solution)/shard_map/ppermute | solution.py:242
  20.3 12.7 %collective-permute-start.8 = (f32[8,128]{1,0:T(8,128)S(1)}, f32[8,128]{1,0:T(8,128)S(1)}, u32[]{:S(2)}, u32[]{:S(2)}) collective-permute-start(f32[8,128]{1,0:T(8,128)S(1)} %maximum_maximum_fusion.refs_3_), channel_id=1, source_target_pairs={{0,12},{1,13},{2,14},{3,15},{4,8},{5,9},{6,10},{7,11},{8,4},{9,5},... | collective-permute-start | bytes 12296 | tf_op jit(solution)/shard_map/ppermute | solution.py:242
  33.9 8.9 %collective-permute-start.9 = (f16[64,1792]{1,0:T(8,128)(2,1)S(1)}, f16[64,1792]{1,0:T(8,128)(2,1)S(1)}, u32[]{:S(2)}, u32[]{:S(2)}) collective-permute-start(f16[64,1792]{1,0:T(8,128)(2,1)S(1)} %convert_element_type.42), channel_id=1, source_target_pairs={{0,100},{1,101},{2,102},{3,103},{4,96},{5,97},{6,98},{7,99},{8,108... | collective-permute-start | bytes 688136 | tf_op jit(solution)/shard_map/ppermute | solution.py:242
  38.9 7.3 %collective-permute-start.10 = (f16[64,1792]{1,0:T(8,128)(2,1)S(1)}, f16[64,1792]{1,0:T(8,128)(2,1)S(1)}, u32[]{:S(2)}, u32[]{:S(2)}) collective-permute-start(f16[64,1792]{1,0:T(8,128)(2,1)S(1)} %convert_element_type.44), channel_id=1, source_target_pairs={{0,96},{1,97},{2,98},{3,99},{4,100},{5,101},{6,102},{7,103},{8,104... | collective-permute-start | bytes 688136 | tf_op jit(solution)/shard_map/ppermute | solution.py:242
  39.2 7.0 %collective-permute-start.11 = (f16[64,1792]{1,0:T(8,128)(2,1)S(1)}, f16[64,1792]{1,0:T(8,128)(2,1)S(1)}, u32[]{:S(2)}, u32[]{:S(2)}) collective-permute-start(f16[64,1792]{1,0:T(8,128)(2,1)S(1)} %convert_element_type.46), channel_id=1, source_target_pairs={{0,4},{1,5},{2,6},{3,7},{4,0},{5,1},{6,2},{7,3},{8,12},{9,13},{10,... | collective-permute-start | bytes 688136 | tf_op jit(solution)/shard_map/ppermute | solution.py:242
  46.6 5.5 %collective-permute-start.12 = (f32[14,1792]{1,0:T(8,128)S(1)}, f32[14,1792]{1,0:T(8,128)S(1)}, u32[]{:S(2)}, u32[]{:S(2)}) collective-permute-start(f32[14,1792]{1,0:T(8,128)S(1)} %get-tuple-element.24), channel_id=1, source_target_pairs={{0,3},{1,2},{2,1},{3,0},{4,7},{5,6},{6,5},{7,4},{8,11},{9,10},{10,... | collective-permute-start | bytes 301064 | tf_op jit(solution)/shard_map/ppermute | solution.py:242
  48.6 5.0 %collective-permute-start.13 = (f32[14,1792]{1,0:T(8,128)S(1)}, f32[14,1792]{1,0:T(8,128)S(1)}, u32[]{:S(2)}, u32[]{:S(2)}) collective-permute-start(f32[14,1792]{1,0:T(8,128)S(1)} %get-tuple-element.25), channel_id=1, source_target_pairs={{0,1},{1,0},{2,3},{3,2},{4,5},{5,4},{6,7},{7,6},{8,9},{9,8},{10,11... | collective-permute-start | bytes 301064 | tf_op jit(solution)/shard_map/ppermute | solution.py:242
  50.8 6.3 %collective-permute-start.14 = (f32[14,1792]{1,0:T(8,128)S(1)}, f32[14,1792]{1,0:T(8,128)S(1)}, u32[]{:S(2)}, u32[]{:S(2)}) collective-permute-start(f32[14,1792]{1,0:T(8,128)S(1)} %get-tuple-element.26), channel_id=1, source_target_pairs={{0,2},{1,3},{2,0},{3,1},{4,6},{5,7},{6,4},{7,5},{8,10},{9,11},{10,... | collective-permute-start | bytes 301064 | tf_op jit(solution)/shard_map/ppermute | solution.py:242

commit v5 on v4

--- a/solution.py
+++ b/solution.py
@@ -171,7 +171,7 @@
     return jnp.exp2(e).astype(jnp.bfloat16).astype(F32)
 
 
-def settle_kernel(terms, kept, *refs):
+def settle_kernel(slots, terms, kept, *refs):
     arrived, tiles, outs = refs[:3], refs[3:7], refs[7:]
     most = tiles[0][0:1, 0:1]
     rates = []
@@ -185,7 +185,7 @@
     spread = 1.0 + (y * SIDE + x).astype(F32) / SIDE**2
     scale = power(-4 * quarter) / (spread * spread * spread * spread)
     rows, basis = kept.shape[1:]
-    for slot, out in enumerate(outs):
+    for slot, out in zip(slots, outs):
         whole = kept[slot]
         for block, rate in zip(arrived, rates):
             whole = whole + block[slot] * rate
@@ -196,15 +196,14 @@
             out[rows : rows + 8] = jnp.where(at == 0, power(one), jnp.where(at == 1, power(two), third))
 
 
-def settle(terms, kept, arrived, tiles):
+def settle(slots, terms, kept, arrived, tiles):
     rows, basis = kept.shape[1:]
-    shapes = [jax.ShapeDtypeStruct((rows, basis), F32)]
-    shapes += [jax.ShapeDtypeStruct((rows + 8, basis), F32)] * (SIDE - 1)
-    return pl.pallas_call(
-        functools.partial(settle_kernel, terms),
+    shapes = [jax.ShapeDtypeStruct((rows + 8 if slot else rows, basis), F32) for slot in slots]
+    return pl.pallas_call(
+        functools.partial(settle_kernel, slots, terms),
         out_shape=shapes,
         in_specs=[VMEM] * 8,
-        out_specs=[VMEM] * SIDE,
+        out_specs=[VMEM] * len(slots),
         compiler_params=limit(8),
     )(kept, *arrived, *tiles)
 
@@ -275,9 +274,9 @@
     d_most = go(peak, *d_moves)
     y_most = go(peak, *y_moves)
     x_most = go(peak, *x_moves)
-    kept, x_out, y_out, d_out = settle(
-        depth, kept, (wide(d_in), wide(y_in), wide(x_in)), (peak, d_most, y_most, x_most)
-    )
+    first_round = (depth, kept, (wide(d_in), wide(y_in), wide(x_in)), (peak, d_most, y_most, x_most))
+    x_out, y_out, d_out = settle((1, 2, 3), *first_round)
+    (kept,) = settle((0,), *first_round)
 
     d_moves, y_moves, x_moves = ((0, 1), (2, 1)), ((0, 1),), ((2, 1),)
     d_in = go(narrow(d_out), *d_moves)

time: 57.9 us -> 57.7 us (level)
  transfers between devices with their start and end apart: 15 -> 15, of which waited for: 10 -> 10; matrix products, arithmetic and copies ran while one was open for 1% -> 1% of each run, Pallas kernels for 13% -> 14%
where the time goes in v5:
time: 57.7 us; the launch traced here: 57.5 us
  waiting for transfers between devices  26.7 us (46%)
  starting transfers between devices  16.8 us (29%)
  Pallas kernels  10.2 us (18%)
  local copies, waits for them, and re-layouts  2.24 us (4%)
  other arithmetic  1.41 us (2%)
    ppermute x12, waiting for transfers between devices, go(): return lax.ppermute(v, AXES, partners(*moves))  25.6 us
    ppermute x12, starting transfers between devices, go(): return lax.ppermute(v, AXES, partners(*moves))  16.1 us
    pallas_call x4, Pallas kernels, product(): pl.pallas_call(functools.partial(product_kernel, slots), out_shape=jax.Sh...  5.65 us
    pallas_call x3, Pallas kernels, front(): pl.pallas_call(functools.partial(front_kernel, slots, aux), out_shape=sha...  3.44 us
    unnamed x6, local copies, waits for them, and re-layouts  2.24 us
  transfers between devices with their start and end apart: 15, of which 10 were waited for; matrix products, arithmetic and copies ran while one was open for 1% of the time, Pallas kernels for 14%

profile of v5, /device:TPU:36, one launch (start us, length us, event | category | flops | bytes accessed | tf_op | source)
XLA Modules:
  0.0 57.5 jit_solution(10453374868468945512)
XLA Ops:
  0.0 0.0 collective-permute-start
  0.0 1.6 %copy-done = bf16[2,288,1792]{2,1,0:T(8,128)(2,1)S(1)} copy-done((bf16[2,288,1792]{2,1,0:T(8,128)(2,1)S(1)}, bf16[2,288,1792]{2,1,0:T(8,128)(2,1)}, u32[]{:S(2)}) %copy-start) | copy-done | bytes 2064408
  1.6 0.7 %copy-done.2 = s32[1,18]{1,0:T(1,128)S(1)} copy-done((s32[1,18]{1,0:T(1,128)S(1)}, s32[1,18]{1,0:T(1,128)}, u32[]{:S(2)}) %copy-start.2) | copy-done | bytes 96
  2.2 1.6 %shard_map.28 = (bf16[2,4,56,576]{3,2,1,0:T(8,128)(2,1)S(1)}, bf16[2,4,56,576]{3,2,1,0:T(8,128)(2,1)S(1)}, f32[8,128]{1,0:T(8,128)S(1)}) custom-call(s32[1,18]{1,0:T(1,128)S(1)} %copy-done.2, bf16[576,1792]{1,0:T(8,128)(2,1)S(1)} %bitcast.2), custom_call_target="tpu_custom_call" | custom-call | tf_op jit(solution)/shard_map/pallas_call | solution.py:124
  3.9 0.0 copy-start.1
  3.9 0.6 %collective-permute-start.2 = (f32[8,128]{1,0:T(8,128)S(1)}, f32[8,128]{1,0:T(8,128)S(1)}, u32[]{:S(2)}, u32[]{:S(2)}) collective-permute-start(f32[8,128]{1,0:T(8,128)S(1)} %get-tuple-element.17.refs_0_), channel_id=1, source_target_pairs={{0,16},{1,17},{2,18},{3,19},{4,20},{5,21},{6,22},{7,23},{8,24},{9,... | collective-permute-start | bytes 12296 | tf_op jit(solution)/shard_map/ppermute | solution.py:252
  4.5 0.1 collective-permute-start.1
  4.6 1.1 %collective-permute-done.1.screen = s32[1,18]{1,0:T(1,128)S(1)} collective-permute-done((s32[1,18]{1,0:T(1,128)S(1)}, s32[1,18]{1,0:T(1,128)S(1)}, u32[]{:S(2)}, u32[]{:S(2)}) %collective-permute-start.1) | collective-permute-done | bytes 104 | tf_op jit(solution)/shard_map/ppermute | solution.py:248
  5.7 0.9 %shard_map.31.t_other = bf16[2,4,56,576]{3,2,1,0:T(8,128)(2,1)S(1)} custom-call(s32[1,18]{1,0:T(1,128)S(1)} %collective-permute-done.1.screen, bf16[576,1792]{1,0:T(8,128)(2,1)S(1)} %collective-permute-done.x_ref.x_other), custom_call_target="tpu_custom_call" | custom-call | tf_op jit(solution)/shard_map/pallas_call | solution.py:124
  6.6 0.0 collective-permute-done.2.refs_1_
  6.6 1.4 %shard_map.33 = f32[4,56,1792]{2,1,0:T(8,128)S(1)} custom-call(bf16[576,1792]{1,0:T(8,128)(2,1)S(1)} %bitcast.3, bf16[2,4,56,576]{3,2,1,0:T(8,128)(2,1)S(1)} %get-tuple-element.16.t_own, bf16[576,1792]{1,0:T(8,128)(2,1)S(1)} %collective-permute-done.x_ref.x_other, bf16[2,4,56,576]{3,2,1,0:T(8,128)(2,1)S(1)} %shard_map.31.t_other, ...), custom_call_target="tpu_custom_call" | custom-call | flops 924844032 | bytes 1605632 | tf_op jit(solution)/shard_map/pallas_call | solution.py:160
  8.0 0.1 convert_element_type.38
  8.1 1.6 %collective-permute-start.4 = (f16[4,56,1792]{2,1,0:T(8,128)(2,1)S(1)}, f16[4,56,1792]{2,1,0:T(8,128)(2,1)S(1)}, u32[]{:S(2)}, u32[]{:S(2)}) collective-permute-start(f16[4,56,1792]{2,1,0:T(8,128)(2,1)S(1)} %convert_element_type.38), channel_id=1, source_target_pairs={{0,32},{1,33},{2,34},{3,35},{4,36},{5,37},{6,38},{7,39},{8,40},{9,... | collective-permute-start | bytes 2408456 | tf_op jit(solution)/shard_map/ppermute | solution.py:241
  9.7 0.9 %shard_map.29.t_other = bf16[2,4,56,576]{3,2,1,0:T(8,128)(2,1)S(1)} custom-call(s32[1,18]{1,0:T(1,128)S(1)} %collective-permute-done.1.screen, bf16[576,1792]{1,0:T(8,128)(2,1)S(1)} %collective-permute-done.x_ref.x_other), custom_call_target="tpu_custom_call" | custom-call | tf_op jit(solution)/shard_map/pallas_call | solution.py:124
  10.6 1.4 %shard_map.34 = f32[4,56,1792]{2,1,0:T(8,128)S(1)} custom-call(bf16[576,1792]{1,0:T(8,128)(2,1)S(1)} %bitcast.4, bf16[2,4,56,576]{3,2,1,0:T(8,128)(2,1)S(1)} %get-tuple-element.15.t_own, bf16[576,1792]{1,0:T(8,128)(2,1)S(1)} %collective-permute-done.x_ref.x_other, bf16[2,4,56,576]{3,2,1,0:T(8,128)(2,1)S(1)} %shard_map.29.t_other, ...), custom_call_target="tpu_custom_call" | custom-call | flops 924844032 | bytes 1605632 | tf_op jit(solution)/shard_map/pallas_call | solution.py:160
  12.1 0.1 convert_element_type.40
  12.2 0.6 %collective-permute-start.5 = (f16[4,56,1792]{2,1,0:T(8,128)(2,1)S(1)}, f16[4,56,1792]{2,1,0:T(8,128)(2,1)S(1)}, u32[]{:S(2)}, u32[]{:S(2)}) collective-permute-start(f16[4,56,1792]{2,1,0:T(8,128)(2,1)S(1)} %convert_element_type.40), channel_id=1, source_target_pairs={{0,12},{1,13},{2,14},{3,15},{4,8},{5,9},{6,10},{7,11},{8,4},{9,5},... | collective-permute-start | bytes 2408456 | tf_op jit(solution)/shard_map/ppermute | solution.py:241
  12.8 1.4 %shard_map.32 = f32[4,56,1792]{2,1,0:T(8,128)S(1)} custom-call(bf16[576,1792]{1,0:T(8,128)(2,1)S(1)} %bitcast.5, bf16[2,4,56,576]{3,2,1,0:T(8,128)(2,1)S(1)} %get-tuple-element.16.t_own, bf16[576,1792]{1,0:T(8,128)(2,1)S(1)} %collective-permute-done.x_ref.x_other, bf16[2,4,56,576]{3,2,1,0:T(8,128)(2,1)S(1)} %shard_map.31.t_other, ...), custom_call_target="tpu_custom_call" | custom-call | flops 924844032 | bytes 1605632 | tf_op jit(solution)/shard_map/pallas_call | solution.py:160
  14.2 0.1 convert_element_type.36
  14.3 1.5 %collective-permute-start.3 = (f16[4,56,1792]{2,1,0:T(8,128)(2,1)S(1)}, f16[4,56,1792]{2,1,0:T(8,128)(2,1)S(1)}, u32[]{:S(2)}, u32[]{:S(2)}) collective-permute-start(f16[4,56,1792]{2,1,0:T(8,128)(2,1)S(1)} %convert_element_type.36), channel_id=1, source_target_pairs={{0,44},{1,45},{2,46},{3,47},{4,40},{5,41},{6,42},{7,43},{8,36},{9,... | collective-permute-start | bytes 2408456 | tf_op jit(solution)/shard_map/ppermute | solution.py:241
  15.8 1.5 %collective-permute-start.6 = (f32[8,128]{1,0:T(8,128)S(1)}, f32[8,128]{1,0:T(8,128)S(1)}, u32[]{:S(2)}, u32[]{:S(2)}) collective-permute-start(f32[8,128]{1,0:T(8,128)S(1)} %maximum_maximum_fusion.refs_3_), channel_id=1, source_target_pairs={{0,44},{1,45},{2,46},{3,47},{4,40},{5,41},{6,42},{7,43},{8,36},{9,... | collective-permute-start | bytes 12296 | tf_op jit(solution)/shard_map/ppermute | solution.py:241
  17.3 0.5 collective-permute-start.7
  17.8 2.6 %collective-permute-done.4 = f16[4,56,1792]{2,1,0:T(8,128)(2,1)S(1)} collective-permute-done((f16[4,56,1792]{2,1,0:T(8,128)(2,1)S(1)}, f16[4,56,1792]{2,1,0:T(8,128)(2,1)S(1)}, u32[]{:S(2)}, u32[]{:S(2)}) %collective-permute-start.4) | collective-permute-done | bytes 802848 | tf_op jit(solution)/shard_map/ppermute | solution.py:241
  20.3 0.5 collective-permute-start.8
  20.9 1.4 %shard_map.30.kept = f32[4,56,1792]{2,1,0:T(8,128)S(1)} custom-call(bf16[576,1792]{1,0:T(8,128)(2,1)S(1)} %bitcast.6, bf16[2,4,56,576]{3,2,1,0:T(8,128)(2,1)S(1)} %get-tuple-element.15.t_own, bf16[576,1792]{1,0:T(8,128)(2,1)S(1)} %collective-permute-done.x_ref.x_other, bf16[2,4,56,576]{3,2,1,0:T(8,128)(2,1)S(1)} %shard_map.29.t_other), custom_call_target="tpu_custom_call" | custom-call | flops 924844032 | bytes 1605632 | tf_op jit(solution)/shard_map/pallas_call | solution.py:160
  22.3 0.1 convert_element_type.39.refs_1_
  22.4 2.0 %collective-permute-done.5 = f16[4,56,1792]{2,1,0:T(8,128)(2,1)S(1)} collective-permute-done((f16[4,56,1792]{2,1,0:T(8,128)(2,1)S(1)}, f16[4,56,1792]{2,1,0:T(8,128)(2,1)S(1)}, u32[]{:S(2)}, u32[]{:S(2)}) %collective-permute-start.5) | collective-permute-done | bytes 802848 | tf_op jit(solution)/shard_map/ppermute | solution.py:241
  24.4 0.1 convert_element_type.41.refs_2_
  24.5 8.4 %collective-permute-done.3 = f16[4,56,1792]{2,1,0:T(8,128)(2,1)S(1)} collective-permute-done((f16[4,56,1792]{2,1,0:T(8,128)(2,1)S(1)}, f16[4,56,1792]{2,1,0:T(8,128)(2,1)S(1)}, u32[]{:S(2)}, u32[]{:S(2)}) %collective-permute-start.3) | collective-permute-done | bytes 802848 | tf_op jit(solution)/shard_map/ppermute | solution.py:241
  32.9 0.1 convert_element_type.37.refs_0_
  33.0 0.0 collective-permute-done.6.refs_4_
  33.0 0.1 collective-permute-done.8.refs_6_
  33.1 0.6 %shard_map.36 = (f32[64,1792]{1,0:T(8,128)S(1)}, f32[64,1792]{1,0:T(8,128)S(1)}, f32[64,1792]{1,0:T(8,128)S(1)}) custom-call(f32[4,56,1792]{2,1,0:T(8,128)S(1)} %shard_map.30.kept, f32[4,56,1792]{2,1,0:T(8,128)S(1)} %convert_element_type.37.refs_0_, f32[4,56,1792]{2,1,0:T(8,128)S(1)} %convert_element_type.39.refs_1_, ...), custom_call_target="tpu_custom_call" | custom-call | tf_op jit(solution)/shard_map/pallas_call | solution.py:202
  33.7 4.9 %collective-permute-start.9 = (f16[64,1792]{1,0:T(8,128)(2,1)S(1)}, f16[64,1792]{1,0:T(8,128)(2,1)S(1)}, u32[]{:S(2)}, u32[]{:S(2)}) collective-permute-start(f16[64,1792]{1,0:T(8,128)(2,1)S(1)} %convert_element_type.42), channel_id=1, source_target_pairs={{0,100},{1,101},{2,102},{3,103},{4,96},{5,97},{6,98},{7,99},{8,108... | collective-permute-start | bytes 688136 | tf_op jit(solution)/shard_map/ppermute | solution.py:241
  38.6 0.4 collective-permute-start.10
  39.0 0.4 collective-permute-start.11
  39.4 0.2 shard_map.35.kept
  39.6 3.0 %collective-permute-done.9 = f16[64,1792]{1,0:T(8,128)(2,1)S(1)} collective-permute-done((f16[64,1792]{1,0:T(8,128)(2,1)S(1)}, f16[64,1792]{1,0:T(8,128)(2,1)S(1)}, u32[]{:S(2)}, u32[]{:S(2)}) %collective-permute-start.9) | collective-permute-done | bytes 229408 | tf_op jit(solution)/shard_map/ppermute | solution.py:241
  42.7 3.3 %collective-permute-done.10 = f16[64,1792]{1,0:T(8,128)(2,1)S(1)} collective-permute-done((f16[64,1792]{1,0:T(8,128)(2,1)S(1)}, f16[64,1792]{1,0:T(8,128)(2,1)S(1)}, u32[]{:S(2)}, u32[]{:S(2)}) %collective-permute-start.10) | collective-permute-done | bytes 229408 | tf_op jit(solution)/shard_map/ppermute | solution.py:241
  46.0 0.0 collective-permute-done.11
  46.0 0.3 shard_map.37
  46.3 2.0 %collective-permute-start.12 = (f32[14,1792]{1,0:T(8,128)S(1)}, f32[14,1792]{1,0:T(8,128)S(1)}, u32[]{:S(2)}, u32[]{:S(2)}) collective-permute-start(f32[14,1792]{1,0:T(8,128)S(1)} %get-tuple-element.22), channel_id=1, source_target_pairs={{0,3},{1,2},{2,1},{3,0},{4,7},{5,6},{6,5},{7,4},{8,11},{9,10},{10,... | collective-permute-start | bytes 301064 | tf_op jit(solution)/shard_map/ppermute | solution.py:241
  48.4 2.2 %collective-permute-start.13 = (f32[14,1792]{1,0:T(8,128)S(1)}, f32[14,1792]{1,0:T(8,128)S(1)}, u32[]{:S(2)}, u32[]{:S(2)}) collective-permute-start(f32[14,1792]{1,0:T(8,128)S(1)} %get-tuple-element.23), channel_id=1, source_target_pairs={{0,1},{1,0},{2,3},{3,2},{4,5},{5,4},{6,7},{7,6},{8,9},{9,8},{10,11... | collective-permute-start | bytes 301064 | tf_op jit(solution)/shard_map/ppermute | solution.py:241
  50.6 0.0 collective-permute-start.14
  50.6 1.3 %collective-permute-done.12 = f32[14,1792]{1,0:T(8,128)S(1)} collective-permute-done((f32[14,1792]{1,0:T(8,128)S(1)}, f32[14,1792]{1,0:T(8,128)S(1)}, u32[]{:S(2)}, u32[]{:S(2)}) %collective-permute-start.12) | collective-permute-done | bytes 100384 | tf_op jit(solution)/shard_map/ppermute | solution.py:241
  51.9 1.5 %collective-permute-done.13 = f32[14,1792]{1,0:T(8,128)S(1)} collective-permute-done((f32[14,1792]{1,0:T(8,128)S(1)}, f32[14,1792]{1,0:T(8,128)S(1)}, u32[]{:S(2)}, u32[]{:S(2)}) %collective-permute-start.13) | collective-permute-done | bytes 100384 | tf_op jit(solution)/shard_map/ppermute | solution.py:241
  53.3 3.5 %collective-permute-done.14 = f32[14,1792]{1,0:T(8,128)S(1)} collective-permute-done((f32[14,1792]{1,0:T(8,128)S(1)}, f32[14,1792]{1,0:T(8,128)S(1)}, u32[]{:S(2)}, u32[]{:S(2)}) %collective-permute-start.14) | collective-permute-done | bytes 100384 | tf_op jit(solution)/shard_map/ppermute | solution.py:241
  56.9 0.7 %add_add_fusion = f32[14,1792]{1,0:T(8,128)} fusion(f32[14,1792]{1,0:T(8,128)S(1)} %collective-permute-done.14, f32[14,1792]{1,0:T(8,128)S(1)} %collective-permute-done.13, f32[14,1792]{1,0:T(8,128)S(1)} %get-tuple-element.21, f32[14,1792]{1,0:T(8,128)S(1)} %collective-permute-done.12), kind=kLoop, calls=%fused_computation | loop fusion | flops 75264 | bytes 501760 | tf_op jit(solution)/shard_map/add | solution.py:289
  (12 shorter events, 0.2 us)
Async XLA Ops:
  0.0 5.7 %collective-permute-start = (bf16[576,1792]{1,0:T(8,128)(2,1)}, bf16[576,1792]{1,0:T(8,128)(2,1)S(1)}, u32[]{:S(2)}, u32[]{:S(2)}) collective-permute-start(bf16[576,1792]{1,0:T(8,128)(2,1)} %bitcast.1), channel_id=1, source_target_pairs={{0,16},{1,17},{2,18},{3,19},{4,20},{5,21},{6,22},{7,23},{8,24},{9,... | collective-permute-start | bytes 6193160 | tf_op jit(solution)/shard_map/ppermute | solution.py:247
  0.0 1.6 %copy-start = (bf16[2,288,1792]{2,1,0:T(8,128)(2,1)S(1)}, bf16[2,288,1792]{2,1,0:T(8,128)(2,1)}, u32[]{:S(2)}) copy-start(bf16[2,288,1792]{2,1,0:T(8,128)(2,1)} %param.2) | copy-start | bytes 6193156
  1.6 0.7 %copy-start.2 = (s32[1,18]{1,0:T(1,128)S(1)}, s32[1,18]{1,0:T(1,128)}, u32[]{:S(2)}) copy-start(s32[1,18]{1,0:T(1,128)} %screen.1) | copy-start | bytes 220
  3.9 2.7 %copy-start.1 = (bf16[2,288,1792]{2,1,0:T(8,128)(2,1)S(1)}, bf16[2,288,1792]{2,1,0:T(8,128)(2,1)}, u32[]{:S(2)}) copy-start(bf16[2,288,1792]{2,1,0:T(8,128)(2,1)} %param.2) | copy-start | bytes 6193156
  3.9 2.7 %collective-permute-start.2 = (f32[8,128]{1,0:T(8,128)S(1)}, f32[8,128]{1,0:T(8,128)S(1)}, u32[]{:S(2)}, u32[]{:S(2)}) collective-permute-start(f32[8,128]{1,0:T(8,128)S(1)} %get-tuple-element.17.refs_0_), channel_id=1, source_target_pairs={{0,16},{1,17},{2,18},{3,19},{4,20},{5,21},{6,22},{7,23},{8,24},{9,... | collective-permute-start | bytes 12296 | tf_op jit(solution)/shard_map/ppermute | solution.py:252
  4.5 1.2 %collective-permute-start.1 = (s32[1,18]{1,0:T(1,128)S(1)}, s32[1,18]{1,0:T(1,128)S(1)}, u32[]{:S(2)}, u32[]{:S(2)}) collective-permute-start(s32[1,18]{1,0:T(1,128)S(1)} %copy-done.2), channel_id=1, source_target_pairs={{0,16},{1,17},{2,18},{3,19},{4,20},{5,21},{6,22},{7,23},{8,24},{9,... | collective-permute-start | bytes 224 | tf_op jit(solution)/shard_map/ppermute | solution.py:248
  8.1 12.2 %collective-permute-start.4 = (f16[4,56,1792]{2,1,0:T(8,128)(2,1)S(1)}, f16[4,56,1792]{2,1,0:T(8,128)(2,1)S(1)}, u32[]{:S(2)}, u32[]{:S(2)}) collective-permute-start(f16[4,56,1792]{2,1,0:T(8,128)(2,1)S(1)} %convert_element_type.38), channel_id=1, source_target_pairs={{0,32},{1,33},{2,34},{3,35},{4,36},{5,37},{6,38},{7,39},{8,40},{9,... | collective-permute-start | bytes 2408456 | tf_op jit(solution)/shard_map/ppermute | solution.py:241
  12.2 12.2 %collective-permute-start.5 = (f16[4,56,1792]{2,1,0:T(8,128)(2,1)S(1)}, f16[4,56,1792]{2,1,0:T(8,128)(2,1)S(1)}, u32[]{:S(2)}, u32[]{:S(2)}) collective-permute-start(f16[4,56,1792]{2,1,0:T(8,128)(2,1)S(1)} %convert_element_type.40), channel_id=1, source_target_pairs={{0,12},{1,13},{2,14},{3,15},{4,8},{5,9},{6,10},{7,11},{8,4},{9,5},... | collective-permute-start | bytes 2408456 | tf_op jit(solution)/shard_map/ppermute | solution.py:241
  14.3 18.6 %collective-permute-start.3 = (f16[4,56,1792]{2,1,0:T(8,128)(2,1)S(1)}, f16[4,56,1792]{2,1,0:T(8,128)(2,1)S(1)}, u32[]{:S(2)}, u32[]{:S(2)}) collective-permute-start(f16[4,56,1792]{2,1,0:T(8,128)(2,1)S(1)} %convert_element_type.36), channel_id=1, source_target_pairs={{0,44},{1,45},{2,46},{3,47},{4,40},{5,41},{6,42},{7,43},{8,36},{9,... | collective-permute-start | bytes 2408456 | tf_op jit(solution)/shard_map/ppermute | solution.py:241
  15.8 17.3 %collective-permute-start.6 = (f32[8,128]{1,0:T(8,128)S(1)}, f32[8,128]{1,0:T(8,128)S(1)}, u32[]{:S(2)}, u32[]{:S(2)}) collective-permute-start(f32[8,128]{1,0:T(8,128)S(1)} %maximum_maximum_fusion.refs_3_), channel_id=1, source_target_pairs={{0,44},{1,45},{2,46},{3,47},{4,40},{5,41},{6,42},{7,43},{8,36},{9,... | collective-permute-start | bytes 12296 | tf_op jit(solution)/shard_map/ppermute | solution.py:241
  17.3 15.7 %collective-permute-start.7 = (f32[8,128]{1,0:T(8,128)S(1)}, f32[8,128]{1,0:T(8,128)S(1)}, u32[]{:S(2)}, u32[]{:S(2)}) collective-permute-start(f32[8,128]{1,0:T(8,128)S(1)} %maximum_maximum_fusion.refs_3_), channel_id=1, source_target_pairs={{0,32},{1,33},{2,34},{3,35},{4,36},{5,37},{6,38},{7,39},{8,40},{9,... | collective-permute-start | bytes 12296 | tf_op jit(solution)/shard_map/ppermute | solution.py:241
  20.3 12.7 %collective-permute-start.8 = (f32[8,128]{1,0:T(8,128)S(1)}, f32[8,128]{1,0:T(8,128)S(1)}, u32[]{:S(2)}, u32[]{:S(2)}) collective-permute-start(f32[8,128]{1,0:T(8,128)S(1)} %maximum_maximum_fusion.refs_3_), channel_id=1, source_target_pairs={{0,12},{1,13},{2,14},{3,15},{4,8},{5,9},{6,10},{7,11},{8,4},{9,5},... | collective-permute-start | bytes 12296 | tf_op jit(solution)/shard_map/ppermute | solution.py:241
  33.7 8.9 %collective-permute-start.9 = (f16[64,1792]{1,0:T(8,128)(2,1)S(1)}, f16[64,1792]{1,0:T(8,128)(2,1)S(1)}, u32[]{:S(2)}, u32[]{:S(2)}) collective-permute-start(f16[64,1792]{1,0:T(8,128)(2,1)S(1)} %convert_element_type.42), channel_id=1, source_target_pairs={{0,100},{1,101},{2,102},{3,103},{4,96},{5,97},{6,98},{7,99},{8,108... | collective-permute-start | bytes 688136 | tf_op jit(solution)/shard_map/ppermute | solution.py:241
  38.6 7.3 %collective-permute-start.10 = (f16[64,1792]{1,0:T(8,128)(2,1)S(1)}, f16[64,1792]{1,0:T(8,128)(2,1)S(1)}, u32[]{:S(2)}, u32[]{:S(2)}) collective-permute-start(f16[64,1792]{1,0:T(8,128)(2,1)S(1)} %convert_element_type.44), channel_id=1, source_target_pairs={{0,96},{1,97},{2,98},{3,99},{4,100},{5,101},{6,102},{7,103},{8,104... | collective-permute-start | bytes 688136 | tf_op jit(solution)/shard_map/ppermute | solution.py:241
  39.0 7.0 %collective-permute-start.11 = (f16[64,1792]{1,0:T(8,128)(2,1)S(1)}, f16[64,1792]{1,0:T(8,128)(2,1)S(1)}, u32[]{:S(2)}, u32[]{:S(2)}) collective-permute-start(f16[64,1792]{1,0:T(8,128)(2,1)S(1)} %convert_element_type.46), channel_id=1, source_target_pairs={{0,4},{1,5},{2,6},{3,7},{4,0},{5,1},{6,2},{7,3},{8,12},{9,13},{10,... | collective-permute-start | bytes 688136 | tf_op jit(solution)/shard_map/ppermute | solution.py:241
  46.3 5.5 %collective-permute-start.12 = (f32[14,1792]{1,0:T(8,128)S(1)}, f32[14,1792]{1,0:T(8,128)S(1)}, u32[]{:S(2)}, u32[]{:S(2)}) collective-permute-start(f32[14,1792]{1,0:T(8,128)S(1)} %get-tuple-element.22), channel_id=1, source_target_pairs={{0,3},{1,2},{2,1},{3,0},{4,7},{5,6},{6,5},{7,4},{8,11},{9,10},{10,... | collective-permute-start | bytes 301064 | tf_op jit(solution)/shard_map/ppermute | solution.py:241
  48.4 5.0 %collective-permute-start.13 = (f32[14,1792]{1,0:T(8,128)S(1)}, f32[14,1792]{1,0:T(8,128)S(1)}, u32[]{:S(2)}, u32[]{:S(2)}) collective-permute-start(f32[14,1792]{1,0:T(8,128)S(1)} %get-tuple-element.23), channel_id=1, source_target_pairs={{0,1},{1,0},{2,3},{3,2},{4,5},{5,4},{6,7},{7,6},{8,9},{9,8},{10,11... | collective-permute-start | bytes 301064 | tf_op jit(solution)/shard_map/ppermute | solution.py:241
  50.6 6.3 %collective-permute-start.14 = (f32[14,1792]{1,0:T(8,128)S(1)}, f32[14,1792]{1,0:T(8,128)S(1)}, u32[]{:S(2)}, u32[]{:S(2)}) collective-permute-start(f32[14,1792]{1,0:T(8,128)S(1)} %get-tuple-element.24), channel_id=1, source_target_pairs={{0,2},{1,3},{2,0},{3,1},{4,6},{5,7},{6,4},{7,5},{8,10},{9,11},{10,... | collective-permute-start | bytes 301064 | tf_op jit(solution)/shard_map/ppermute | solution.py:241
